TPU v7x, 128 devices: a whole 4x4x4 slice. The times are simulated.
128 devices in a mesh: row: 8 (over x, core), col: 16 (over z, y).
Axes of the slice: x: 4, y: 4, z: 4, core: 2. Of those that a mesh axis runs over, the one named last changes fastest.
Arguments:
- jump: float32 [3, 512, 2048], P(None, 'row', 'col'), may hold values from -6 to 6
- external: float32 [3, 512, 2048], P(None, 'row', 'col'), may hold values from -12 to 12
- cohesive: float32 [512, 2048], P('row', 'col'), may hold values from 0.5 to 4
- bond_mask: int32 [2, 512, 2048], P(None, 'row', 'col'), may hold values 0 or 1
- load_factor: float32 [1], replicated, may hold values from 0.5 to 1.5
- arc_radius: float32 [1], replicated, may hold values from 0.5 to 1.5
- stiffness: bfloat16 [1536, 1536], replicated, may hold values from -1 to 2
- coupling: float32 [3, 1536], replicated, may hold values from -6 to 6
- old_state: float32 [20480, 1536], P(('row', 'col')), may hold values from -3 to 3
- old_history: float32 [20480, 1536], P(('row', 'col')), may hold values from 0 to 1.5
- newton_steps: int32 [20480], P(('row', 'col')), may hold values from 0 to 9, as said below
- point_ids: int32 [20480], P(('row', 'col')), may hold values from 0 to 8191, as said below
Outputs:
- new_jump: float32 [3, 512, 2048], P(None, 'row', 'col')
- new_load: float32 [1], replicated
- new_state: float32 [10240, 1536], P(('row', 'col'))
- new_history: float32 [10240, 1536], P(('row', 'col'))
Inputs may be any that keep to these rules, and one draw needn't show every extreme that they name: `newton_steps`: within one block the live slots number between 20 and 160, and some block has all 160 live; in all at most 8960 slots are live; a live slot's count is at least 2. `point_ids`: the slots of one block name distinct points of that block.
All inputs are finite; a program needn't handle non-finite values. No bound on the sum of `bond_mask` on one device may be relied on, other than what follows from the above.
Results may differ from a plain program's by a relative error of at most 0.0028.
Values sent between devices are 32-bit elements; how exact they have to be, the bound alone decides.
No kernel may reach another device: no remote copies, remote signals or barrier semaphores. Data moves between devices by JAX's collectives and lax.ppermute only.
A program may use at most 64 MiB of HBM per device.

v0:
```python
import functools

import jax
import jax.numpy as jnp
from jax import lax
from jax.sharding import Mesh
from jax.sharding import PartitionSpec as P

MAX_STEPS = 9
SWEEPS = 3
ROW_COL = ("row_0", "row_1", "col_0", "col_1")
ROW = ("row_0", "row_1")
COL = ("col_0", "col_1")


softening = 1.0


def laid_out(parts, dim):
    lengths = list(parts.shape[1:])
    lengths[dim] *= parts.shape[0]
    return jnp.moveaxis(parts, 0, dim).reshape(lengths)


def gather_in_order(array, axes, sequence):
    parts = array[None]
    for k in sequence:
        parts = lax.all_gather(parts, axes[k], axis=0, tiled=True)
    block = [lax.axis_size(axes[k]) for k in reversed(sequence)]
    parts = parts.reshape(*block, *array.shape)
    turned = sorted(range(len(sequence)), key=lambda place: sequence[len(sequence) - 1 - place])
    return parts.transpose(*turned, *range(len(sequence), parts.ndim)).reshape(-1, *array.shape)


def whole_of(array, axes, sequence, dim):
    return laid_out(gather_in_order(array, axes, sequence), dim)


def in_one_piece(arrays, axis, split_dim, concat_dim, along):
    ends, at = ([], 0)
    for a in arrays[:-1]:
        at += a.shape[along]
        ends.append(at)
    both = jnp.concatenate(arrays, axis=along)
    return tuple(
        jnp.split(
            lax.all_to_all(both, axis, split_axis=split_dim, concat_axis=concat_dim, tiled=True),
            ends,
            axis=along,
        )
    )


def shifted_2(value, axis, steps):
    count = lax.axis_size(axis)
    first, last = (max(0, -steps), min(count, count - steps))
    return lax.ppermute(value, axis, [(source, source + steps) for source in range(first, last)])


def padded_2(array, sides, width):
    edges = {}
    for axis, dim in sides:
        size, length = (lax.axis_size(axis), array.shape[dim])
        up = [(i, (i + 1) % size) for i in range(size - 1)]
        last = lax.slice_in_dim(array, length - width, length, axis=dim)
        first = lax.slice_in_dim(array, 0, width, axis=dim)
        edges[dim] = (
            lax.ppermute(last, axis, up),
            lax.ppermute(first, axis, [(b, a) for a, b in up]),
        )
    done = []
    for _, dim in sides:
        low, high = edges[dim]
        around = [(width, width) if d in done else (0, 0) for d in range(array.ndim)]
        array = jnp.concatenate([jnp.pad(low, around), array, jnp.pad(high, around)], axis=dim)
        done.append(dim)
    return array


def by_axis(array, axes):
    return functools.reduce(lax.psum, axes, array)


def micro_solve(state, history, drive, steps, stiffness, coupling):
    diagonal = jnp.diagonal(stiffness).astype(jnp.float32)
    load = jnp.dot(drive, coupling, precision=lax.Precision.HIGHEST)
    damage = jnp.exp(-history)

    def advance(count, current):
        bent = jnp.tanh(current)
        force = jnp.dot(current.astype(jnp.bfloat16), stiffness, preferred_element_type=jnp.float32)
        misfit = force + softening * damage * bent - load
        slope = diagonal + softening * damage * (1.0 - bent * bent)
        return jnp.where((count < steps)[:, None], current - misfit / slope, current)

    state = lax.fori_loop(0, MAX_STEPS, advance, state)
    bent = jnp.tanh(state)
    cells = state.shape[1]
    traction = (
        jnp.dot(softening * damage * bent, coupling.T, precision=lax.Precision.HIGHEST) / cells
    )
    weight = softening * damage * (1.0 - bent * bent)
    products = jnp.stack(
        [
            coupling[0] * coupling[0],
            coupling[1] * coupling[1],
            coupling[2] * coupling[2],
            coupling[0] * coupling[1],
            coupling[0] * coupling[2],
            coupling[1] * coupling[2],
        ]
    )
    tangent = jnp.dot(weight, products.T, precision=lax.Precision.HIGHEST) / cells
    history = jnp.maximum(history, jnp.abs(state))
    return (state, history, traction, tangent)


def block_solve(scale, tangent, source):
    d00 = scale + tangent[0]
    d11 = scale + tangent[1]
    d22 = scale + tangent[2]
    d01, d02, d12 = (tangent[3], tangent[4], tangent[5])
    c00 = d11 * d22 - d12 * d12
    c11 = d00 * d22 - d02 * d02
    c22 = d00 * d11 - d01 * d01
    c01 = d02 * d12 - d01 * d22
    c02 = d01 * d12 - d02 * d11
    c12 = d01 * d02 - d00 * d12
    determinant = d00 * c00 + d01 * c01 + d02 * c02
    first = (c00 * source[0] + c01 * source[1] + c02 * source[2]) / determinant
    second = (c01 * source[0] + c11 * source[1] + c12 * source[2]) / determinant
    third = (c02 * source[0] + c12 * source[1] + c22 * source[2]) / determinant
    return jnp.stack([first, second, third])


def neighbours(padded, bond_x, low_x, bond_y, low_y):
    return (
        bond_x * padded[:, 2:, 1:-1]
        + low_x * padded[:, :-2, 1:-1]
        + bond_y * padded[:, 1:-1, 2:]
        + low_y * padded[:, 1:-1, :-2]
    )


def on_device(
    jump,
    external,
    cohesive,
    bond_mask,
    load_factor,
    arc_radius,
    stiffness,
    coupling,
    old_state,
    old_history,
    newton_steps,
    point_ids,
):
    devices = lax.axis_size(ROW_COL)
    here = lax.axis_index(ROW_COL)
    slots, cells = old_state.shape
    new_cap = slots // 2
    pair = 2 * ((slots + 2 * devices + 1) // (2 * devices))
    width = devices * pair
    rows_x, rows_y = (jump.shape[1], jump.shape[2])
    live = newton_steps > 0
    live_int = live.astype(jnp.int32)
    live_float = live.astype(jnp.float32)
    counts = whole_of(jnp.sum(live_int)[None], ROW_COL, (0, 2, 3, 1), 0)
    starts = jnp.cumsum(counts, dtype=jnp.int32) - counts
    rank = starts[here] + jnp.cumsum(live_int, dtype=jnp.int32) - live_int
    home_block = rank // 2 % devices
    peers = jnp.arange(devices, dtype=jnp.int32)
    aimed = ((home_block[:, None] == peers[None, :]) & live[:, None]).astype(jnp.int32)
    within = jnp.sum((jnp.cumsum(aimed, axis=0, dtype=jnp.int32) - aimed) * aimed, axis=1)
    send_index = jnp.where(live, home_block * pair + within, width)
    new_slot = jnp.arange(new_cap, dtype=jnp.int32)
    wanted = 2 * (here + devices * (new_slot // 2)) + new_slot % 2
    valid = wanted < jnp.sum(counts)
    source = jnp.sum((starts[None, :] <= wanted[:, None]).astype(jnp.int32), axis=1) - 1
    coming = ((source[:, None] == peers[None, :]) & valid[:, None]).astype(jnp.int32)
    order = jnp.sum((jnp.cumsum(coming, axis=0, dtype=jnp.int32) - coming) * coming, axis=1)
    recv_index = jnp.where(valid, source * pair + order, 0)
    drive = jump.reshape(3, rows_x * rows_y)[:, point_ids].T
    blank = jnp.zeros((width, cells), jnp.float32)
    state, history, traction, tangent = micro_solve(
        old_state, old_history, drive, newton_steps, stiffness, coupling
    )
    outgoing = (
        blank.at[send_index].set(state, mode="drop"),
        blank.at[send_index].set(history, mode="drop"),
    )
    arrived = in_one_piece((outgoing[0], outgoing[1]), ROW_COL, 0, 0, 1)
    new_state = jnp.where(valid[:, None], arrived[0][recv_index], 0.0)
    new_history = jnp.where(valid[:, None], arrived[1][recv_index], 0.0)
    points = rows_x * rows_y
    soft = jnp.zeros((points,), jnp.float32).at[point_ids].add(live_float).reshape(rows_x, rows_y)
    rve_traction = (
        jnp.zeros((3, points), jnp.float32)
        .at[:, point_ids]
        .add((traction * live_float[:, None]).T)
        .reshape(3, rows_x, rows_y)
    )
    rve_tangent = (
        jnp.zeros((6, points), jnp.float32)
        .at[:, point_ids]
        .add((tangent * live_float[:, None]).T)
        .reshape(6, rows_x, rows_y)
    )
    bond_x = 0.25 + 0.75 * bond_mask[0].astype(jnp.float32)
    bond_y = 0.25 + 0.75 * bond_mask[1].astype(jnp.float32)
    edge_x = shifted_2(bond_x[-1:, :], ROW, 1)
    edge_y = shifted_2(bond_y[:, -1:], COL, 1)
    low_x = jnp.concatenate([edge_x, bond_x[:-1]], axis=0)
    low_y = jnp.concatenate([edge_y, bond_y[:, :-1]], axis=1)
    scale = bond_x + low_x + bond_y + low_y + (1.0 - soft) * cohesive
    padded_jump = padded_2(jump, ((ROW, 1), (COL, 2)), 1)
    residual = (
        scale * jump
        - neighbours(padded_jump, bond_x, low_x, bond_y, low_y)
        + rve_traction
        - load_factor[0] * external
    )
    source_terms = jnp.concatenate([-residual, external])

    def solve_both(values):
        return jnp.concatenate(
            [
                block_solve(scale, rve_tangent, values[:3]),
                block_solve(scale, rve_tangent, values[3:]),
            ]
        )

    iterate = solve_both(source_terms)
    for sweep in range(SWEEPS):
        padded = padded_2(iterate, ((ROW, 1), (COL, 2)), 1)
        iterate = solve_both(source_terms + neighbours(padded, bond_x, low_x, bond_y, low_y))
    correction, direction = (iterate[:3], iterate[3:])
    cross, square = (
        by_axis(jnp.sum(correction * direction), ROW_COL),
        by_axis(jnp.sum(direction * direction), ROW_COL),
    )
    entries = 3.0 * rows_x * rows_y * devices
    shifted = square + 0.25 * entries
    increment = (arc_radius[0] * jnp.sqrt(entries) * jnp.sqrt(shifted) - cross) / shifted
    new_jump = jump + correction + increment * direction
    new_load = load_factor + increment
    return (new_jump, new_load, new_state, new_history)


def solution(mesh):
    split = Mesh(mesh.devices.reshape(4, 2, 4, 4), ("row_0", "row_1", "col_0", "col_1"))
    placed = (
        P(None, ROW, COL),
        P(None, ROW, COL),
        P(ROW, COL),
        P(None, ROW, COL),
        P(),
        P(),
        P(),
        P(),
        P(ROW_COL, None),
        P(ROW_COL, None),
        P(ROW_COL),
        P(ROW_COL),
    )
    return jax.shard_map(
        on_device,
        mesh=split,
        in_specs=placed,
        out_specs=(P(None, ROW, COL), P(), P(ROW_COL, None), P(ROW_COL, None)),
        check_vma=False,
    )
```

profile of v0, /device:TPU:0, one launch (start us, length us, event | category | flops | bytes accessed | tf_op | source)
XLA Modules:
  0.0 311.2 jit_solution(1537372548901469388)
XLA Ops:
  2.5 4.2 %collective-permute-start.5 = (f32[3,64,1]{2,1,0:T(8,128)}, f32[3,64,1]{2,1,0:T(8,128)}, u32[]{:S(2)}, u32[]{:S(2)}) collective-permute-start(f32[3,64,1]{2,1,0:T(8,128)} %get-tuple-element.198), channel_id=1, source_target_pairs={{0,1},{1,2},{2,3},{3,4},{4,5},{5,6},{6,7},{7,8},{8,9},{9,10},{10,1... | collective-permute-start | bytes 2312 | tf_op jit(solution)/shard_map/ppermute | solution.py:68
  28.2 8.0 %all-reduce.10 = s32[4]{0:T(128)S(1)} all-reduce(s32[4]{0:T(128)S(1)} %dynamic-update-slice), channel_id=1, replica_groups=mesh['row_0'=4,'row_1'=2,'col_0'=4,'col_1'=4] {'row_0'}, use_global_device_ids=true, to_apply=%add.10 | all-reduce | flops 4 | bytes 32
  37.7 9.7 %all-reduce.11 = s32[16]{0:T(128)S(1)} all-reduce(s32[16]{0:T(128)S(1)} %dynamic-update-slice.1), channel_id=1, replica_groups=mesh['row_0'=4,'row_1'=2,'col_0'=4,'col_1'=4] {'col_0'}, use_global_device_ids=true, to_apply=%add.11 | all-reduce | flops 16 | bytes 128
  48.9 8.5 %all-reduce.12 = s32[64]{0:T(128)S(1)} all-reduce(s32[64]{0:T(128)S(1)} %dynamic-update-slice.2), channel_id=1, replica_groups=mesh['row_0'=4,'row_1'=2,'col_0'=4,'col_1'=4] {'col_1'}, use_global_device_ids=true, to_apply=%add.12 | all-reduce | flops 64 | bytes 512
  69.5 24.3 %gather_fusion.1 = bf16[1536]{0:T(1024)(128)(2,1)S(1)} fusion(bf16[1536,1536]{1,0:T(8,128)(2,1)} %param.20, s32[1536]{0:T(1024)S(1)} %or_reduce_fusion), kind=kCustom, calls=%fused_computation.1 | custom fusion | bytes 18432 | tf_op jit(solution)/shard_map/jit(diagonal)/cond/branch_0_fun/gather | solution.py:85
  93.9 34.3 %while.13 = (s32[]{:T(128)}, f32[160,1536]{1,0:T(8,128)S(1)}, s32[160]{0:T(256)S(1)}, bf16[1536,1536]{1,0:T(8,128)(2,1)}, f32[160,1536]{1,0:T(8,128)S(1)}, /*ind...) while((s32[]{:T(128)}, f32[160,1536]{1,0:T(8,128)S(1)}, s32[160]{0:T(256)S(1)}, ...), condition=%wide.region_2.3_spmd, body=%wide.region_1.0_spmd.sunk | while | flops 757678272 | bytes 10624033 | solution.py:96
  94.0 3.7 %fusion.134 = f32[160,1536]{1,0:T(8,128)S(1)} fusion(f32[160,1536]{1,0:T(8,128)S(1)} %copy.73, f32[160,1536]{1,0:T(8,128)} %get-tuple-element.280, bf16[1536,1536]{1,0:T(8,128)(2,1)} %get-tuple-element.278, f32[160,1536]{1,0:T(8,128)S(1)} %get-tuple-element.279, f32[1536]{0:T(1024)S(1)} %get-tuple-element.281, ...), kind=kOutput, calls=%fused_computation.13.clone.1 | convolution fusion | flops 757678080 | bytes 8657056 | tf_op jit(solution)/shard_map/while/body/eval_jaxpr/dot_general | solution.py:91
  97.8 3.7 %fusion.134 = f32[160,1536]{1,0:T(8,128)S(1)} fusion(f32[160,1536]{1,0:T(8,128)S(1)} %copy.73, f32[160,1536]{1,0:T(8,128)} %get-tuple-element.280, bf16[1536,1536]{1,0:T(8,128)(2,1)} %get-tuple-element.278, f32[160,1536]{1,0:T(8,128)S(1)} %get-tuple-element.279, f32[1536]{0:T(1024)S(1)} %get-tuple-element.281, ...), kind=kOutput, calls=%fused_computation.13.clone.1 | convolution fusion | flops 757678080 | bytes 8657056 | tf_op jit(solution)/shard_map/while/body/eval_jaxpr/dot_general | solution.py:91
  101.6 3.7 %fusion.134 = f32[160,1536]{1,0:T(8,128)S(1)} fusion(f32[160,1536]{1,0:T(8,128)S(1)} %copy.73, f32[160,1536]{1,0:T(8,128)} %get-tuple-element.280, bf16[1536,1536]{1,0:T(8,128)(2,1)} %get-tuple-element.278, f32[160,1536]{1,0:T(8,128)S(1)} %get-tuple-element.279, f32[1536]{0:T(1024)S(1)} %get-tuple-element.281, ...), kind=kOutput, calls=%fused_computation.13.clone.1 | convolution fusion | flops 757678080 | bytes 8657056 | tf_op jit(solution)/shard_map/while/body/eval_jaxpr/dot_general | solution.py:91
  105.4 3.7 %fusion.134 = f32[160,1536]{1,0:T(8,128)S(1)} fusion(f32[160,1536]{1,0:T(8,128)S(1)} %copy.73, f32[160,1536]{1,0:T(8,128)} %get-tuple-element.280, bf16[1536,1536]{1,0:T(8,128)(2,1)} %get-tuple-element.278, f32[160,1536]{1,0:T(8,128)S(1)} %get-tuple-element.279, f32[1536]{0:T(1024)S(1)} %get-tuple-element.281, ...), kind=kOutput, calls=%fused_computation.13.clone.1 | convolution fusion | flops 757678080 | bytes 8657056 | tf_op jit(solution)/shard_map/while/body/eval_jaxpr/dot_general | solution.py:91
  109.2 3.7 %fusion.134 = f32[160,1536]{1,0:T(8,128)S(1)} fusion(f32[160,1536]{1,0:T(8,128)S(1)} %copy.73, f32[160,1536]{1,0:T(8,128)} %get-tuple-element.280, bf16[1536,1536]{1,0:T(8,128)(2,1)} %get-tuple-element.278, f32[160,1536]{1,0:T(8,128)S(1)} %get-tuple-element.279, f32[1536]{0:T(1024)S(1)} %get-tuple-element.281, ...), kind=kOutput, calls=%fused_computation.13.clone.1 | convolution fusion | flops 757678080 | bytes 8657056 | tf_op jit(solution)/shard_map/while/body/eval_jaxpr/dot_general | solution.py:91
  113.1 3.7 %fusion.134 = f32[160,1536]{1,0:T(8,128)S(1)} fusion(f32[160,1536]{1,0:T(8,128)S(1)} %copy.73, f32[160,1536]{1,0:T(8,128)} %get-tuple-element.280, bf16[1536,1536]{1,0:T(8,128)(2,1)} %get-tuple-element.278, f32[160,1536]{1,0:T(8,128)S(1)} %get-tuple-element.279, f32[1536]{0:T(1024)S(1)} %get-tuple-element.281, ...), kind=kOutput, calls=%fused_computation.13.clone.1 | convolution fusion | flops 757678080 | bytes 8657056 | tf_op jit(solution)/shard_map/while/body/eval_jaxpr/dot_general | solution.py:91
  116.9 3.7 %fusion.134 = f32[160,1536]{1,0:T(8,128)S(1)} fusion(f32[160,1536]{1,0:T(8,128)S(1)} %copy.73, f32[160,1536]{1,0:T(8,128)} %get-tuple-element.280, bf16[1536,1536]{1,0:T(8,128)(2,1)} %get-tuple-element.278, f32[160,1536]{1,0:T(8,128)S(1)} %get-tuple-element.279, f32[1536]{0:T(1024)S(1)} %get-tuple-element.281, ...), kind=kOutput, calls=%fused_computation.13.clone.1 | convolution fusion | flops 757678080 | bytes 8657056 | tf_op jit(solution)/shard_map/while/body/eval_jaxpr/dot_general | solution.py:91
  120.7 3.7 %fusion.134 = f32[160,1536]{1,0:T(8,128)S(1)} fusion(f32[160,1536]{1,0:T(8,128)S(1)} %copy.73, f32[160,1536]{1,0:T(8,128)} %get-tuple-element.280, bf16[1536,1536]{1,0:T(8,128)(2,1)} %get-tuple-element.278, f32[160,1536]{1,0:T(8,128)S(1)} %get-tuple-element.279, f32[1536]{0:T(1024)S(1)} %get-tuple-element.281, ...), kind=kOutput, calls=%fused_computation.13.clone.1 | convolution fusion | flops 757678080 | bytes 8657056 | tf_op jit(solution)/shard_map/while/body/eval_jaxpr/dot_general | solution.py:91
  124.5 3.7 %fusion.134 = f32[160,1536]{1,0:T(8,128)S(1)} fusion(f32[160,1536]{1,0:T(8,128)S(1)} %copy.73, f32[160,1536]{1,0:T(8,128)} %get-tuple-element.280, bf16[1536,1536]{1,0:T(8,128)(2,1)} %get-tuple-element.278, f32[160,1536]{1,0:T(8,128)S(1)} %get-tuple-element.279, f32[1536]{0:T(1024)S(1)} %get-tuple-element.281, ...), kind=kOutput, calls=%fused_computation.13.clone.1 | convolution fusion | flops 757678080 | bytes 8657056 | tf_op jit(solution)/shard_map/while/body/eval_jaxpr/dot_general | solution.py:91
  141.3 21.2 %slice_reduce_fusion = (f32[8192]{0:T(1024)S(1)}, f32[8192]{0:T(1024)S(1)}, f32[8192]{0:T(1024)S(1)}, f32[8192]{0:T(1024)S(1)}, f32[8192]{0:T(1024)S(1)}, /*index=5*/f32[8192]{0:T(1024)S(1)}) fusion(f32[6,8192]{0,1:T(8,128)} %scatter_custom_fusion.1), kind=kLoop, calls=%fused_computation.16 | loop fusion | bytes 393216 | tf_op jit(solution)/shard_map/slice | solution.py:119
  173.1 4.7 %collective-permute-done.4 = f32[3,64,1]{2,1,0:T(8,128)S(1)} collective-permute-done((f32[3,64,1]{2,1,0:T(8,128)S(1)}, f32[3,64,1]{2,1,0:T(8,128)S(1)}, u32[]{:S(2)}, u32[]{:S(2)}) %collective-permute-start.4) | collective-permute-done | bytes 800 | tf_op jit(solution)/shard_map/ppermute | solution.py:69
  184.7 3.6 %collective-permute-start.7 = (f32[6,1,128]{2,1,0:T(1,128)S(1)}, f32[6,1,128]{2,1,0:T(1,128)}, u32[]{:S(2)}, u32[]{:S(2)}) collective-permute-start(f32[6,1,128]{2,1,0:T(1,128)S(1)} %get-tuple-element.195), channel_id=1, source_target_pairs={{0,16},{16,32},{32,48},{48,64},{64,80},{80,96},{96,112},{1,17},{17... | collective-permute-start | bytes 9224 | tf_op jit(solution)/shard_map/ppermute | solution.py:68
  194.8 7.8 %all-to-all-start = ((f32[128,2,3072]{2,1,0:T(2,128)}), f32[128,2,3072]{2,1,0:T(2,128)S(1)}, u32[]{:S(2)}, u32[]{:S(2)}) async-start(f32[128,2,3072]{2,1,0:T(2,128)} %all_to_all.8), calls=%async_computation | async-start | bytes 6291456 | tf_op jit(solution)/shard_map/all_to_all | solution.py:47
  216.2 23.6 %collective-permute-done.13 = f32[6,64,1]{2,1,0:T(8,128)S(1)} collective-permute-done((f32[6,64,1]{2,1,0:T(8,128)S(1)}, f32[6,64,1]{2,1,0:T(8,128)S(1)}, u32[]{:S(2)}, u32[]{:S(2)}) %collective-permute-start.13) | collective-permute-done | bytes 1568 | tf_op jit(solution)/shard_map/ppermute | solution.py:68
  255.3 4.4 %collective-permute-done.16 = f32[6,64,1]{2,1,0:T(8,128)S(1)} collective-permute-done((f32[6,64,1]{2,1,0:T(8,128)S(1)}, f32[6,64,1]{2,1,0:T(8,128)S(1)}, u32[]{:S(2)}, u32[]{:S(2)}) %collective-permute-start.16) | collective-permute-done | bytes 1568 | tf_op jit(solution)/shard_map/ppermute | solution.py:69
  260.6 9.8 %all-reduce.16 = (f32[]{:T(128)}, f32[]{:T(128)}) all-reduce(f32[]{:T(128)} %get-tuple-element.136, f32[]{:T(128)} %get-tuple-element.135), channel_id=1, replica_groups=mesh['row_0'=4,'row_1'=2,'col_0'=4,'col_1'=4] {'row_0'}, use_global_device_ids=true, to_apply=%region_6.7 | all-reduce | flops 2 | bytes 16 | tf_op jit(solution)/shard_map/psum | solution.py:81
  273.5 13.5 %all-reduce.15 = (f32[]{:T(128)}, f32[]{:T(128)}) all-reduce(f32[]{:T(128)} %get-tuple-element.157, f32[]{:T(128)} %get-tuple-element.158), channel_id=1, replica_groups=mesh['row_0'=4,'row_1'=2,'col_0'=4,'col_1'=4] {'col_0'}, use_global_device_ids=true, to_apply=%region_8.9 | all-reduce | flops 2 | bytes 16 | tf_op jit(solution)/shard_map/psum | solution.py:81
  287.0 11.0 %all-reduce.14 = (f32[]{:T(128)}, f32[]{:T(128)}) all-reduce(f32[]{:T(128)} %get-tuple-element.153, f32[]{:T(128)} %get-tuple-element.154), channel_id=1, replica_groups=mesh['row_0'=4,'row_1'=2,'col_0'=4,'col_1'=4] {'col_1'}, use_global_device_ids=true, to_apply=%region_9.10 | all-reduce | flops 2 | bytes 16 | tf_op jit(solution)/shard_map/psum | solution.py:81
  (218 shorter events, 116.0 us)
Async XLA Ops:
  0.6 46.8 %copy-start.23 = (u32[128]{0:T(128)S(1)}, u32[128]{0:T(128)}, u32[]{:S(2)}) copy-start(u32[128]{0:T(128)} %constant.205) | copy-start | bytes 1540
  0.7 56.8 %copy-start.22 = (u32[128]{0:T(128)S(1)}, u32[128]{0:T(128)}, u32[]{:S(2)}) copy-start(u32[128]{0:T(128)} %constant.210) | copy-start | bytes 1540
  0.7 61.8 %copy-start.1 = (f32[160,1536]{1,0:T(8,128)S(1)}, f32[160,1536]{1,0:T(8,128)}, u32[]{:S(2)}) copy-start(f32[160,1536]{1,0:T(8,128)} %param.23) | copy-start | bytes 2949124
  0.7 61.7 %copy-start.21 = (s32[160]{0:T(256)S(1)}, s32[160]{0:T(256)}, u32[]{:S(2)}) copy-start(s32[160]{0:T(256)} %param.25) | copy-start | bytes 1924
  2.5 170.6 %collective-permute-start.5 = (f32[3,64,1]{2,1,0:T(8,128)}, f32[3,64,1]{2,1,0:T(8,128)}, u32[]{:S(2)}, u32[]{:S(2)}) collective-permute-start(f32[3,64,1]{2,1,0:T(8,128)} %get-tuple-element.198), channel_id=1, source_target_pairs={{0,1},{1,2},{2,3},{3,4},{4,5},{5,6},{6,7},{7,8},{8,9},{9,10},{10,1... | collective-permute-start | bytes 2312 | tf_op jit(solution)/shard_map/ppermute | solution.py:68
  8.0 169.7 %collective-permute-start.2 = (f32[3,1,128]{2,1,0:T(1,128)}, f32[3,1,128]{2,1,0:T(1,128)}, u32[]{:S(2)}, u32[]{:S(2)}) collective-permute-start(f32[3,1,128]{2,1,0:T(1,128)} %get-tuple-element.200), channel_id=1, source_target_pairs={{16,0},{32,16},{48,32},{64,48},{80,64},{96,80},{112,96},{17,1},{33... | collective-permute-start | bytes 4616 | tf_op jit(solution)/shard_map/ppermute | solution.py:69
  9.3 168.5 %collective-permute-start.3 = (f32[3,1,128]{2,1,0:T(1,128)S(1)}, f32[3,1,128]{2,1,0:T(1,128)}, u32[]{:S(2)}, u32[]{:S(2)}) collective-permute-start(f32[3,1,128]{2,1,0:T(1,128)S(1)} %get-tuple-element.199), channel_id=1, source_target_pairs={{0,16},{16,32},{32,48},{48,64},{64,80},{80,96},{96,112},{1,17},{17... | collective-permute-start | bytes 4616 | tf_op jit(solution)/shard_map/ppermute | solution.py:68
  13.7 164.1 %copy-start.10 = (f32[64,128]{1,0:T(8,128)}, f32[64,128]{1,0:T(8,128)S(1)}, u32[]{:S(2)}) copy-start(f32[64,128]{1,0:T(8,128)S(1)} %get-tuple-element.201) | copy-start | bytes 98308
  14.2 158.1 %collective-permute-start = (f32[1,128]{1,0:T(1,128)}, f32[1,128]{1,0:T(1,128)}, u32[]{:S(2)}, u32[]{:S(2)}) collective-permute-start(f32[1,128]{1,0:T(1,128)} %slice_bitcast_fusion.23), channel_id=1, source_target_pairs={{0,16},{16,32},{32,48},{48,64},{64,80},{80,96},{96,112},{1,17},{17... | collective-permute-start | bytes 1544 | tf_op jit(solution)/shard_map/ppermute | solution.py:57
  17.9 153.1 %collective-permute-start.1 = (f32[64,1]{1,0:T(8,128)}, f32[64,1]{1,0:T(8,128)S(1)}, u32[]{:S(2)}, u32[]{:S(2)}) collective-permute-start(f32[64,1]{1,0:T(8,128)} %slice.472), channel_id=1, source_target_pairs={{0,1},{1,2},{2,3},{3,4},{4,5},{5,6},{6,7},{7,8},{8,9},{9,10},{10,1... | collective-permute-start | bytes 776 | tf_op jit(solution)/shard_map/ppermute | solution.py:57
  171.0 6.8 %collective-permute-start.4 = (f32[3,64,1]{2,1,0:T(8,128)S(1)}, f32[3,64,1]{2,1,0:T(8,128)S(1)}, u32[]{:S(2)}, u32[]{:S(2)}) collective-permute-start(f32[3,64,1]{2,1,0:T(8,128)S(1)} %copy-done.18), channel_id=1, source_target_pairs={{1,0},{2,1},{3,2},{4,3},{5,4},{6,5},{7,6},{8,7},{9,8},{10,9},{11,1... | collective-permute-start | bytes 2312 | tf_op jit(solution)/shard_map/ppermute | solution.py:69
  179.9 22.8 %collective-permute-start.9 = (f32[6,64,1]{2,1,0:T(8,128)}, f32[6,64,1]{2,1,0:T(8,128)}, u32[]{:S(2)}, u32[]{:S(2)}) collective-permute-start(f32[6,64,1]{2,1,0:T(8,128)} %get-tuple-element.194), channel_id=1, source_target_pairs={{0,1},{1,2},{2,3},{3,4},{4,5},{5,6},{6,7},{7,8},{8,9},{9,10},{10,1... | collective-permute-start | bytes 4616 | tf_op jit(solution)/shard_map/ppermute | solution.py:68
  183.5 19.3 %collective-permute-start.6 = (f32[6,1,128]{2,1,0:T(1,128)S(1)}, f32[6,1,128]{2,1,0:T(1,128)}, u32[]{:S(2)}, u32[]{:S(2)}) collective-permute-start(f32[6,1,128]{2,1,0:T(1,128)S(1)} %get-tuple-element.196), channel_id=1, source_target_pairs={{16,0},{32,16},{48,32},{64,48},{80,64},{96,80},{112,96},{17,1},{33... | collective-permute-start | bytes 9224 | tf_op jit(solution)/shard_map/ppermute | solution.py:69
  184.7 18.0 %collective-permute-start.7 = (f32[6,1,128]{2,1,0:T(1,128)S(1)}, f32[6,1,128]{2,1,0:T(1,128)}, u32[]{:S(2)}, u32[]{:S(2)}) collective-permute-start(f32[6,1,128]{2,1,0:T(1,128)S(1)} %get-tuple-element.195), channel_id=1, source_target_pairs={{0,16},{16,32},{32,48},{48,64},{64,80},{80,96},{96,112},{1,17},{17... | collective-permute-start | bytes 9224 | tf_op jit(solution)/shard_map/ppermute | solution.py:68
  188.4 14.3 %collective-permute-start.8 = (f32[6,64,1]{2,1,0:T(8,128)}, f32[6,64,1]{2,1,0:T(8,128)}, u32[]{:S(2)}, u32[]{:S(2)}) collective-permute-start(f32[6,64,1]{2,1,0:T(8,128)} %get-tuple-element.193), channel_id=1, source_target_pairs={{1,0},{2,1},{3,2},{4,3},{5,4},{6,5},{7,6},{8,7},{9,8},{10,9},{11,1... | collective-permute-start | bytes 4616 | tf_op jit(solution)/shard_map/ppermute | solution.py:69
  194.8 106.1 %all-to-all-start = ((f32[128,2,3072]{2,1,0:T(2,128)}), f32[128,2,3072]{2,1,0:T(2,128)S(1)}, u32[]{:S(2)}, u32[]{:S(2)}) async-start(f32[128,2,3072]{2,1,0:T(2,128)} %all_to_all.8), calls=%async_computation | async-start | bytes 6291456 | tf_op jit(solution)/shard_map/all_to_all | solution.py:47
  207.6 34.5 %collective-permute-start.10 = (f32[6,1,128]{2,1,0:T(1,128)S(1)}, f32[6,1,128]{2,1,0:T(1,128)S(1)}, u32[]{:S(2)}, u32[]{:S(2)}) collective-permute-start(f32[6,1,128]{2,1,0:T(1,128)S(1)} %get-tuple-element.192), channel_id=1, source_target_pairs={{16,0},{32,16},{48,32},{64,48},{80,64},{96,80},{112,96},{17,1},{33... | collective-permute-start | bytes 9224 | tf_op jit(solution)/shard_map/ppermute | solution.py:69
  208.9 33.2 %collective-permute-start.11 = (f32[6,1,128]{2,1,0:T(1,128)S(1)}, f32[6,1,128]{2,1,0:T(1,128)S(1)}, u32[]{:S(2)}, u32[]{:S(2)}) collective-permute-start(f32[6,1,128]{2,1,0:T(1,128)S(1)} %get-tuple-element.191), channel_id=1, source_target_pairs={{0,16},{16,32},{32,48},{48,64},{64,80},{80,96},{96,112},{1,17},{17... | collective-permute-start | bytes 9224 | tf_op jit(solution)/shard_map/ppermute | solution.py:68
  212.0 27.8 %collective-permute-start.13 = (f32[6,64,1]{2,1,0:T(8,128)S(1)}, f32[6,64,1]{2,1,0:T(8,128)S(1)}, u32[]{:S(2)}, u32[]{:S(2)}) collective-permute-start(f32[6,64,1]{2,1,0:T(8,128)S(1)} %get-tuple-element.190), channel_id=1, source_target_pairs={{0,1},{1,2},{2,3},{3,4},{4,5},{5,6},{6,7},{7,8},{8,9},{9,10},{10,1... | collective-permute-start | bytes 4616 | tf_op jit(solution)/shard_map/ppermute | solution.py:68
  214.9 27.1 %collective-permute-start.12 = (f32[6,64,1]{2,1,0:T(8,128)S(1)}, f32[6,64,1]{2,1,0:T(8,128)S(1)}, u32[]{:S(2)}, u32[]{:S(2)}) collective-permute-start(f32[6,64,1]{2,1,0:T(8,128)S(1)} %get-tuple-element.189), channel_id=1, source_target_pairs={{1,0},{2,1},{3,2},{4,3},{5,4},{6,5},{7,6},{8,7},{9,8},{10,9},{11,1... | collective-permute-start | bytes 4616 | tf_op jit(solution)/shard_map/ppermute | solution.py:69
  242.5 17.2 %collective-permute-start.14 = (f32[6,1,128]{2,1,0:T(1,128)S(1)}, f32[6,1,128]{2,1,0:T(1,128)S(1)}, u32[]{:S(2)}, u32[]{:S(2)}) collective-permute-start(f32[6,1,128]{2,1,0:T(1,128)S(1)} %get-tuple-element.188), channel_id=1, source_target_pairs={{16,0},{32,16},{48,32},{64,48},{80,64},{96,80},{112,96},{17,1},{33... | collective-permute-start | bytes 9224 | tf_op jit(solution)/shard_map/ppermute | solution.py:69
  243.8 15.9 %collective-permute-start.15 = (f32[6,1,128]{2,1,0:T(1,128)S(1)}, f32[6,1,128]{2,1,0:T(1,128)S(1)}, u32[]{:S(2)}, u32[]{:S(2)}) collective-permute-start(f32[6,1,128]{2,1,0:T(1,128)S(1)} %get-tuple-element.187), channel_id=1, source_target_pairs={{0,16},{16,32},{32,48},{48,64},{64,80},{80,96},{96,112},{1,17},{17... | collective-permute-start | bytes 9224 | tf_op jit(solution)/shard_map/ppermute | solution.py:68
  247.0 8.4 %collective-permute-start.17 = (f32[6,64,1]{2,1,0:T(8,128)S(1)}, f32[6,64,1]{2,1,0:T(8,128)S(1)}, u32[]{:S(2)}, u32[]{:S(2)}) collective-permute-start(f32[6,64,1]{2,1,0:T(8,128)S(1)} %get-tuple-element.186), channel_id=1, source_target_pairs={{0,1},{1,2},{2,3},{3,4},{4,5},{5,6},{6,7},{7,8},{8,9},{9,10},{10,1... | collective-permute-start | bytes 4616 | tf_op jit(solution)/shard_map/ppermute | solution.py:68
  250.2 9.5 %collective-permute-start.16 = (f32[6,64,1]{2,1,0:T(8,128)S(1)}, f32[6,64,1]{2,1,0:T(8,128)S(1)}, u32[]{:S(2)}, u32[]{:S(2)}) collective-permute-start(f32[6,64,1]{2,1,0:T(8,128)S(1)} %get-tuple-element.185), channel_id=1, source_target_pairs={{1,0},{2,1},{3,2},{4,3},{5,4},{6,5},{7,6},{8,7},{9,8},{10,9},{11,1... | collective-permute-start | bytes 4616 | tf_op jit(solution)/shard_map/ppermute | solution.py:69
  (20 other events, 416.2 us)
where the time goes:
time: 313 us; the launch traced here: 311 us
  local copies, waits for them, and re-layouts  81.1 us (26%)
  blocking collectives  65.4 us (21%)
  starting transfers between devices  51.3 us (16%)
  waiting for transfers between devices  37.8 us (12%)
  matrix products  37.1 us (12%)
  other arithmetic  30.9 us (10%)
  between operations  7.23 us (2%)
    psum x4, blocking collectives, by_axis(): return functools.reduce(lax.psum, axes, array)  37.4 us
    dot_general x9, matrix products, advance(): jnp.dot(current.astype(jnp.bfloat16), stiffness, preferred_element_type=j...  33.3 us
    unnamed x4, blocking collectives  28 us
    ppermute x8, starting transfers between devices, padded_2(): lax.ppermute(last, axis, up)  27.1 us
    ppermute x8, waiting for transfers between devices, padded_2(): lax.ppermute(last, axis, up)  26.6 us
    gather x1, local copies, waits for them, and re-layouts, micro_solve(): diagonal = jnp.diagonal(stiffness).astype(jnp.float32)  24.3 us
    slice x1, local copies, waits for them, and re-layouts, block_solve(): d00 = scale + tangent[0]  21.2 us
    ppermute x8, waiting for transfers between devices, padded_2(): lax.ppermute(first, axis, [(b, a) for a, b in up])  11.2 us
  transfers between devices with their start and end apart: 19, of which 5 were waited for; matrix products, arithmetic and copies ran while one was open for 43% of the time, Pallas kernels for 0%

commit v1 on v0

v1 whole, which is shorter than its diff:
```python
import functools

import jax
import jax.numpy as jnp
from jax import lax
from jax.experimental import pallas as pl
from jax.experimental.pallas import tpu as pltpu
from jax.sharding import PartitionSpec as P


MAX_STEPS = 9
SWEEPS = 3
HALO = 4
FIELDS = 9
LANES = 128
ROWS_COLS = ("row", "col")
VMEM = pl.BlockSpec(memory_space=pltpu.VMEM)
SMEM = pl.BlockSpec(memory_space=pltpu.SMEM)
ANY = pl.BlockSpec(memory_space=pl.ANY)
F32 = jnp.float32
BF16 = jnp.bfloat16


def iota(shape, dim):
    return lax.broadcasted_iota(jnp.int32, shape, dim)


def three_parts(x):
    high = x.astype(BF16)
    rest = x - high.astype(F32)
    middle = rest.astype(BF16)
    low = (rest - middle.astype(F32)).astype(BF16)
    return high, middle, low


def times_transposed(a, b):
    return lax.dot_general(a, b, (((1,), (1,)), ((), ())), preferred_element_type=F32)


def put_row_edges(get, first_ref, last_ref, rows):
    for c in range(FIELDS):
        field = get(c)
        first_ref[HALO * c : HALO * (c + 1), :] = field[:HALO]
        last_ref[HALO * c : HALO * (c + 1), :] = field[rows - HALO :]


def with_row_halo(field, below, above, c):
    part = slice(HALO * c, HALO * (c + 1))
    return jnp.concatenate([field, below[part], above[part]], axis=0)


def fields_kernel(jump_ref, external_ref, cohesive_ref, mask_ref, slots_ref, out_ref, first_ref, last_ref):
    rows, lanes = cohesive_ref.shape
    slots = slots_ref.shape[1]
    ids = slots_ref[0:1, :]
    live = slots_ref[1:2, :] > 0
    at_row = ((iota((rows, slots), 0) == ids // lanes) & live).astype(F32).astype(BF16)
    at_lane = (iota((lanes, slots), 0) == ids % lanes).astype(F32).astype(BF16)
    soft = times_transposed(at_row, at_lane)
    for c in range(3):
        out_ref[c] = jump_ref[c]
        out_ref[3 + c] = external_ref[c]
    out_ref[6] = (1.0 - soft) * cohesive_ref[...]
    out_ref[7] = 0.25 + 0.75 * mask_ref[0].astype(F32)
    out_ref[8] = 0.25 + 0.75 * mask_ref[1].astype(F32)
    put_row_edges(lambda c: out_ref[c], first_ref, last_ref, rows)


def lane_edges_kernel(field_ref, below_ref, above_ref, out_ref):
    below, above = below_ref[...], above_ref[...]
    rows = field_ref.shape[1] + 2 * HALO
    lane = iota((rows, LANES), 1)
    wide = jnp.zeros((rows, LANES), F32)
    for c in range(FIELDS):
        whole = with_row_halo(field_ref[c], below, above, c)
        turned = pltpu.roll(whole, (2 * c + 1) * HALO, 1)
        wide = jnp.where(lane // (2 * HALO) == c, turned, wide)
    square = jnp.concatenate([wide, jnp.zeros((LANES - rows, LANES), F32)], axis=0)
    out_ref[...] = square.T[: 2 * HALO * FIELDS]


def newton_kernel(
    slots_ref, jump_ref, stiffness_ref, coupling_ref, state_in_ref, history_ref,
    state_ref, grid_ref, first_ref, last_ref,
    damage_ref, load_ref, diagonal_ref, rounded_ref,
):
    slots, cells = state_in_ref.shape
    rows, lanes = jump_ref.shape[1:]
    wide = slots_ref.shape[1]
    own = iota((slots, wide), 0) == iota((slots, wide), 1)

    def column(values):
        return jnp.sum(jnp.where(own, values, 0.0), axis=1, keepdims=True)

    ids_row = slots_ref[0:1, :]
    steps_row = slots_ref[1:2, :]
    steps = column(steps_row.astype(F32))
    at_x = column((ids_row // lanes).astype(F32))
    at_y = column((ids_row % lanes).astype(F32))
    pick_x = (iota((slots, rows), 1).astype(F32) == at_x).astype(F32).astype(BF16)
    pick_y = iota((slots, lanes), 1).astype(F32) == at_y
    drive = []
    for c in range(3):
        parts = three_parts(jump_ref[c])
        picked = [jnp.dot(pick_x, part, preferred_element_type=F32) for part in parts]
        whole = (picked[0] + picked[1]) + picked[2]
        drive.append(jnp.sum(jnp.where(pick_y, whole, 0.0), axis=1, keepdims=True))
    eye = iota((LANES, LANES), 0) == iota((LANES, LANES), 1)
    for t in range(cells // LANES):
        part = slice(t * LANES, (t + 1) * LANES)
        block = stiffness_ref[part, part].astype(F32)
        diagonal_ref[:, part] = jnp.sum(jnp.where(eye, block, 0.0), axis=0, keepdims=True)
    load_ref[...] = (
        drive[0] * coupling_ref[0:1, :] + drive[1] * coupling_ref[1:2, :] + drive[2] * coupling_ref[2:3, :]
    )
    damage_ref[...] = jnp.exp(-history_ref[...])
    first = state_in_ref[...]
    state_ref[...] = first
    rounded_ref[0] = first.astype(BF16)
    width = 256

    def advance(count, carry):
        now = lax.rem(count, 2)
        rounded = rounded_ref[now]
        moves = count.astype(F32) < steps
        for t in range(cells // width):
            part = slice(t * width, (t + 1) * width)
            force = jnp.dot(rounded, stiffness_ref[:, part], preferred_element_type=F32)
            current = state_ref[:, part]
            bent = jnp.tanh(current)
            damage = damage_ref[:, part]
            misfit = force + damage * bent - load_ref[:, part]
            slope = diagonal_ref[:, part] + damage * (1.0 - bent * bent)
            current = jnp.where(moves, current - misfit / slope, current)
            state_ref[:, part] = current
            rounded_ref[1 - now, :, part] = current.astype(BF16)
        return carry

    lax.fori_loop(0, MAX_STEPS, advance, 0)
    bent = jnp.tanh(state_ref[...])
    damage = damage_ref[...]
    pull = damage * bent
    weight = damage * (1.0 - bent * bent)
    c0, c1, c2 = (coupling_ref[k : k + 1, :] for k in range(3))
    sums = [jnp.sum(pull * c, axis=1, keepdims=True) for c in (c0, c1, c2)]
    sums += [
        jnp.sum(weight * c, axis=1, keepdims=True)
        for c in (c0 * c0, c1 * c1, c2 * c2, c0 * c1, c0 * c2, c1 * c2)
    ]
    lane = iota((slots, LANES), 1)
    table = jnp.zeros((slots, LANES), F32)
    for k, value in enumerate(sums):
        table = jnp.where(lane == k, value * (1.0 / cells), table)
    table = jnp.where(steps > 0.0, table, 0.0)
    table = jnp.concatenate([table, jnp.zeros((wide - slots, LANES), F32)], axis=0).T
    at_row = iota((rows, wide), 0) == ids_row // lanes
    at_lane = (iota((lanes, wide), 0) == ids_row % lanes).astype(F32).astype(BF16)
    pieces = []
    for c in range(FIELDS):
        placed = jnp.where(at_row, table[c : c + 1, :], 0.0)
        pieces.extend(three_parts(placed))
    spread = times_transposed(jnp.concatenate(pieces, axis=0), at_lane)
    for c in range(FIELDS):
        at = 3 * c * rows
        grid_ref[c] = spread[at : at + rows] + spread[at + rows : at + 2 * rows] + spread[at + 2 * rows : at + 3 * rows]
    put_row_edges(lambda c: grid_ref[c], first_ref, last_ref, rows)


def copy_rows(source_ref, target_ref, steps_ref, start):
    slots, cells = source_ref.shape
    sides = target_ref.shape[1] // 2
    width = cells // sides
    block_rows = 2 * target_ref.shape[0]

    def one(i, rank):
        alive = steps_ref[i] > 0

        @pl.when(alive)
        def _():
            at = lax.rem(rank, block_rows)
            block, side = at // 2, lax.rem(at, 2)
            for k in range(sides):
                target_ref[block, pl.ds(side * sides + k, 1), :] = source_ref[pl.ds(i, 1), k * width : (k + 1) * width]

        return rank + alive.astype(jnp.int32)

    lax.fori_loop(0, slots, one, start)


def pack_history_kernel(here_ref, steps_ref, counts_ref, history_ref, out_ref, plan_ref):
    devices = counts_ref.shape[0]
    here = here_ref[0]
    counts = counts_ref[...]
    before = (iota((devices, devices), 1) < iota((devices, devices), 0)).astype(F32).astype(BF16)
    starts = jnp.dot(before, counts.astype(BF16), preferred_element_type=F32)
    row = iota((devices, LANES), 0)
    start = jnp.sum(jnp.where(row < here, counts, 0.0)[:, 0:1]).astype(jnp.int32)
    total = jnp.sum(counts, axis=0, keepdims=True)
    slot = iota((1, LANES), 1)
    wanted = (2 * (here + devices * (slot // 2)) + slot % 2).astype(F32)
    source = jnp.sum(jnp.where(starts <= wanted, 1.0, 0.0), axis=0, keepdims=True) - 1.0
    index = jnp.where(wanted < total, 2.0 * source + (slot % 2).astype(F32), -1.0).astype(jnp.int32)
    line = iota((8, LANES), 0)
    plan_ref[...] = jnp.where(line == 0, index, jnp.where(line == 1, start, 0))
    copy_rows(history_ref, out_ref, steps_ref, start)


def pack_state_kernel(plan_ref, steps_ref, state_ref, out_ref):
    copy_rows(state_ref, out_ref, steps_ref, plan_ref[1, 0])


def after_kernel(data_ref, first_ref, second_ref, out_ref):
    del data_ref, first_ref, second_ref, out_ref


def unpack_kernel(plan_ref, state_ref, history_ref, new_state_ref, new_history_ref):
    new_cap, cells = new_state_ref.shape
    sides = state_ref.shape[1] // 2
    width = cells // sides

    def one(s, carry):
        index = plan_ref[0, s]
        valid = index >= 0
        at = jnp.maximum(index, 0)
        block, side = at // 2, lax.rem(at, 2)
        for k in range(sides):
            part = slice(k * width, (k + 1) * width)
            state = state_ref[block, pl.ds(side * sides + k, 1), :]
            history = history_ref[block, pl.ds(side * sides + k, 1), :]
            new_state_ref[pl.ds(s, 1), part] = jnp.where(valid, state, 0.0)
            new_history_ref[pl.ds(s, 1), part] = jnp.where(valid, jnp.maximum(history, jnp.abs(state)), 0.0)
        return carry

    lax.fori_loop(0, new_cap, one, 0)


def macro_kernel(
    place_ref, load_ref,
    field_ref, f_below_ref, f_above_ref, f_left_ref, f_right_ref,
    grid_ref, g_below_ref, g_above_ref, g_left_ref, g_right_ref,
    moved_ref, sums_ref,
):
    rows = field_ref.shape[1]
    tall = rows + 2 * HALO
    lane = iota((tall, LANES), 1)
    line = iota((tall, LANES), 0)
    row_at, col_at = place_ref[0], place_ref[1]
    has_above = (row_at > 0).astype(jnp.int32)
    has_below = (row_at < place_ref[2] - 1).astype(jnp.int32)
    has_left = (col_at > 0).astype(jnp.int32)
    has_right = (col_at < place_ref[3] - 1).astype(jnp.int32)
    row_ok = jnp.where(line < rows, 1, jnp.where(line < rows + HALO, has_below, has_above)) > 0
    side_ok = jnp.where(lane < HALO, has_right, jnp.where(lane >= LANES - HALO, has_left, 0)) > 0
    valid = (row_ok, row_ok & side_ok)

    def padded(ref, below_ref, above_ref, left_ref, right_ref):
        below, above = below_ref[...], above_ref[...]
        fill = jnp.zeros((LANES - left_ref.shape[0], LANES), F32)
        left = jnp.concatenate([left_ref[...], fill], axis=0).T[:tall]
        right = jnp.concatenate([right_ref[...], fill], axis=0).T[:tall]

        def one(c):
            middle = with_row_halo(ref[c], below, above, c)
            from_left = pltpu.roll(left, (LANES - HALO - 2 * HALO * c) % LANES, 1)
            from_right = pltpu.roll(right, (LANES - HALO - 2 * HALO * c) % LANES, 1)
            side = jnp.where(lane >= LANES - HALO, from_left, jnp.where(lane < HALO, from_right, 0.0))
            return (middle, side)

        return one

    def pairs(f, *operands):
        return tuple(f(*parts) for parts in zip(*operands))

    def below_of(v):
        return pairs(lambda x: pltpu.roll(x, tall - 1, 0), v)

    def above_of(v):
        return pairs(lambda x: pltpu.roll(x, 1, 0), v)

    def right_of(v):
        a, b = (pltpu.roll(x, LANES - 1, 1) for x in v)
        end = lane == LANES - 1
        return (jnp.where(end, b, a), jnp.where(end, a, b))

    def left_of(v):
        a, b = (pltpu.roll(x, 1, 1) for x in v)
        end = lane == 0
        return (jnp.where(end, b, a), jnp.where(end, a, b))

    field = padded(field_ref, f_below_ref, f_above_ref, f_left_ref, f_right_ref)
    grid = padded(grid_ref, g_below_ref, g_above_ref, g_left_ref, g_right_ref)
    bond_x, bond_y = field(7), field(8)
    low_x, low_y = above_of(bond_x), left_of(bond_y)
    scale = pairs(lambda a, b, c, d, e: a + b + c + d + e, bond_x, low_x, bond_y, low_y, field(6))

    def neighbours(v):
        return pairs(
            lambda bx, vb, lx, va, by, vr, ly, vl: bx * vb + lx * va + by * vr + ly * vl,
            bond_x, below_of(v), low_x, above_of(v), bond_y, right_of(v), low_y, left_of(v),
        )

    load = load_ref[0]
    sources = []
    for c in range(3):
        jump = field(c)
        external = field(3 + c)
        residual = pairs(
            lambda s, j, n, t, e: s * j - n + t - load * e, scale, jump, neighbours(jump), grid(c), external
        )
        sources.append((pairs(lambda r: -r, residual), external))

    def inverse_of(s, t00, t11, t22, t01, t02, t12, ok):
        d00, d11, d22 = s + t00, s + t11, s + t22
        c00 = d11 * d22 - t12 * t12
        c11 = d00 * d22 - t02 * t02
        c22 = d00 * d11 - t01 * t01
        c01 = t02 * t12 - t01 * d22
        c02 = t01 * t12 - t02 * d11
        c12 = t01 * t02 - d00 * t12
        determinant = d00 * c00 + t01 * c01 + t02 * c02
        over = jnp.where(ok, 1.0 / jnp.where(ok, determinant, 1.0), 0.0)
        return tuple(c * over for c in (c00, c11, c22, c01, c02, c12))

    both = pairs(inverse_of, scale, *(grid(3 + k) for k in range(6)), valid)
    i00, i11, i22, i01, i02, i12 = (tuple(both[t][k] for t in range(2)) for k in range(6))

    def dot3(a, x, b, y, c, z):
        return pairs(lambda a, x, b, y, c, z: a * x + b * y + c * z, a, x, b, y, c, z)

    def solve(w):
        return [
            dot3(i00, w[0], i01, w[1], i02, w[2]),
            dot3(i01, w[0], i11, w[1], i12, w[2]),
            dot3(i02, w[0], i12, w[1], i22, w[2]),
        ]

    done = []
    for half in range(2):
        source = [sources[c][half] for c in range(3)]
        iterate = solve(source)
        for _ in range(SWEEPS):
            iterate = solve([pairs(jnp.add, source[c], neighbours(iterate[c])) for c in range(3)])
        done.append([iterate[c][0][:rows] for c in range(3)])
    cross = square = 0.0
    for c in range(3):
        moved_ref[c] = done[0][c]
        moved_ref[3 + c] = done[1][c]
        cross = cross + done[0][c] * done[1][c]
        square = square + done[1][c] * done[1][c]
    half = iota(sums_ref.shape, 1) < LANES // 2
    sums_ref[...] = jnp.where(half, jnp.sum(cross), jnp.sum(square))


def finish_kernel(entries, load_ref, radius_ref, sums_ref, jump_ref, moved_ref, new_jump_ref, new_load_ref):
    whole = jnp.sum(sums_ref[...], axis=0, keepdims=True)
    half = iota(whole.shape, 1) < LANES // 2
    other = pltpu.roll(whole, LANES // 2, 1)
    cross, square = jnp.where(half, whole, other), jnp.where(half, other, whole)
    shifted = square + 0.25 * entries
    increment = (radius_ref[0] * (entries**0.5) * jnp.sqrt(shifted) - cross) / shifted
    for c in range(3):
        new_jump_ref[c] = jump_ref[c] + moved_ref[c] + increment * moved_ref[3 + c]
    new_load_ref[0] = load_ref[0] + jnp.max(increment)


def shape(*dims, dtype=F32):
    return jax.ShapeDtypeStruct(dims, dtype)


def call(kernel, outs, ins, out_specs, mib, scratch=(), cost=None, aliases=None):
    return pl.pallas_call(
        kernel,
        out_shape=outs,
        in_specs=ins,
        out_specs=out_specs,
        scratch_shapes=scratch,
        cost_estimate=cost,
        input_output_aliases=aliases or {},
        compiler_params=pltpu.CompilerParams(vmem_limit_bytes=mib * 1024 * 1024),
    )


def swap(first, last, axis):
    size = lax.axis_size(axis)
    up = [(i, i + 1) for i in range(size - 1)]
    down = [(i + 1, i) for i in range(size - 1)]
    above = lax.ppermute(last, axis, up)
    below = lax.ppermute(first, axis, down)
    return below, above


def on_device(
    jump, external, cohesive, bond_mask, load_factor, arc_radius, stiffness, coupling,
    old_state, old_history, newton_steps, point_ids,
):
    n_row, n_col = lax.axis_size("row"), lax.axis_size("col")
    devices = n_row * n_col
    row_at, col_at = lax.axis_index("row"), lax.axis_index("col")
    here = (row_at * n_col + col_at).astype(jnp.int32)
    slots, cells = old_state.shape
    _, rows, lanes = jump.shape
    edge = HALO * FIELDS
    blocks = shape(devices, 8, 2 * cells // 8)
    place = jnp.stack([row_at, col_at, n_row, n_col]).astype(jnp.int32)

    table = jnp.zeros((8, 256), jnp.int32)
    table = table.at[0, :slots].set(point_ids).at[1, :slots].set(newton_steps)

    def lane_edges(fields, below, above):
        return call(lane_edges_kernel, shape(2 * edge, LANES), [VMEM] * 3, VMEM, 4)(fields, below, above)

    live = jnp.sum((newton_steps > 0).astype(F32))
    counts = lax.all_to_all(jnp.broadcast_to(live, (devices, LANES)), ROWS_COLS, 0, 0, tiled=True)
    fields, first, last = call(
        fields_kernel,
        (shape(FIELDS, rows, lanes), shape(edge, LANES), shape(edge, LANES)),
        [VMEM] * 5,
        (VMEM,) * 3,
        4,
    )(jump, external, cohesive, bond_mask, table)
    f_below, f_above = swap(first, last, "row")
    turned = lane_edges(fields, f_below, f_above)
    f_right, f_left = swap(turned, turned, "col")
    packed_history, plan = call(
        pack_history_kernel,
        (blocks, shape(8, LANES, dtype=jnp.int32)),
        [SMEM, SMEM, VMEM, VMEM],
        (VMEM, VMEM),
        6,
    )(here[None], newton_steps, counts, old_history)
    history = lax.all_to_all(packed_history, ROWS_COLS, 0, 0, tiled=True)
    state, grid, first, last = call(
        newton_kernel,
        (shape(slots, cells), shape(FIELDS, rows, lanes), shape(edge, LANES), shape(edge, LANES)),
        [VMEM] * 6,
        (VMEM,) * 4,
        28,
        scratch=(
            pltpu.VMEM((slots, cells), F32),
            pltpu.VMEM((slots, cells), F32),
            pltpu.VMEM((1, cells), F32),
            pltpu.VMEM((2, slots, cells), BF16),
        ),
        cost=pl.CostEstimate(
            flops=2 * MAX_STEPS * slots * cells * cells,
            transcendentals=2 * MAX_STEPS * slots * cells,
            bytes_accessed=2 * cells * cells + 12 * slots * cells,
        ),
    )(table, jump, stiffness, coupling, old_state, old_history)
    g_below, g_above = swap(first, last, "row")
    packed_state = call(pack_state_kernel, blocks, [SMEM, SMEM, VMEM], VMEM, 6)(plan, newton_steps, state)
    turned = lane_edges(grid, g_below, g_above)
    g_right, g_left = swap(turned, turned, "col")
    packed_state = call(after_kernel, blocks, [ANY] * 3, ANY, 1, aliases={0: 0})(packed_state, g_right, g_left)
    arrived = lax.all_to_all(packed_state, ROWS_COLS, 0, 0, tiled=True)
    moved, sums = call(
        macro_kernel,
        (shape(6, rows, lanes), shape(devices, LANES)),
        [SMEM, SMEM] + [VMEM] * 10,
        (VMEM, VMEM),
        12,
        cost=pl.CostEstimate(flops=200_000_000, transcendentals=0, bytes_accessed=2_000_000),
    )(
        place, load_factor,
        fields, f_below, f_above, f_left, f_right,
        grid, g_below, g_above, g_left, g_right,
    )
    sums = lax.all_to_all(sums, ROWS_COLS, 0, 0, tiled=True)
    new_state, new_history = call(
        unpack_kernel,
        (shape(slots // 2, cells), shape(slots // 2, cells)),
        [SMEM, VMEM, VMEM],
        (VMEM, VMEM),
        8,
    )(plan, arrived, history)
    new_jump, new_load = call(
        functools.partial(finish_kernel, 3.0 * rows * lanes * devices),
        (shape(3, rows, lanes), shape(1)),
        [SMEM, SMEM, VMEM, VMEM, VMEM],
        (VMEM, SMEM),
        4,
    )(load_factor, arc_radius, sums, jump, moved)
    return (new_jump, new_load, new_state, new_history)


def solution(mesh):
    whole = P(None, "row", "col")
    slot_rows = P(ROWS_COLS, None)
    return jax.shard_map(
        on_device,
        mesh=mesh,
        in_specs=(
            whole, whole, P("row", "col"), whole, P(), P(), P(), P(),
            slot_rows, slot_rows, P(ROWS_COLS), P(ROWS_COLS),
        ),
        out_specs=(whole, P(), slot_rows, slot_rows),
        check_vma=False,
    )
```

time: 313 us -> 153 us (0.49)
  local copies, waits for them, and re-layouts: 81.1 us -> 12.5 us
  blocking collectives: 65.4 us -> 0 us
  matrix products: 37.1 us -> 0 us
  other arithmetic: 30.9 us -> 0.68 us
  Pallas kernels: 0 us -> 29 us
  waiting for transfers between devices: 37.8 us -> 48.3 us
  starting transfers between devices: 51.3 us -> 59.7 us
  between operations: 7.23 us -> 2.18 us
    all_to_all x1 -> x4, waiting for transfers between devices: 0.01 us -> 47.4 us  [the longest x1 23 us: on_device(): arrived = lax.all_to_all(packed_state, ROWS_COLS, 0, 0, tiled=True)]
    psum x4 -> x0, blocking collectives: 37.4 us -> none  [by_axis(): return functools.reduce(lax.psum, axes, array)]
    dot_general x12 -> x0, matrix products: 37.1 us -> none  [the longest x9 33.3 us: advance(): jnp.dot(current.astype(jnp.bfloat16), stiffness, preferred_element_type=j...]
    ppermute x18 -> x8, waiting for transfers between devices: 37.8 us -> 0.87 us  [the longest x4 0.86 us: swap(): above = lax.ppermute(last, axis, up)]
    all_to_all x1 -> x4, starting transfers between devices: 7.81 us -> 38.5 us  [the longest x1 14.6 us: on_device(): sums = lax.all_to_all(sums, ROWS_COLS, 0, 0, tiled=True)]
    gather x4 -> x0, local copies, waits for them, and re-layouts: 29.5 us -> none  [the longest x1 24.3 us: micro_solve(): diagonal = jnp.diagonal(stiffness).astype(jnp.float32)]
    pallas_call x0 -> x10, Pallas kernels: none -> 29 us  [the longest x1 11.8 us: on_device(): call(newton_kernel, (shape(slots, cells), shape(FIELDS, rows, lanes), sha...]
    unnamed x4 -> x0, blocking collectives: 28 us -> none
  transfers between devices with their start and end apart: 19 -> 12, of which waited for: 5 -> 4; matrix products, arithmetic and copies ran while one was open for 43% -> 1% of each run, Pallas kernels for 0% -> 17%
where the time goes in v1:
time: 153 us; the launch traced here: 152 us
  starting transfers between devices  59.7 us (39%)
  waiting for transfers between devices  48.3 us (32%)
  Pallas kernels  29 us (19%)
  local copies, waits for them, and re-layouts  12.5 us (8%)
  between operations  2.18 us (1%)
    all_to_all x1, waiting for transfers between devices, on_device(): arrived = lax.all_to_all(packed_state, ROWS_COLS, 0, 0, tiled=True)  23 us
    all_to_all x1, waiting for transfers between devices, on_device(): history = lax.all_to_all(packed_history, ROWS_COLS, 0, 0, tiled=True)  19.8 us
    ppermute x4, starting transfers between devices, swap(): above = lax.ppermute(last, axis, up)  15.9 us
    all_to_all x1, starting transfers between devices, on_device(): sums = lax.all_to_all(sums, ROWS_COLS, 0, 0, tiled=True)  14.6 us
    all_to_all x1, starting transfers between devices, on_device(): lax.all_to_all(jnp.broadcast_to(live, (devices, LANES)), ROWS_COLS, 0, 0,...  12.4 us
    pallas_call x1, Pallas kernels, on_device(): call(newton_kernel, (shape(slots, cells), shape(FIELDS, rows, lanes), sha...  11.8 us
    unnamed x24, local copies, waits for them, and re-layouts  9.75 us
    all_to_all x1, starting transfers between devices, on_device(): history = lax.all_to_all(packed_history, ROWS_COLS, 0, 0, tiled=True)  6.88 us
  transfers between devices with their start and end apart: 12, of which 4 were waited for; matrix products, arithmetic and copies ran while one was open for 1% of the time, Pallas kernels for 17%

profile of v1, /device:TPU:0, one launch (start us, length us, event | category | flops | bytes accessed | tf_op | source)
XLA Modules:
  0.0 152.3 jit_solution(18370909205450013043)
XLA Ops:
  5.7 1.3 collective-permute-start
  6.9 3.0 %collective-permute-start.1 = (f32[36,128]{1,0:T(8,128)S(1)}, f32[36,128]{1,0:T(8,128)S(1)}, u32[]{:S(2)}, u32[]{:S(2)}) collective-permute-start(f32[36,128]{1,0:T(8,128)S(1)} %get-tuple-element.45), channel_id=1, source_target_pairs={{0,16},{16,32},{32,48},{48,64},{64,80},{80,96},{96,112},{1,17},{17... | collective-permute-start | bytes 55304 | tf_op jit(solution)/shard_map/ppermute | solution.py:387
  10.0 1.2 copy-done
  12.1 2.3 %copy-done.9 = bf16[1536,1536]{1,0:T(8,128)(2,1)S(1)} copy-done((bf16[1536,1536]{1,0:T(8,128)(2,1)S(1)}, bf16[1536,1536]{1,0:T(8,128)(2,1)}, u32[]{:S(2)}) %copy-start.9) | copy-done | bytes 4718616
  14.4 1.2 copy-done.10
  16.4 11.8 %shard_map.149 = (f32[160,1536]{1,0:T(8,128)S(1)}, f32[9,64,128]{2,1,0:T(8,128)S(1)}, f32[36,128]{1,0:T(8,128)S(1)}, f32[36,128]{1,0:T(8,128)S(1)}) custom-call(s32[8,256]{1,0:T(8,128)S(1)} %scatter.9.slots_ref, f32[3,64,128]{2,1,0:T(8,128)S(1)} %copy-done.3, bf16[1536,1536]{1,0:T(8,128)(2,1)S(1)} %copy-done.9, f32[3,1536]{1,0:T(4,128)S(1)} %copy-done.11, ...), custom_call_target="tpu_custom_call" | custom-call | flops 6794772480 | bytes 7667712 | tf_op jit(solution)/shard_map/pallas_call | solution.py:432
  28.1 1.4 collective-permute-start.4
  29.6 3.8 %collective-permute-start.5 = (f32[36,128]{1,0:T(8,128)S(1)}, f32[36,128]{1,0:T(8,128)S(1)}, u32[]{:S(2)}, u32[]{:S(2)}) collective-permute-start(f32[36,128]{1,0:T(8,128)S(1)} %get-tuple-element.48), channel_id=1, source_target_pairs={{0,16},{16,32},{32,48},{48,64},{64,80},{80,96},{96,112},{1,17},{17... | collective-permute-start | bytes 55304 | tf_op jit(solution)/shard_map/ppermute | solution.py:387
  34.0 1.3 broadcast_in_dim.8
  35.3 12.4 %all-to-all-start.1 = ((f32[128,1,128]{2,1,0:T(1,128)}), f32[128,1,128]{2,1,0:T(1,128)S(1)}, u32[]{:S(2)}, u32[]{:S(2)}) async-start(f32[128,1,128]{2,1,0:T(1,128)} %broadcast_in_dim.8), calls=%async_computation.1 | async-start | bytes 131072 | tf_op jit(solution)/shard_map/all_to_all | solution.py:413
  47.9 1.3 collective-permute-start.3
  49.2 4.5 %collective-permute-start.2 = (f32[72,128]{1,0:T(8,128)S(1)}, f32[72,128]{1,0:T(8,128)S(1)}, u32[]{:S(2)}, u32[]{:S(2)}) collective-permute-start(f32[72,128]{1,0:T(8,128)S(1)} %shard_map.148), channel_id=1, source_target_pairs={{0,1},{1,2},{2,3},{3,4},{4,5},{5,6},{6,7},{7,8},{8,9},{9,10},{10,1... | collective-permute-start | bytes 110600 | tf_op jit(solution)/shard_map/ppermute | solution.py:387
  54.0 1.3 collective-permute-start.7
  55.3 4.5 %collective-permute-start.6 = (f32[72,128]{1,0:T(8,128)S(1)}, f32[72,128]{1,0:T(8,128)S(1)}, u32[]{:S(2)}, u32[]{:S(2)}) collective-permute-start(f32[72,128]{1,0:T(8,128)S(1)} %shard_map.150), channel_id=1, source_target_pairs={{0,1},{1,2},{2,3},{3,4},{4,5},{5,6},{6,7},{7,8},{8,9},{9,10},{10,1... | collective-permute-start | bytes 110600 | tf_op jit(solution)/shard_map/ppermute | solution.py:387
  61.4 3.1 %shard_map.151 = (f32[6,64,128]{2,1,0:T(8,128)S(1)}, f32[128,128]{1,0:T(8,128)}) custom-call(s32[4]{0:T(128)S(1)} %pad_add_fusion.place_ref, f32[1]{0:T(128)S(6)} %copy.20.load_ref, f32[9,64,128]{2,1,0:T(8,128)S(1)} %get-tuple-element.43.field_ref, f32[36,128]{1,0:T(8,128)S(1)} %collective-permute-done.below_ref.f_below_ref, ...), custom_call_target="tpu_custom_call" | custom-call | flops 200000000 | bytes 2000000 | tf_op jit(solution)/shard_map/pallas_call | solution.py:456
  64.6 14.6 %all-to-all-start = ((f32[128,1,128]{2,1,0:T(1,128)}), f32[128,1,128]{2,1,0:T(1,128)S(1)}, u32[]{:S(2)}, u32[]{:S(2)}) async-start(f32[128,1,128]{2,1,0:T(1,128)} %bitcast.5), calls=%async_computation | async-start | bytes 131072 | tf_op jit(solution)/shard_map/all_to_all | solution.py:468
  79.2 4.8 %shard_map.153 = (f32[128,8,384]{2,1,0:T(8,128)}, s32[8,128]{1,0:T(8,128)S(1)}) custom-call(s32[1]{0:T(128)} %bitcast.7.here_ref, s32[160]{0:T(256)S(1)} %copy-done.8, f32[128,128]{1,0:T(8,128)S(1)} %bitcast.10, f32[160,1536]{1,0:T(8,128)S(1)} %copy-done.1), custom_call_target="tpu_custom_call" | custom-call | tf_op jit(solution)/shard_map/pallas_call | solution.py:424
  84.1 4.6 %all-to-all-done = f32[128,1,128]{2,1,0:T(1,128)S(1)} async-done(((f32[128,1,128]{2,1,0:T(1,128)}), f32[128,1,128]{2,1,0:T(1,128)S(1)}, u32[]{:S(2)}, u32[]{:S(2)}) %all-to-all-start) | async-done | bytes 65568 | tf_op jit(solution)/shard_map/all_to_all | solution.py:468
  88.6 6.9 %all-to-all-start.3 = ((f32[128,8,384]{2,1,0:T(8,128)}), f32[128,8,384]{2,1,0:T(8,128)S(1)}, u32[]{:S(2)}, u32[]{:S(2)}) async-start(f32[128,8,384]{2,1,0:T(8,128)} %get-tuple-element.55), calls=%async_computation.3 | async-start | bytes 3145728 | tf_op jit(solution)/shard_map/all_to_all | solution.py:431
  95.5 4.7 %shard_map.154.data_ref = f32[128,8,384]{2,1,0:T(8,128)} custom-call(s32[8,128]{1,0:T(8,128)S(1)} %get-tuple-element.53.plan_ref, s32[160]{0:T(256)S(1)} %copy-done.8, f32[160,1536]{1,0:T(8,128)S(1)} %get-tuple-element.54.state_ref), custom_call_target="tpu_custom_call" | custom-call | tf_op jit(solution)/shard_map/pallas_call | solution.py:451
  100.2 19.8 %all-to-all-done.3.history_ref = f32[128,8,384]{2,1,0:T(8,128)S(1)} async-done(((f32[128,8,384]{2,1,0:T(8,128)}), f32[128,8,384]{2,1,0:T(8,128)S(1)}, u32[]{:S(2)}, u32[]{:S(2)}) %all-to-all-start.3) | async-done | bytes 1572896 | tf_op jit(solution)/shard_map/all_to_all | solution.py:431
  120.0 4.6 %all-to-all-start.2 = ((f32[128,8,384]{2,1,0:T(8,128)}), f32[128,8,384]{2,1,0:T(8,128)S(1)}, u32[]{:S(2)}, u32[]{:S(2)}) async-start(f32[128,8,384]{2,1,0:T(8,128)} %shard_map.155), calls=%async_computation.2 | async-start | bytes 3145728 | tf_op jit(solution)/shard_map/all_to_all | solution.py:455
  126.1 23.0 %all-to-all-done.2.state_ref = f32[128,8,384]{2,1,0:T(8,128)S(1)} async-done(((f32[128,8,384]{2,1,0:T(8,128)}), f32[128,8,384]{2,1,0:T(8,128)S(1)}, u32[]{:S(2)}, u32[]{:S(2)}) %all-to-all-start.2) | async-done | bytes 1572896 | tf_op jit(solution)/shard_map/all_to_all | solution.py:455
  149.1 3.2 %shard_map.156 = (f32[80,1536]{1,0:T(8,128)}, f32[80,1536]{1,0:T(8,128)}) custom-call(s32[8,128]{1,0:T(8,128)S(1)} %get-tuple-element.53.plan_ref, f32[128,8,384]{2,1,0:T(8,128)S(1)} %all-to-all-done.2.state_ref, f32[128,8,384]{2,1,0:T(8,128)S(1)} %all-to-all-done.3.history_ref), custom_call_target="tpu_custom_call" | custom-call | tf_op jit(solution)/shard_map/pallas_call | solution.py:469
  (39 shorter events, 9.4 us)
Async XLA Ops:
  2.1 0.9 copy-start.2
  3.0 0.9 copy-start.5
  3.9 0.8 copy-start.6
  4.7 0.8 copy-start.7
  5.7 42.0 %collective-permute-start = (f32[36,128]{1,0:T(8,128)S(1)}, f32[36,128]{1,0:T(8,128)S(1)}, u32[]{:S(2)}, u32[]{:S(2)}) collective-permute-start(f32[36,128]{1,0:T(8,128)S(1)} %get-tuple-element.44), channel_id=1, source_target_pairs={{16,0},{32,16},{48,32},{64,48},{80,64},{96,80},{112,96},{17,1},{33... | collective-permute-start | bytes 55304 | tf_op jit(solution)/shard_map/ppermute | solution.py:388
  6.9 40.7 %collective-permute-start.1 = (f32[36,128]{1,0:T(8,128)S(1)}, f32[36,128]{1,0:T(8,128)S(1)}, u32[]{:S(2)}, u32[]{:S(2)}) collective-permute-start(f32[36,128]{1,0:T(8,128)S(1)} %get-tuple-element.45), channel_id=1, source_target_pairs={{0,16},{16,32},{32,48},{48,64},{64,80},{80,96},{96,112},{1,17},{17... | collective-permute-start | bytes 55304 | tf_op jit(solution)/shard_map/ppermute | solution.py:387
  10.0 1.2 copy-start
  11.2 0.9 copy-start.3
  12.1 2.3 %copy-start.9 = (bf16[1536,1536]{1,0:T(8,128)(2,1)S(1)}, bf16[1536,1536]{1,0:T(8,128)(2,1)}, u32[]{:S(2)}) copy-start(bf16[1536,1536]{1,0:T(8,128)(2,1)} %stiffness_ref.1) | copy-start | bytes 14155780
  14.4 1.2 copy-start.10
  15.6 0.7 copy-start.11
  16.4 17.0 %copy-start.8 = (s32[160]{0:T(256)S(1)}, s32[160]{0:T(256)}, u32[]{:S(2)}) copy-start(s32[160]{0:T(256)} %steps_ref.3) | copy-start | bytes 1924
  28.1 51.1 %copy-start.1 = (f32[160,1536]{1,0:T(8,128)S(1)}, f32[160,1536]{1,0:T(8,128)}, u32[]{:S(2)}) copy-start(f32[160,1536]{1,0:T(8,128)} %history_ref.3) | copy-start | bytes 2949124
  28.1 25.6 %collective-permute-start.4 = (f32[36,128]{1,0:T(8,128)S(1)}, f32[36,128]{1,0:T(8,128)S(1)}, u32[]{:S(2)}, u32[]{:S(2)}) collective-permute-start(f32[36,128]{1,0:T(8,128)S(1)} %get-tuple-element.47), channel_id=1, source_target_pairs={{16,0},{32,16},{48,32},{64,48},{80,64},{96,80},{112,96},{17,1},{33... | collective-permute-start | bytes 55304 | tf_op jit(solution)/shard_map/ppermute | solution.py:388
  29.6 24.2 %collective-permute-start.5 = (f32[36,128]{1,0:T(8,128)S(1)}, f32[36,128]{1,0:T(8,128)S(1)}, u32[]{:S(2)}, u32[]{:S(2)}) collective-permute-start(f32[36,128]{1,0:T(8,128)S(1)} %get-tuple-element.48), channel_id=1, source_target_pairs={{0,16},{16,32},{32,48},{48,64},{64,80},{80,96},{96,112},{1,17},{17... | collective-permute-start | bytes 55304 | tf_op jit(solution)/shard_map/ppermute | solution.py:387
  35.3 29.3 %all-to-all-start.1 = ((f32[128,1,128]{2,1,0:T(1,128)}), f32[128,1,128]{2,1,0:T(1,128)S(1)}, u32[]{:S(2)}, u32[]{:S(2)}) async-start(f32[128,1,128]{2,1,0:T(1,128)} %broadcast_in_dim.8), calls=%async_computation.1 | async-start | bytes 131072 | tf_op jit(solution)/shard_map/all_to_all | solution.py:413
  47.9 12.7 %collective-permute-start.3 = (f32[72,128]{1,0:T(8,128)S(1)}, f32[72,128]{1,0:T(8,128)S(1)}, u32[]{:S(2)}, u32[]{:S(2)}) collective-permute-start(f32[72,128]{1,0:T(8,128)S(1)} %shard_map.148), channel_id=1, source_target_pairs={{1,0},{2,1},{3,2},{4,3},{5,4},{6,5},{7,6},{8,7},{9,8},{10,9},{11,1... | collective-permute-start | bytes 110600 | tf_op jit(solution)/shard_map/ppermute | solution.py:388
  49.2 11.4 %collective-permute-start.2 = (f32[72,128]{1,0:T(8,128)S(1)}, f32[72,128]{1,0:T(8,128)S(1)}, u32[]{:S(2)}, u32[]{:S(2)}) collective-permute-start(f32[72,128]{1,0:T(8,128)S(1)} %shard_map.148), channel_id=1, source_target_pairs={{0,1},{1,2},{2,3},{3,4},{4,5},{5,6},{6,7},{7,8},{8,9},{9,10},{10,1... | collective-permute-start | bytes 110600 | tf_op jit(solution)/shard_map/ppermute | solution.py:387
  54.0 6.6 %collective-permute-start.7 = (f32[72,128]{1,0:T(8,128)S(1)}, f32[72,128]{1,0:T(8,128)S(1)}, u32[]{:S(2)}, u32[]{:S(2)}) collective-permute-start(f32[72,128]{1,0:T(8,128)S(1)} %shard_map.150), channel_id=1, source_target_pairs={{1,0},{2,1},{3,2},{4,3},{5,4},{6,5},{7,6},{8,7},{9,8},{10,9},{11,1... | collective-permute-start | bytes 110600 | tf_op jit(solution)/shard_map/ppermute | solution.py:388
  55.3 6.2 %collective-permute-start.6 = (f32[72,128]{1,0:T(8,128)S(1)}, f32[72,128]{1,0:T(8,128)S(1)}, u32[]{:S(2)}, u32[]{:S(2)}) collective-permute-start(f32[72,128]{1,0:T(8,128)S(1)} %shard_map.150), channel_id=1, source_target_pairs={{0,1},{1,2},{2,3},{3,4},{4,5},{5,6},{6,7},{7,8},{8,9},{9,10},{10,1... | collective-permute-start | bytes 110600 | tf_op jit(solution)/shard_map/ppermute | solution.py:387
  64.6 24.1 %all-to-all-start = ((f32[128,1,128]{2,1,0:T(1,128)}), f32[128,1,128]{2,1,0:T(1,128)S(1)}, u32[]{:S(2)}, u32[]{:S(2)}) async-start(f32[128,1,128]{2,1,0:T(1,128)} %bitcast.5), calls=%async_computation | async-start | bytes 131072 | tf_op jit(solution)/shard_map/all_to_all | solution.py:468
  88.6 31.3 %all-to-all-start.3 = ((f32[128,8,384]{2,1,0:T(8,128)}), f32[128,8,384]{2,1,0:T(8,128)S(1)}, u32[]{:S(2)}, u32[]{:S(2)}) async-start(f32[128,8,384]{2,1,0:T(8,128)} %get-tuple-element.55), calls=%async_computation.3 | async-start | bytes 3145728 | tf_op jit(solution)/shard_map/all_to_all | solution.py:431
  100.2 25.1 %copy-start.4 = (f32[3,64,128]{2,1,0:T(8,128)S(1)}, f32[3,64,128]{2,1,0:T(8,128)}, u32[]{:S(2)}) copy-start(f32[3,64,128]{2,1,0:T(8,128)} %jump_ref.5) | copy-start | bytes 294916
  120.0 29.1 %all-to-all-start.2 = ((f32[128,8,384]{2,1,0:T(8,128)}), f32[128,8,384]{2,1,0:T(8,128)S(1)}, u32[]{:S(2)}, u32[]{:S(2)}) async-start(f32[128,8,384]{2,1,0:T(8,128)} %shard_map.155), calls=%async_computation.2 | async-start | bytes 3145728 | tf_op jit(solution)/shard_map/all_to_all | solution.py:455

commit v2 on v1

v2 whole, which is shorter than its diff:
```python
import functools

import jax
import jax.numpy as jnp
from jax import lax
from jax.experimental import pallas as pl
from jax.experimental.pallas import tpu as pltpu
from jax.sharding import PartitionSpec as P


MAX_STEPS = 9
SWEEPS = 3
HALO = 4
INPUT_FIELDS = 9
FIELDS = 18
LANES = 128
ROWS_COLS = ("row", "col")
VMEM = pl.BlockSpec(memory_space=pltpu.VMEM)
SMEM = pl.BlockSpec(memory_space=pltpu.SMEM)
HBM = pl.BlockSpec(memory_space=pltpu.HBM)
F32 = jnp.float32
BF16 = jnp.bfloat16


def iota(shape, dim):
    return lax.broadcasted_iota(jnp.int32, shape, dim)


def three_parts(x):
    high = x.astype(BF16)
    rest = x - high.astype(F32)
    middle = rest.astype(BF16)
    low = (rest - middle.astype(F32)).astype(BF16)
    return high, middle, low


def times_transposed(a, b):
    return lax.dot_general(a, b, (((1,), (1,)), ((), ())), preferred_element_type=F32)


def put_row_edges(field_ref, first_ref, last_ref):
    fields, rows, _ = field_ref.shape
    for c in range(fields):
        first_ref[HALO * c : HALO * (c + 1), :] = field_ref[c, :HALO, :]
        last_ref[HALO * c : HALO * (c + 1), :] = field_ref[c, rows - HALO :, :]


def with_row_halo(field, below, above, c):
    part = slice(HALO * c, HALO * (c + 1))
    return jnp.concatenate([field, below[part], above[part]], axis=0)


def count_kernel(steps_ref, out_ref):
    live = jnp.sum((steps_ref[...] > 0).astype(F32), axis=1, keepdims=True)
    out_ref[...] = jnp.broadcast_to(live[None], out_ref.shape)


def lane_edges_kernel(field_ref, below_ref, above_ref, to_left_ref, to_right_ref):
    below, above = below_ref[...], above_ref[...]
    fields, rows, lanes = field_ref.shape
    tall = rows + 2 * HALO
    group = iota((tall, lanes), 1) // HALO
    heads = tails = jnp.zeros((tall, lanes), F32)
    for c in range(fields):
        whole = with_row_halo(field_ref[c], below, above, c)
        heads = jnp.where(group == c, pltpu.roll(whole, HALO * c, 1) if c else whole, heads)
        tails = jnp.where(group == c, pltpu.roll(whole, HALO * (c + 1), 1), tails)
    fill = jnp.zeros((lanes - tall, lanes), F32)
    to_left_ref[...] = jnp.concatenate([heads, fill], axis=0).T[: HALO * fields]
    to_right_ref[...] = jnp.concatenate([tails, fill], axis=0).T[: HALO * fields]


def newton_kernel(
    ids_ref, steps_ref, jump_ref, stiffness_ref, coupling_ref, old_state_ref, history_ref,
    state_ref, grid_ref,
    damage_ref, load_ref, diagonal_ref, rounded_ref,
):
    slots, cells = state_ref.shape
    _, rows, lanes = jump_ref.shape
    wide = 2 * lanes
    fill = jnp.zeros((1, wide - slots), jnp.int32)
    ids_row = jnp.concatenate([ids_ref[...], fill], axis=1)
    steps_row = jnp.concatenate([steps_ref[...], fill], axis=1)
    own = iota((slots, wide), 0) == iota((slots, wide), 1)

    def column(values):
        return jnp.sum(jnp.where(own, values, 0.0), axis=1, keepdims=True)

    steps = column(steps_row.astype(F32))
    at_x = column((ids_row // lanes).astype(F32))
    at_y = column((ids_row % lanes).astype(F32))
    pick_x = (iota((slots, rows), 1).astype(F32) == at_x).astype(F32).astype(BF16)
    pick_y = iota((slots, lanes), 1).astype(F32) == at_y
    at_row = iota((rows, wide), 0) == ids_row // lanes
    at_lane = (iota((lanes, wide), 0) == ids_row % lanes).astype(F32).astype(BF16)
    drive = []
    for c in range(3):
        parts = three_parts(jump_ref[c])
        picked = [jnp.dot(pick_x, part, preferred_element_type=F32) for part in parts]
        whole = (picked[0] + picked[1]) + picked[2]
        drive.append(jnp.sum(jnp.where(pick_y, whole, 0.0), axis=1, keepdims=True))
    load_ref[...] = (
        drive[0] * coupling_ref[0:1, :] + drive[1] * coupling_ref[1:2, :] + drive[2] * coupling_ref[2:3, :]
    )
    damage_ref[...] = jnp.exp(-history_ref[...])
    first_state = old_state_ref[...]
    state_ref[...] = first_state
    rounded_ref[0] = first_state.astype(BF16)
    eye = iota((LANES, LANES), 0) == iota((LANES, LANES), 1)
    for t in range(cells // LANES):
        part = slice(t * LANES, (t + 1) * LANES)
        block = stiffness_ref[part, part].astype(F32)
        diagonal_ref[:, part] = jnp.sum(jnp.where(eye, block, 0.0), axis=0, keepdims=True)
    width = 256

    def advance(count, carry):
        now = lax.rem(count, 2)
        rounded = rounded_ref[now]
        moving = count.astype(F32) < steps
        for t in range(cells // width):
            part = slice(t * width, (t + 1) * width)
            force = jnp.dot(rounded, stiffness_ref[:, part], preferred_element_type=F32)
            current = state_ref[:, part]
            bent = jnp.tanh(current)
            damage = damage_ref[:, part]
            misfit = force + damage * bent - load_ref[:, part]
            slope = diagonal_ref[:, part] + damage * (1.0 - bent * bent)
            current = jnp.where(moving, current - misfit / slope, current)
            state_ref[:, part] = current
            rounded_ref[1 - now, :, part] = current.astype(BF16)
        return carry

    lax.fori_loop(0, MAX_STEPS, advance, 0)
    bent = jnp.tanh(state_ref[...])
    damage = damage_ref[...]
    pull = damage * bent
    weight = damage * (1.0 - bent * bent)
    c0, c1, c2 = (coupling_ref[k : k + 1, :] for k in range(3))
    sums = [jnp.sum(pull * c, axis=1, keepdims=True) for c in (c0, c1, c2)]
    sums += [
        jnp.sum(weight * c, axis=1, keepdims=True)
        for c in (c0 * c0, c1 * c1, c2 * c2, c0 * c1, c0 * c2, c1 * c2)
    ]
    lane = iota((slots, LANES), 1)
    table = jnp.zeros((slots, LANES), F32)
    for k, value in enumerate(sums):
        table = jnp.where(lane == k, value * (1.0 / cells), table)
    table = jnp.where(steps > 0.0, table, 0.0)
    table = jnp.concatenate([table, jnp.zeros((wide - slots, LANES), F32)], axis=0).T
    pieces = []
    for c in range(len(sums)):
        placed = jnp.where(at_row, table[c : c + 1, :], 0.0)
        pieces.extend(three_parts(placed))
    spread = times_transposed(jnp.concatenate(pieces, axis=0), at_lane)
    for c in range(len(sums)):
        at = 3 * c * rows
        grid_ref[c] = spread[at : at + rows] + spread[at + rows : at + 2 * rows] + spread[at + 2 * rows : at + 3 * rows]


def fields_kernel(
    ids_ref, steps_ref, jump_ref, external_ref, cohesive_ref, mask_ref, grid_ref, field_ref, first_ref, last_ref
):
    rows, lanes = cohesive_ref.shape
    slots = ids_ref.shape[1]
    ids = ids_ref[...]
    at_row = ((iota((rows, slots), 0) == ids // lanes) & (steps_ref[...] > 0)).astype(F32).astype(BF16)
    at_lane = (iota((lanes, slots), 0) == ids % lanes).astype(F32).astype(BF16)
    soft = times_transposed(at_row, at_lane)
    for c in range(3):
        field_ref[c] = jump_ref[c]
        field_ref[3 + c] = external_ref[c]
    field_ref[6] = (1.0 - soft) * cohesive_ref[...]
    field_ref[7] = 0.25 + 0.75 * mask_ref[0].astype(F32)
    field_ref[8] = 0.25 + 0.75 * mask_ref[1].astype(F32)
    for c in range(FIELDS - INPUT_FIELDS):
        field_ref[INPUT_FIELDS + c] = grid_ref[c]
    put_row_edges(field_ref, first_ref, last_ref)


def pack_kernel(here_ref, steps_ref, counts_ref, state_ref, history_ref, out_ref, plan_ref):
    slots, cells = state_ref.shape
    devices = counts_ref.shape[0]
    here = here_ref[0]
    counts = counts_ref[...]
    before = (iota((devices, devices), 1) < iota((devices, devices), 0)).astype(F32).astype(BF16)
    starts = jnp.dot(before, counts.astype(BF16), preferred_element_type=F32)
    row = iota((devices, LANES), 0)
    start = jnp.sum(jnp.where(row < here, counts, 0.0)[:, 0:1]).astype(jnp.int32)
    total = jnp.sum(counts, axis=0, keepdims=True)
    slot = iota((1, LANES), 1)
    wanted = (2 * (here + devices * (slot // 2)) + slot % 2).astype(F32)
    source = jnp.sum(jnp.where(starts <= wanted, 1.0, 0.0), axis=0, keepdims=True) - 1.0
    index = jnp.where(wanted < total, 2.0 * source + (slot % 2).astype(F32), -1.0).astype(jnp.int32)
    plan_ref[...] = jnp.broadcast_to(index, plan_ref.shape)
    places = out_ref.shape[0]
    unused = lax.rem(2 * (start // 2) + places - 2, places)
    group = 8

    def one(block, rank):
        at = pl.multiple_of(block * group, group)
        state = state_ref[pl.ds(at, group), :]
        history = history_ref[pl.ds(at, group), :]
        for k in range(group):
            alive = steps_ref[at + k] > 0
            to = jnp.where(alive, lax.rem(rank, places), unused)
            out_ref[pl.ds(to, 1), 0, :cells] = state[k : k + 1]
            out_ref[pl.ds(to, 1), 0, cells : 2 * cells] = history[k : k + 1]
            rank = rank + alive.astype(jnp.int32)
        return rank

    lax.fori_loop(0, slots // group, one, start)


def macro_kernel(
    place_ref, load_ref, field_ref, below_ref, above_ref, left_ref, right_ref, packed_hbm,
    moved_ref, packed_out, sums_ref, sem,
):
    del packed_hbm
    rows = field_ref.shape[1]
    tall = rows + 2 * HALO
    lane = iota((tall, LANES), 1)
    line = iota((tall, LANES), 0)
    row_at, col_at = place_ref[0], place_ref[1]
    has_above = (row_at > 0).astype(jnp.int32)
    has_below = (row_at < place_ref[2] - 1).astype(jnp.int32)
    has_left = (col_at > 0).astype(jnp.int32)
    has_right = (col_at < place_ref[3] - 1).astype(jnp.int32)
    row_ok = jnp.where(line < rows, 1, jnp.where(line < rows + HALO, has_below, has_above)) > 0
    side_ok = jnp.where(lane < HALO, has_right, jnp.where(lane >= LANES - HALO, has_left, 0)) > 0
    valid = (row_ok, row_ok & side_ok)
    below, above = below_ref[...], above_ref[...]
    fill = jnp.zeros((LANES - left_ref.shape[0], LANES), F32)
    left = jnp.concatenate([left_ref[...], fill], axis=0).T[:tall]
    right = jnp.concatenate([right_ref[...], fill], axis=0).T[:tall]

    def field(c):
        middle = with_row_halo(field_ref[c], below, above, c)
        from_left = pltpu.roll(left, (LANES - HALO - HALO * c) % LANES, 1)
        from_right = pltpu.roll(right, (LANES - HALO * c) % LANES, 1) if c else right
        side = jnp.where(lane >= LANES - HALO, from_left, jnp.where(lane < HALO, from_right, 0.0))
        return (middle, side)

    def grid(c):
        return field(INPUT_FIELDS + c)

    def pairs(f, *operands):
        return tuple(f(*parts) for parts in zip(*operands))

    def below_of(v):
        return pairs(lambda x: pltpu.roll(x, tall - 1, 0), v)

    def above_of(v):
        return pairs(lambda x: pltpu.roll(x, 1, 0), v)

    def right_of(v):
        a, b = (pltpu.roll(x, LANES - 1, 1) for x in v)
        end = lane == LANES - 1
        return (jnp.where(end, b, a), jnp.where(end, a, b))

    def left_of(v):
        a, b = (pltpu.roll(x, 1, 1) for x in v)
        end = lane == 0
        return (jnp.where(end, b, a), jnp.where(end, a, b))

    bond_x, bond_y = field(7), field(8)
    low_x, low_y = above_of(bond_x), left_of(bond_y)
    scale = pairs(lambda a, b, c, d, e: a + b + c + d + e, bond_x, low_x, bond_y, low_y, field(6))

    def neighbours(v):
        return pairs(
            lambda bx, vb, lx, va, by, vr, ly, vl: bx * vb + lx * va + by * vr + ly * vl,
            bond_x, below_of(v), low_x, above_of(v), bond_y, right_of(v), low_y, left_of(v),
        )

    load = load_ref[0]
    sources = []
    for c in range(3):
        jump = field(c)
        external = field(3 + c)
        residual = pairs(
            lambda s, j, n, t, e: s * j - n + t - load * e, scale, jump, neighbours(jump), grid(c), external
        )
        sources.append((pairs(lambda r: -r, residual), external))

    def inverse_of(s, t00, t11, t22, t01, t02, t12, ok):
        d00, d11, d22 = s + t00, s + t11, s + t22
        c00 = d11 * d22 - t12 * t12
        c11 = d00 * d22 - t02 * t02
        c22 = d00 * d11 - t01 * t01
        c01 = t02 * t12 - t01 * d22
        c02 = t01 * t12 - t02 * d11
        c12 = t01 * t02 - d00 * t12
        determinant = d00 * c00 + t01 * c01 + t02 * c02
        over = jnp.where(ok, 1.0 / jnp.where(ok, determinant, 1.0), 0.0)
        return tuple(c * over for c in (c00, c11, c22, c01, c02, c12))

    both = pairs(inverse_of, scale, *(grid(3 + k) for k in range(6)), valid)
    i00, i11, i22, i01, i02, i12 = (tuple(both[t][k] for t in range(2)) for k in range(6))

    def dot3(a, x, b, y, c, z):
        return pairs(lambda a, x, b, y, c, z: a * x + b * y + c * z, a, x, b, y, c, z)

    def solve(w):
        return [
            dot3(i00, w[0], i01, w[1], i02, w[2]),
            dot3(i01, w[0], i11, w[1], i12, w[2]),
            dot3(i02, w[0], i12, w[1], i22, w[2]),
        ]

    done = []
    for half in range(2):
        source = [sources[c][half] for c in range(3)]
        iterate = solve(source)
        for _ in range(SWEEPS):
            iterate = solve([pairs(jnp.add, source[c], neighbours(iterate[c])) for c in range(3)])
        done.append([iterate[c][0][:rows] for c in range(3)])
    cross = square = 0.0
    for c in range(3):
        moved_ref[c] = field_ref[c] + done[0][c]
        moved_ref[3 + c] = done[1][c]
        cross = cross + done[0][c] * done[1][c]
        square = square + done[1][c] * done[1][c]
    half = iota((1, 1, LANES), 2) < LANES // 2
    sums_ref[...] = jnp.broadcast_to(jnp.where(half, jnp.sum(cross), jnp.sum(square)), sums_ref.shape)
    copy = pltpu.make_async_copy(sums_ref, packed_out.at[:, :, packed_out.shape[2] - LANES :], sem)
    copy.start()
    copy.wait()


def last_kernel(
    entries, plan_ref, load_ref, radius_ref, arrived_ref, moved_ref,
    new_jump_ref, new_load_ref, new_state_ref, new_history_ref,
):
    new_cap, cells = new_state_ref.shape
    whole = 0.5 * jnp.sum(arrived_ref[:, 0, 2 * cells :], axis=0, keepdims=True)
    half = iota(whole.shape, 1) < LANES // 2
    other = pltpu.roll(whole, LANES // 2, 1)
    cross, square = jnp.where(half, whole, other), jnp.where(half, other, whole)
    shifted = square + 0.25 * entries
    increment = (radius_ref[0] * (entries**0.5) * jnp.sqrt(shifted) - cross) / shifted
    for c in range(3):
        new_jump_ref[c] = moved_ref[c] + increment * moved_ref[3 + c]
    new_load_ref[0] = load_ref[0] + jnp.max(increment)
    group = 8

    def one(block, carry):
        at = pl.multiple_of(block * group, group)
        for k in range(group):
            index = plan_ref[0, at + k]
            valid = index >= 0
            source = jnp.maximum(index, 0)
            state = arrived_ref[pl.ds(source, 1), 0, :cells]
            history = arrived_ref[pl.ds(source, 1), 0, cells : 2 * cells]
            new_state_ref[pl.ds(at + k, 1), :] = jnp.where(valid, state, 0.0)
            new_history_ref[pl.ds(at + k, 1), :] = jnp.where(valid, jnp.maximum(history, jnp.abs(state)), 0.0)
        return carry

    lax.fori_loop(0, new_cap // group, one, 0)


LONG = pl.CostEstimate(flops=10_000_000_000, transcendentals=0, bytes_accessed=60_000_000)


def shape(*dims, dtype=F32):
    return jax.ShapeDtypeStruct(dims, dtype)


def call(kernel, outs, ins, out_specs, mib, scratch=(), cost=None, aliases=None):
    return pl.pallas_call(
        kernel,
        out_shape=outs,
        in_specs=ins,
        out_specs=out_specs,
        scratch_shapes=scratch,
        cost_estimate=cost,
        input_output_aliases=aliases or {},
        compiler_params=pltpu.CompilerParams(vmem_limit_bytes=mib * 1024 * 1024),
    )


def swap(first, last, axis):
    size = lax.axis_size(axis)
    up = [(i, i + 1) for i in range(size - 1)]
    down = [(i + 1, i) for i in range(size - 1)]
    above = lax.ppermute(last, axis, up)
    below = lax.ppermute(first, axis, down)
    return below, above


def on_device(
    jump, external, cohesive, bond_mask, load_factor, arc_radius, stiffness, coupling,
    old_state, old_history, newton_steps, point_ids,
):
    n_row, n_col = lax.axis_size("row"), lax.axis_size("col")
    devices = n_row * n_col
    row_at, col_at = lax.axis_index("row"), lax.axis_index("col")
    here = (row_at * n_col + col_at).astype(jnp.int32)
    slots, cells = old_state.shape
    _, rows, lanes = jump.shape
    edge = HALO * FIELDS
    width = 2 * cells + LANES
    packed_shape = shape(2 * devices, 1, width)
    place = jnp.stack([row_at, col_at, n_row, n_col]).astype(jnp.int32)
    ids_row = point_ids.reshape(1, slots)
    steps_row = newton_steps.reshape(1, slots)

    mine = call(count_kernel, shape(devices, 1, LANES), [VMEM], VMEM, 2, cost=LONG)(steps_row)
    counts = lax.all_to_all(mine, ROWS_COLS, 0, 0, tiled=True).reshape(devices, LANES)
    state, grid = call(
        newton_kernel,
        (shape(slots, cells), shape(FIELDS - INPUT_FIELDS, rows, lanes)),
        [VMEM] * 7,
        (VMEM, VMEM),
        24,
        scratch=(
            pltpu.VMEM((slots, cells), F32),
            pltpu.VMEM((slots, cells), F32),
            pltpu.VMEM((1, cells), F32),
            pltpu.VMEM((2, slots, cells), BF16),
        ),
        cost=pl.CostEstimate(
            flops=2 * MAX_STEPS * slots * cells * cells,
            transcendentals=2 * MAX_STEPS * slots * cells,
            bytes_accessed=2 * cells * cells + 12 * slots * cells,
        ),
    )(ids_row, steps_row, jump, stiffness, coupling, old_state, old_history)
    fields, first, last = call(
        fields_kernel,
        (shape(FIELDS, rows, lanes), shape(edge, lanes), shape(edge, lanes)),
        [VMEM] * 7,
        (VMEM,) * 3,
        4,
    )(ids_row, steps_row, jump, external, cohesive, bond_mask, grid)
    below, above = swap(first, last, "row")
    packed, plan = call(
        pack_kernel,
        (packed_shape, shape(8, LANES, dtype=jnp.int32)),
        [SMEM, SMEM, VMEM, VMEM, VMEM],
        (VMEM, VMEM),
        12,
    )(here[None], newton_steps, counts, state, old_history)
    to_left, to_right = call(
        lane_edges_kernel, (shape(edge, lanes), shape(edge, lanes)), [VMEM] * 3, (VMEM, VMEM), 4
    )(fields, below, above)
    right, left = swap(to_left, to_right, "col")
    moved, packed = call(
        macro_kernel,
        (shape(6, rows, lanes), packed_shape),
        [SMEM, SMEM] + [VMEM] * 5 + [HBM],
        (VMEM, HBM),
        12,
        scratch=(pltpu.VMEM((2 * devices, 1, LANES), F32), pltpu.SemaphoreType.DMA),
        cost=pl.CostEstimate(flops=200_000_000, transcendentals=0, bytes_accessed=2_000_000),
        aliases={7: 1},
    )(place, load_factor, fields, below, above, left, right, packed)
    arrived = lax.all_to_all(packed.reshape(devices, 1, 2 * width), ROWS_COLS, 0, 0, tiled=True)
    arrived = arrived.reshape(2 * devices, 1, width)
    new_jump, new_load, new_state, new_history = call(
        functools.partial(last_kernel, 3.0 * rows * lanes * devices),
        (shape(3, rows, lanes), shape(1), shape(slots // 2, cells), shape(slots // 2, cells)),
        [SMEM, SMEM, SMEM, VMEM, VMEM],
        (VMEM, SMEM, VMEM, VMEM),
        12,
    )(plan, load_factor, arc_radius, arrived, moved)
    return (new_jump, new_load, new_state, new_history)


def solution(mesh):
    whole = P(None, "row", "col")
    slot_rows = P(ROWS_COLS, None)
    return jax.shard_map(
        on_device,
        mesh=mesh,
        in_specs=(
            whole, whole, P("row", "col"), whole, P(), P(), P(), P(),
            slot_rows, slot_rows, P(ROWS_COLS), P(ROWS_COLS),
        ),
        out_specs=(whole, P(), slot_rows, slot_rows),
        check_vma=False,
    )
```

time: 153 us -> 107 us (0.70)
  starting transfers between devices: 59.7 us -> 29 us
  Pallas kernels: 29 us -> 21.9 us
  local copies, waits for them, and re-layouts: 12.5 us -> 7.74 us
  waiting for transfers between devices: 48.3 us -> 45.1 us
    all_to_all x4 -> x2, starting transfers between devices: 38.5 us -> 20.4 us  [the longest x1 11.9 us: on_device(): lax.all_to_all(mine, ROWS_COLS, 0, 0, tiled=True).reshape(devices, LANES)]
    ppermute x4 -> x2, starting transfers between devices: 15.9 us -> 6.03 us  [swap(): above = lax.ppermute(last, axis, up)]
    pallas_call x10 -> x7, Pallas kernels: 29 us -> 21.9 us  [the longest x1 11.9 us: on_device(): call(newton_kernel, (shape(slots, cells), shape(FIELDS - INPUT_FIELDS, ro...]
    ppermute x4 -> x2, starting transfers between devices: 5.29 us -> 2.59 us  [swap(): below = lax.ppermute(first, axis, down)]
    all_to_all x4 -> x2, waiting for transfers between devices: 47.4 us -> 45.1 us  [the longest x1 41.1 us: on_device(): lax.all_to_all(packed.reshape(devices, 1, 2 * width), ROWS_COLS, 0, 0, ti...]
    unnamed x24, local copies, waits for them, and re-layouts: 9.75 us -> 7.74 us
  transfers between devices with their start and end apart: 12 -> 6, of which waited for: 4 -> 2; matrix products, arithmetic and copies ran while one was open for 1% -> 0% of each run, Pallas kernels for 17% -> 4%
where the time goes in v2:
time: 107 us; the launch traced here: 106 us
  waiting for transfers between devices  45.1 us (42%)
  starting transfers between devices  29 us (27%)
  Pallas kernels  21.9 us (20%)
  local copies, waits for them, and re-layouts  7.74 us (7%)
  between operations  2.08 us (2%)
    all_to_all x1, waiting for transfers between devices, on_device(): lax.all_to_all(packed.reshape(devices, 1, 2 * width), ROWS_COLS, 0, 0, ti...  41.1 us
    pallas_call x1, Pallas kernels, on_device(): call(newton_kernel, (shape(slots, cells), shape(FIELDS - INPUT_FIELDS, ro...  11.9 us
    all_to_all x1, starting transfers between devices, on_device(): lax.all_to_all(mine, ROWS_COLS, 0, 0, tiled=True).reshape(devices, LANES)  11.9 us
    all_to_all x1, starting transfers between devices, on_device(): lax.all_to_all(packed.reshape(devices, 1, 2 * width), ROWS_COLS, 0, 0, ti...  8.53 us
    unnamed x24, local copies, waits for them, and re-layouts  7.74 us
    ppermute x2, starting transfers between devices, swap(): above = lax.ppermute(last, axis, up)  6.03 us
    all_to_all x1, waiting for transfers between devices, on_device(): lax.all_to_all(mine, ROWS_COLS, 0, 0, tiled=True).reshape(devices, LANES)  4.03 us
    pallas_call x1, Pallas kernels, on_device(): call(macro_kernel, (shape(6, rows, lanes), packed_shape), [SMEM, SMEM] +...  3.18 us
  transfers between devices with their start and end apart: 6, of which 2 were waited for; matrix products, arithmetic and copies ran while one was open for 0% of the time, Pallas kernels for 4%

profile of v2, /device:TPU:0, one launch (start us, length us, event | category | flops | bytes accessed | tf_op | source)
XLA Modules:
  0.0 105.9 jit_solution(35382558533962468)
XLA Ops:
  0.6 1.2 %copy-done = f32[160,1536]{1,0:T(8,128)S(1)} copy-done((f32[160,1536]{1,0:T(8,128)S(1)}, f32[160,1536]{1,0:T(8,128)}, u32[]{:S(2)}) %copy-start) | copy-done | bytes 983064
  1.8 0.9 copy-done.2
  2.7 0.7 copy-done.6
  3.4 0.7 copy-done.8
  4.1 2.3 %copy-done.9 = bf16[1536,1536]{1,0:T(8,128)(2,1)S(1)} copy-done((bf16[1536,1536]{1,0:T(8,128)(2,1)S(1)}, bf16[1536,1536]{1,0:T(8,128)(2,1)}, u32[]{:S(2)}) %copy-start.9) | copy-done | bytes 4718616
  6.4 1.2 %copy-done.10 = f32[160,1536]{1,0:T(8,128)S(1)} copy-done((f32[160,1536]{1,0:T(8,128)S(1)}, f32[160,1536]{1,0:T(8,128)}, u32[]{:S(2)}) %copy-start.10) | copy-done | bytes 983064
  7.6 0.7 copy-done.11
  8.4 11.9 %shard_map.148 = (f32[160,1536]{1,0:T(8,128)S(1)}, f32[9,64,128]{2,1,0:T(8,128)S(1)}) custom-call(s32[1,160]{1,0:T(1,128)S(1)} %bitcast.13, s32[1,160]{1,0:T(1,128)S(1)} %bitcast.10, f32[3,64,128]{2,1,0:T(8,128)S(1)} %copy-done.2, bf16[1536,1536]{1,0:T(8,128)(2,1)S(1)} %copy-done.9, f32[3,1536]{1,0:T(4,128)S(1)} %copy-done.11, f32[160,1536]{1,0:T(8,128)S(1)} %copy-done.10, ...), custom_call_target="tpu_custom_call" | custom-call | flops 6794772480 | bytes 7667712 | tf_op jit(solution)/shard_map/pallas_call | solution.py:409
  20.3 0.2 shard_map.150
  20.4 1.3 %collective-permute-start = (f32[72,128]{1,0:T(8,128)S(1)}, f32[72,128]{1,0:T(8,128)S(1)}, u32[]{:S(2)}, u32[]{:S(2)}) collective-permute-start(f32[72,128]{1,0:T(8,128)S(1)} %get-tuple-element.19), channel_id=1, source_target_pairs={{16,0},{32,16},{48,32},{64,48},{80,64},{96,80},{112,96},{17,1},{33... | collective-permute-start | bytes 110600 | tf_op jit(solution)/shard_map/ppermute | solution.py:386
  21.8 0.0 copy-start.7
  21.8 3.2 %collective-permute-start.1 = (f32[72,128]{1,0:T(8,128)S(1)}, f32[72,128]{1,0:T(8,128)S(1)}, u32[]{:S(2)}, u32[]{:S(2)}) collective-permute-start(f32[72,128]{1,0:T(8,128)S(1)} %get-tuple-element.20), channel_id=1, source_target_pairs={{0,16},{16,32},{32,48},{48,64},{64,80},{80,96},{96,112},{1,17},{17... | collective-permute-start | bytes 110600 | tf_op jit(solution)/shard_map/ppermute | solution.py:385
  24.9 0.7 shard_map.147
  25.7 11.9 %all-to-all-start = ((f32[128,1,128]{2,1,0:T(1,128)}), f32[128,1,128]{2,1,0:T(1,128)S(1)}, u32[]{:S(2)}, u32[]{:S(2)}) async-start(f32[128,1,128]{2,1,0:T(1,128)} %shard_map.147), calls=%async_computation | async-start | bytes 131072 | tf_op jit(solution)/shard_map/all_to_all | solution.py:408
  37.6 0.5 shard_map.151
  38.0 2.9 %collective-permute-start.2 = (f32[72,128]{1,0:T(8,128)S(1)}, f32[72,128]{1,0:T(8,128)S(1)}, u32[]{:S(2)}, u32[]{:S(2)}) collective-permute-start(f32[72,128]{1,0:T(8,128)S(1)} %get-tuple-element.21), channel_id=1, source_target_pairs={{0,1},{1,2},{2,3},{3,4},{4,5},{5,6},{6,7},{7,8},{8,9},{9,10},{10,1... | collective-permute-start | bytes 110600 | tf_op jit(solution)/shard_map/ppermute | solution.py:385
  40.9 1.3 %collective-permute-start.3 = (f32[72,128]{1,0:T(8,128)S(1)}, f32[72,128]{1,0:T(8,128)S(1)}, u32[]{:S(2)}, u32[]{:S(2)}) collective-permute-start(f32[72,128]{1,0:T(8,128)S(1)} %get-tuple-element.22), channel_id=1, source_target_pairs={{1,0},{2,1},{3,2},{4,3},{5,4},{6,5},{7,6},{8,7},{9,8},{10,9},{11,1... | collective-permute-start | bytes 110600 | tf_op jit(solution)/shard_map/ppermute | solution.py:386
  42.2 0.1 pad_add_fusion.place_ref
  43.0 4.0 %all-to-all-done = f32[128,1,128]{2,1,0:T(1,128)S(1)} async-done(((f32[128,1,128]{2,1,0:T(1,128)}), f32[128,1,128]{2,1,0:T(1,128)S(1)}, u32[]{:S(2)}, u32[]{:S(2)}) %all-to-all-start) | async-done | bytes 65568 | tf_op jit(solution)/shard_map/all_to_all | solution.py:408
  47.0 3.2 %shard_map.149 = (f32[256,1,3200]{2,1,0:T(1,128)}, s32[8,128]{1,0:T(8,128)S(1)}) custom-call(s32[1]{0:T(128)} %bitcast.here_ref, s32[160]{0:T(256)S(1)} %copy-done.7, f32[128,128]{1,0:T(8,128)S(1)} %bitcast.9, f32[160,1536]{1,0:T(8,128)S(1)} %get-tuple-element.15.state_ref, f32[160,1536]{1,0:T(8,128)S(1)} %copy-done.1), custom_call_target="tpu_custom_call" | custom-call | tf_op jit(solution)/shard_map/pallas_call | solution.py:435
  50.2 3.2 %shard_map.152 = (f32[6,64,128]{2,1,0:T(8,128)S(1)}, f32[256,1,3200]{2,1,0:T(1,128)}) custom-call(s32[4]{0:T(128)S(1)} %pad_add_fusion.place_ref, f32[1]{0:T(128)S(6)} %copy.20.load_ref, f32[18,64,128]{2,1,0:T(8,128)S(1)} %get-tuple-element.18.field_ref, f32[72,128]{1,0:T(8,128)S(1)} %collective-permute-done.below_ref, ...), custom_call_target="tpu_custom_call", output_to_operand_aliasing={{1}: (7, {})} | custom-call | flops 200000000 | bytes 2000000 | tf_op jit(solution)/shard_map/pallas_call | solution.py:446
  53.3 8.5 %all-to-all-start.1 = ((f32[128,1,6400]{2,1,0:T(1,128)}), f32[128,1,6400]{2,1,0:T(1,128)S(1)}, u32[]{:S(2)}, u32[]{:S(2)}) async-start(f32[128,1,6400]{2,1,0:T(1,128)} %bitcast.6), calls=%async_computation.1 | async-start | bytes 6553600 | tf_op jit(solution)/shard_map/all_to_all | solution.py:456
  62.5 41.1 %all-to-all-done.1 = f32[128,1,6400]{2,1,0:T(1,128)S(1)} async-done(((f32[128,1,6400]{2,1,0:T(1,128)}), f32[128,1,6400]{2,1,0:T(1,128)S(1)}, u32[]{:S(2)}, u32[]{:S(2)}) %all-to-all-start.1) | async-done | bytes 3276832 | tf_op jit(solution)/shard_map/all_to_all | solution.py:456
  103.6 2.3 %shard_map.153 = (f32[3,64,128]{2,1,0:T(8,128)}, f32[1]{0:T(128)}, f32[80,1536]{1,0:T(8,128)}, f32[80,1536]{1,0:T(8,128)}) custom-call(s32[8,128]{1,0:T(8,128)S(1)} %get-tuple-element.16.plan_ref, f32[1]{0:T(128)S(6)} %copy.20.load_ref, f32[1]{0:T(128)S(6)} %copy.21.radius_ref, f32[256,1,3200]{2,1,0:T(1,128)S(1)} %bitcast.8, ...), custom_call_target="tpu_custom_call" | custom-call | tf_op jit(solution)/shard_map/pallas_call | solution.py:458
  (20 shorter events, 0.0 us)
Async XLA Ops:
  0.6 1.2 %copy-start = (f32[160,1536]{1,0:T(8,128)S(1)}, f32[160,1536]{1,0:T(8,128)}, u32[]{:S(2)}) copy-start(f32[160,1536]{1,0:T(8,128)} %history_ref.3) | copy-start | bytes 2949124
  1.8 0.9 copy-start.2
  2.7 0.7 copy-start.6
  3.4 0.7 copy-start.8
  4.1 2.3 %copy-start.9 = (bf16[1536,1536]{1,0:T(8,128)(2,1)S(1)}, bf16[1536,1536]{1,0:T(8,128)(2,1)}, u32[]{:S(2)}) copy-start(bf16[1536,1536]{1,0:T(8,128)(2,1)} %stiffness_ref.1) | copy-start | bytes 14155780
  6.4 1.2 %copy-start.10 = (f32[160,1536]{1,0:T(8,128)S(1)}, f32[160,1536]{1,0:T(8,128)}, u32[]{:S(2)}) copy-start(f32[160,1536]{1,0:T(8,128)} %old_state_ref.1) | copy-start | bytes 2949124
  7.6 0.7 copy-start.11
  8.4 11.9 %copy-start.3 = (f32[3,64,128]{2,1,0:T(8,128)S(1)}, f32[3,64,128]{2,1,0:T(8,128)}, u32[]{:S(2)}) copy-start(f32[3,64,128]{2,1,0:T(8,128)} %external_ref.1) | copy-start | bytes 294916
  8.4 11.9 %copy-start.4 = (s32[2,64,128]{2,1,0:T(8,128)S(1)}, s32[2,64,128]{2,1,0:T(8,128)}, u32[]{:S(2)}) copy-start(s32[2,64,128]{2,1,0:T(8,128)} %mask_ref.1) | copy-start | bytes 196612
  8.4 11.9 %copy-start.5 = (f32[64,128]{1,0:T(8,128)S(1)}, f32[64,128]{1,0:T(8,128)}, u32[]{:S(2)}) copy-start(f32[64,128]{1,0:T(8,128)} %cohesive_ref.1) | copy-start | bytes 98308
  20.4 17.1 %collective-permute-start = (f32[72,128]{1,0:T(8,128)S(1)}, f32[72,128]{1,0:T(8,128)S(1)}, u32[]{:S(2)}, u32[]{:S(2)}) collective-permute-start(f32[72,128]{1,0:T(8,128)S(1)} %get-tuple-element.19), channel_id=1, source_target_pairs={{16,0},{32,16},{48,32},{64,48},{80,64},{96,80},{112,96},{17,1},{33... | collective-permute-start | bytes 110600 | tf_op jit(solution)/shard_map/ppermute | solution.py:386
  21.7 25.2 %copy-start.1 = (f32[160,1536]{1,0:T(8,128)S(1)}, f32[160,1536]{1,0:T(8,128)}, u32[]{:S(2)}) copy-start(f32[160,1536]{1,0:T(8,128)} %history_ref.3) | copy-start | bytes 2949124
  21.8 25.2 %copy-start.7 = (s32[160]{0:T(256)S(1)}, s32[160]{0:T(256)}, u32[]{:S(2)}) copy-start(s32[160]{0:T(256)} %steps_ref.1) | copy-start | bytes 1924
  21.8 15.8 %collective-permute-start.1 = (f32[72,128]{1,0:T(8,128)S(1)}, f32[72,128]{1,0:T(8,128)S(1)}, u32[]{:S(2)}, u32[]{:S(2)}) collective-permute-start(f32[72,128]{1,0:T(8,128)S(1)} %get-tuple-element.20), channel_id=1, source_target_pairs={{0,16},{16,32},{32,48},{48,64},{64,80},{80,96},{96,112},{1,17},{17... | collective-permute-start | bytes 110600 | tf_op jit(solution)/shard_map/ppermute | solution.py:385
  25.7 21.3 %all-to-all-start = ((f32[128,1,128]{2,1,0:T(1,128)}), f32[128,1,128]{2,1,0:T(1,128)S(1)}, u32[]{:S(2)}, u32[]{:S(2)}) async-start(f32[128,1,128]{2,1,0:T(1,128)} %shard_map.147), calls=%async_computation | async-start | bytes 131072 | tf_op jit(solution)/shard_map/all_to_all | solution.py:408
  38.0 12.1 %collective-permute-start.2 = (f32[72,128]{1,0:T(8,128)S(1)}, f32[72,128]{1,0:T(8,128)S(1)}, u32[]{:S(2)}, u32[]{:S(2)}) collective-permute-start(f32[72,128]{1,0:T(8,128)S(1)} %get-tuple-element.21), channel_id=1, source_target_pairs={{0,1},{1,2},{2,3},{3,4},{4,5},{5,6},{6,7},{7,8},{8,9},{9,10},{10,1... | collective-permute-start | bytes 110600 | tf_op jit(solution)/shard_map/ppermute | solution.py:385
  40.9 9.2 %collective-permute-start.3 = (f32[72,128]{1,0:T(8,128)S(1)}, f32[72,128]{1,0:T(8,128)S(1)}, u32[]{:S(2)}, u32[]{:S(2)}) collective-permute-start(f32[72,128]{1,0:T(8,128)S(1)} %get-tuple-element.22), channel_id=1, source_target_pairs={{1,0},{2,1},{3,2},{4,3},{5,4},{6,5},{7,6},{8,7},{9,8},{10,9},{11,1... | collective-permute-start | bytes 110600 | tf_op jit(solution)/shard_map/ppermute | solution.py:386
  53.3 50.3 %all-to-all-start.1 = ((f32[128,1,6400]{2,1,0:T(1,128)}), f32[128,1,6400]{2,1,0:T(1,128)S(1)}, u32[]{:S(2)}, u32[]{:S(2)}) async-start(f32[128,1,6400]{2,1,0:T(1,128)} %bitcast.6), calls=%async_computation.1 | async-start | bytes 6553600 | tf_op jit(solution)/shard_map/all_to_all | solution.py:456

commit v3 on v2

--- a/solution.py
+++ b/solution.py
@@ -13,6 +13,8 @@
 HALO = 4
 INPUT_FIELDS = 9
 FIELDS = 18
+EARLY = 1152
+NEWTON_MIB = 52
 LANES = 128
 ROWS_COLS = ("row", "col")
 VMEM = pl.BlockSpec(memory_space=pltpu.VMEM)
@@ -71,10 +73,20 @@
 
 
 def newton_kernel(
-    ids_ref, steps_ref, jump_ref, stiffness_ref, coupling_ref, old_state_ref, history_ref,
+    ids_ref, steps_ref, jump_ref, stiffness_hbm, coupling_ref, old_state_hbm, history_hbm,
     state_ref, grid_ref,
-    damage_ref, load_ref, diagonal_ref, rounded_ref,
+    stiffness_ref, damage_ref, load_ref, diagonal_ref, rounded_ref, sems,
 ):
+    width = 256
+    cuts = [slice(t * width, (t + 1) * width) for t in range(stiffness_hbm.shape[1] // width)]
+    copies = [
+        pltpu.make_async_copy(stiffness_hbm.at[:, part], stiffness_ref.at[:, part], sems.at[t])
+        for t, part in enumerate(cuts)
+    ]
+    get_history = pltpu.make_async_copy(history_hbm, damage_ref, sems.at[len(cuts)])
+    get_state = pltpu.make_async_copy(old_state_hbm, state_ref, sems.at[len(cuts) + 1])
+    for copy in (get_history, get_state, *copies):
+        copy.start()
     slots, cells = state_ref.shape
     _, rows, lanes = jump_ref.shape
     wide = 2 * lanes
@@ -102,23 +114,21 @@
     load_ref[...] = (
         drive[0] * coupling_ref[0:1, :] + drive[1] * coupling_ref[1:2, :] + drive[2] * coupling_ref[2:3, :]
     )
-    damage_ref[...] = jnp.exp(-history_ref[...])
-    first_state = old_state_ref[...]
-    state_ref[...] = first_state
-    rounded_ref[0] = first_state.astype(BF16)
-    eye = iota((LANES, LANES), 0) == iota((LANES, LANES), 1)
-    for t in range(cells // LANES):
-        part = slice(t * LANES, (t + 1) * LANES)
-        block = stiffness_ref[part, part].astype(F32)
-        diagonal_ref[:, part] = jnp.sum(jnp.where(eye, block, 0.0), axis=0, keepdims=True)
-    width = 256
-
-    def advance(count, carry):
-        now = lax.rem(count, 2)
+    get_history.wait()
+    damage_ref[...] = jnp.exp(-damage_ref[...])
+    get_state.wait()
+    rounded_ref[0] = state_ref[...].astype(BF16)
+    eye = iota((width, width), 0) == iota((width, width), 1)
+
+    def advance(count, carry, waiting=False):
+        now = count % 2 if waiting else lax.rem(count, 2)
         rounded = rounded_ref[now]
-        moving = count.astype(F32) < steps
-        for t in range(cells // width):
-            part = slice(t * width, (t + 1) * width)
+        moving = steps > jnp.asarray(count, jnp.int32).astype(F32)
+        for t, part in enumerate(cuts):
+            if waiting:
+                copies[t].wait()
+                block = stiffness_ref[part, part].astype(F32)
+                diagonal_ref[:, part] = jnp.sum(jnp.where(eye, block, 0.0), axis=0, keepdims=True)
             force = jnp.dot(rounded, stiffness_ref[:, part], preferred_element_type=F32)
             current = state_ref[:, part]
             bent = jnp.tanh(current)
@@ -130,7 +140,8 @@
             rounded_ref[1 - now, :, part] = current.astype(BF16)
         return carry
 
-    lax.fori_loop(0, MAX_STEPS, advance, 0)
+    advance(0, 0, waiting=True)
+    lax.fori_loop(1, MAX_STEPS, advance, 0)
     bent = jnp.tanh(state_ref[...])
     damage = damage_ref[...]
     pull = damage * bent
@@ -177,8 +188,26 @@
     put_row_edges(field_ref, first_ref, last_ref)
 
 
-def pack_kernel(here_ref, steps_ref, counts_ref, state_ref, history_ref, out_ref, plan_ref):
-    slots, cells = state_ref.shape
+def pack_rows(pieces, out_ref, steps_ref, start):
+    slots, places = pieces[0][0].shape[0], out_ref.shape[0]
+    unused = lax.rem(2 * (start // 2) + places - 2, places)
+    group = 8
+
+    def one(block, rank):
+        at = pl.multiple_of(block * group, group)
+        rows = [(ref[pl.ds(at, group), low:high], to) for ref, low, high, to in pieces]
+        for k in range(group):
+            alive = steps_ref[at + k] > 0
+            place = jnp.where(alive, lax.rem(rank, places), unused)
+            for values, to in rows:
+                out_ref[pl.ds(place, 1), 0, to : to + values.shape[1]] = values[k : k + 1]
+            rank = rank + alive.astype(jnp.int32)
+        return rank
+
+    lax.fori_loop(0, slots // group, one, start)
+
+
+def pack_history_kernel(here_ref, steps_ref, counts_ref, history_ref, out_ref, plan_ref):
     devices = counts_ref.shape[0]
     here = here_ref[0]
     counts = counts_ref[...]
@@ -191,24 +220,17 @@
     wanted = (2 * (here + devices * (slot // 2)) + slot % 2).astype(F32)
     source = jnp.sum(jnp.where(starts <= wanted, 1.0, 0.0), axis=0, keepdims=True) - 1.0
     index = jnp.where(wanted < total, 2.0 * source + (slot % 2).astype(F32), -1.0).astype(jnp.int32)
-    plan_ref[...] = jnp.broadcast_to(index, plan_ref.shape)
-    places = out_ref.shape[0]
-    unused = lax.rem(2 * (start // 2) + places - 2, places)
-    group = 8
-
-    def one(block, rank):
-        at = pl.multiple_of(block * group, group)
-        state = state_ref[pl.ds(at, group), :]
-        history = history_ref[pl.ds(at, group), :]
-        for k in range(group):
-            alive = steps_ref[at + k] > 0
-            to = jnp.where(alive, lax.rem(rank, places), unused)
-            out_ref[pl.ds(to, 1), 0, :cells] = state[k : k + 1]
-            out_ref[pl.ds(to, 1), 0, cells : 2 * cells] = history[k : k + 1]
-            rank = rank + alive.astype(jnp.int32)
-        return rank
-
-    lax.fori_loop(0, slots // group, one, start)
+    line = iota(plan_ref.shape, 0)
+    plan_ref[...] = jnp.where(line == 0, index, start)
+    pack_rows([(history_ref, 0, EARLY, 0)], out_ref, steps_ref, start)
+
+
+def pack_state_kernel(plan_ref, steps_ref, state_ref, history_ref, out_ref):
+    cells = state_ref.shape[1]
+    pieces = [(state_ref, 0, cells, 0)]
+    if EARLY < cells:
+        pieces.append((history_ref, EARLY, cells, cells))
+    pack_rows(pieces, out_ref, steps_ref, plan_ref[1, 0])
 
 
 def macro_kernel(
@@ -328,11 +350,11 @@
 
 
 def last_kernel(
-    entries, plan_ref, load_ref, radius_ref, arrived_ref, moved_ref,
+    entries, plan_ref, load_ref, radius_ref, early_ref, arrived_ref, moved_ref,
     new_jump_ref, new_load_ref, new_state_ref, new_history_ref,
 ):
     new_cap, cells = new_state_ref.shape
-    whole = 0.5 * jnp.sum(arrived_ref[:, 0, 2 * cells :], axis=0, keepdims=True)
+    whole = 0.5 * jnp.sum(arrived_ref[:, 0, arrived_ref.shape[2] - LANES :], axis=0, keepdims=True)
     half = iota(whole.shape, 1) < LANES // 2
     other = pltpu.roll(whole, LANES // 2, 1)
     cross, square = jnp.where(half, whole, other), jnp.where(half, other, whole)
@@ -350,9 +372,13 @@
             valid = index >= 0
             source = jnp.maximum(index, 0)
             state = arrived_ref[pl.ds(source, 1), 0, :cells]
-            history = arrived_ref[pl.ds(source, 1), 0, cells : 2 * cells]
+            early = early_ref[pl.ds(source, 1), 0, :]
             new_state_ref[pl.ds(at + k, 1), :] = jnp.where(valid, state, 0.0)
-            new_history_ref[pl.ds(at + k, 1), :] = jnp.where(valid, jnp.maximum(history, jnp.abs(state)), 0.0)
+            size = jnp.abs(state)
+            new_history_ref[pl.ds(at + k, 1), :EARLY] = jnp.where(valid, jnp.maximum(early, size[:, :EARLY]), 0.0)
+            if EARLY < cells:
+                late = arrived_ref[pl.ds(source, 1), 0, cells : 2 * cells - EARLY]
+                new_history_ref[pl.ds(at + k, 1), EARLY:] = jnp.where(valid, jnp.maximum(late, size[:, EARLY:]), 0.0)
         return carry
 
     lax.fori_loop(0, new_cap // group, one, 0)
@@ -398,7 +424,8 @@
     slots, cells = old_state.shape
     _, rows, lanes = jump.shape
     edge = HALO * FIELDS
-    width = 2 * cells + LANES
+    width = 2 * cells - EARLY + LANES
+    early_shape = shape(2 * devices, 1, EARLY)
     packed_shape = shape(2 * devices, 1, width)
     place = jnp.stack([row_at, col_at, n_row, n_col]).astype(jnp.int32)
     ids_row = point_ids.reshape(1, slots)
@@ -406,17 +433,28 @@
 
     mine = call(count_kernel, shape(devices, 1, LANES), [VMEM], VMEM, 2, cost=LONG)(steps_row)
     counts = lax.all_to_all(mine, ROWS_COLS, 0, 0, tiled=True).reshape(devices, LANES)
+    early, plan = call(
+        pack_history_kernel,
+        (early_shape, shape(8, LANES, dtype=jnp.int32)),
+        [SMEM, SMEM, VMEM, VMEM],
+        (VMEM, VMEM),
+        6,
+    )(here[None], newton_steps, counts, old_history)
+    early = lax.all_to_all(early.reshape(devices, 1, 2 * EARLY), ROWS_COLS, 0, 0, tiled=True)
+    early = early.reshape(early_shape.shape)
     state, grid = call(
         newton_kernel,
         (shape(slots, cells), shape(FIELDS - INPUT_FIELDS, rows, lanes)),
-        [VMEM] * 7,
+        [VMEM] * 3 + [HBM, VMEM, HBM, HBM],
         (VMEM, VMEM),
-        24,
+        NEWTON_MIB,
         scratch=(
+            pltpu.VMEM(stiffness.shape, BF16),
             pltpu.VMEM((slots, cells), F32),
             pltpu.VMEM((slots, cells), F32),
             pltpu.VMEM((1, cells), F32),
             pltpu.VMEM((2, slots, cells), BF16),
+            pltpu.SemaphoreType.DMA((cells // 256 + 2,)),
         ),
         cost=pl.CostEstimate(
             flops=2 * MAX_STEPS * slots * cells * cells,
@@ -432,13 +470,9 @@
         4,
     )(ids_row, steps_row, jump, external, cohesive, bond_mask, grid)
     below, above = swap(first, last, "row")
-    packed, plan = call(
-        pack_kernel,
-        (packed_shape, shape(8, LANES, dtype=jnp.int32)),
-        [SMEM, SMEM, VMEM, VMEM, VMEM],
-        (VMEM, VMEM),
-        12,
-    )(here[None], newton_steps, counts, state, old_history)
+    packed = call(pack_state_kernel, packed_shape, [SMEM, SMEM, VMEM, VMEM], VMEM, 8)(
+        plan, newton_steps, state, old_history
+    )
     to_left, to_right = call(
         lane_edges_kernel, (shape(edge, lanes), shape(edge, lanes)), [VMEM] * 3, (VMEM, VMEM), 4
     )(fields, below, above)
@@ -458,10 +492,10 @@
     new_jump, new_load, new_state, new_history = call(
         functools.partial(last_kernel, 3.0 * rows * lanes * devices),
         (shape(3, rows, lanes), shape(1), shape(slots // 2, cells), shape(slots // 2, cells)),
-        [SMEM, SMEM, SMEM, VMEM, VMEM],
+        [SMEM, SMEM, SMEM, VMEM, VMEM, VMEM],
         (VMEM, SMEM, VMEM, VMEM),
         12,
-    )(plan, load_factor, arc_radius, arrived, moved)
+    )(plan, load_factor, arc_radius, early, arrived, moved)
     return (new_jump, new_load, new_state, new_history)
 
 

time: 107 us -> 109 us (1.019)
  starting transfers between devices: 29 us -> 38.4 us
  local copies, waits for them, and re-layouts: 7.74 us -> 0.72 us
  Pallas kernels: 21.9 us -> 26.5 us
  waiting for transfers between devices: 45.1 us -> 40.5 us
    all_to_all x1, waiting for transfers between devices: 41.1 us -> 29.1 us  [on_device(): lax.all_to_all(packed.reshape(devices, 1, 2 * width), ROWS_COLS, 0, 0, ti...]
    unnamed x24 -> x20, local copies, waits for them, and re-layouts: 7.74 us -> 0.72 us
    all_to_all x1, starting transfers between devices: 8.53 us -> 14.2 us  [on_device(): lax.all_to_all(packed.reshape(devices, 1, 2 * width), ROWS_COLS, 0, 0, ti...]
    all_to_all x1, waiting for transfers between devices: 4.03 us -> 9.42 us  [on_device(): lax.all_to_all(mine, ROWS_COLS, 0, 0, tiled=True).reshape(devices, LANES)]
    all_to_all x0 -> x1, starting transfers between devices: none -> 4.63 us  [on_device(): lax.all_to_all(early.reshape(devices, 1, 2 * EARLY), ROWS_COLS, 0, 0, til...]
    pallas_call x1, Pallas kernels: 11.9 us -> 14.4 us  [on_device(): call(newton_kernel, (shape(slots, cells), shape(FIELDS - INPUT_FIELDS, ro...]
    pallas_call x1 -> x2, Pallas kernels: 3.17 us -> 5.22 us  [the longest x1 2.74 us: on_device(): call(pack_state_kernel, packed_shape, [SMEM, SMEM, VMEM, VMEM], VMEM, 8)]
    ppermute x2, waiting for transfers between devices: 0.01 us -> 1.15 us  [swap(): below = lax.ppermute(first, axis, down)]
  transfers between devices with their start and end apart: 6 -> 7, of which waited for: 2 -> 4; matrix products, arithmetic and copies ran while one was open for 0% -> 0% of each run, Pallas kernels for 4% -> 19%
where the time goes in v3:
time: 109 us; the launch traced here: 108 us
  waiting for transfers between devices  40.5 us (37%)
  starting transfers between devices  38.4 us (35%)
  Pallas kernels  26.5 us (24%)
  between operations  2.13 us (2%)
    all_to_all x1, waiting for transfers between devices, on_device(): lax.all_to_all(packed.reshape(devices, 1, 2 * width), ROWS_COLS, 0, 0, ti...  29.1 us
    pallas_call x1, Pallas kernels, on_device(): call(newton_kernel, (shape(slots, cells), shape(FIELDS - INPUT_FIELDS, ro...  14.4 us
    all_to_all x1, starting transfers between devices, on_device(): lax.all_to_all(packed.reshape(devices, 1, 2 * width), ROWS_COLS, 0, 0, ti...  14.2 us
    all_to_all x1, starting transfers between devices, on_device(): lax.all_to_all(mine, ROWS_COLS, 0, 0, tiled=True).reshape(devices, LANES)  11.2 us
    all_to_all x1, waiting for transfers between devices, on_device(): lax.all_to_all(mine, ROWS_COLS, 0, 0, tiled=True).reshape(devices, LANES)  9.42 us
    ppermute x2, starting transfers between devices, swap(): above = lax.ppermute(last, axis, up)  5.84 us
    all_to_all x1, starting transfers between devices, on_device(): lax.all_to_all(early.reshape(devices, 1, 2 * EARLY), ROWS_COLS, 0, 0, til...  4.63 us
    pallas_call x1, Pallas kernels, on_device(): call(macro_kernel, (shape(6, rows, lanes), packed_shape), [SMEM, SMEM] +...  3.19 us
  transfers between devices with their start and end apart: 7, of which 4 were waited for; matrix products, arithmetic and copies ran while one was open for 0% of the time, Pallas kernels for 19%

profile of v3, /device:TPU:0, one launch (start us, length us, event | category | flops | bytes accessed | tf_op | source)
XLA Modules:
  0.0 108.4 jit_solution(3482531733841936443)
XLA Ops:
  0.6 0.7 copy-done.6
  1.3 0.7 shard_map.147
  2.1 11.2 %all-to-all-start = ((f32[128,1,128]{2,1,0:T(1,128)}), f32[128,1,128]{2,1,0:T(1,128)S(1)}, u32[]{:S(2)}, u32[]{:S(2)}) async-start(f32[128,1,128]{2,1,0:T(1,128)} %shard_map.147), calls=%async_computation | async-start | bytes 131072 | tf_op jit(solution)/shard_map/all_to_all | solution.py:435
  13.3 9.4 %all-to-all-done = f32[128,1,128]{2,1,0:T(1,128)S(1)} async-done(((f32[128,1,128]{2,1,0:T(1,128)}), f32[128,1,128]{2,1,0:T(1,128)S(1)}, u32[]{:S(2)}, u32[]{:S(2)}) %all-to-all-start) | async-done | bytes 65568 | tf_op jit(solution)/shard_map/all_to_all | solution.py:435
  22.7 2.5 %shard_map.148 = (f32[256,1,1152]{2,1,0:T(1,128)}, s32[8,128]{1,0:T(8,128)S(1)}) custom-call(s32[1]{0:T(128)} %bitcast.here_ref, s32[160]{0:T(256)S(1)} %copy-done.7, f32[128,128]{1,0:T(8,128)S(1)} %bitcast.12, f32[160,1536]{1,0:T(8,128)S(1)} %copy-done), custom_call_target="tpu_custom_call" | custom-call | tf_op jit(solution)/shard_map/pallas_call | solution.py:436
  25.2 4.6 %all-to-all-start.1 = ((f32[128,1,2304]{2,1,0:T(1,128)}), f32[128,1,2304]{2,1,0:T(1,128)S(1)}, u32[]{:S(2)}, u32[]{:S(2)}) async-start(f32[128,1,2304]{2,1,0:T(1,128)} %bitcast.3), calls=%async_computation.1 | async-start | bytes 2359296 | tf_op jit(solution)/shard_map/all_to_all | solution.py:443
  29.8 0.0 copy-start.3
  29.8 0.0 copy-start.4
  29.9 0.0 copy-start.1
  29.9 14.4 %shard_map.149 = (f32[160,1536]{1,0:T(8,128)S(1)}, f32[9,64,128]{2,1,0:T(8,128)S(1)}) custom-call(s32[1,160]{1,0:T(1,128)S(1)} %bitcast.16, s32[1,160]{1,0:T(1,128)S(1)} %bitcast.14, f32[3,64,128]{2,1,0:T(8,128)S(1)} %copy-done.2, bf16[1536,1536]{1,0:T(8,128)(2,1)} %stiffness_hbm.1, f32[3,1536]{1,0:T(4,128)S(1)} %copy-done.9, f32[160,1536]{1,0:T(8,128)} %old_state_hbm.1, ...), custom_call_target="tpu_custom_call" | custom-call | flops 6794772480 | bytes 7667712 | tf_op jit(solution)/shard_map/pallas_call | solution.py:445
  44.3 0.2 shard_map.150
  44.5 1.3 %collective-permute-start = (f32[72,128]{1,0:T(8,128)S(1)}, f32[72,128]{1,0:T(8,128)S(1)}, u32[]{:S(2)}, u32[]{:S(2)}) collective-permute-start(f32[72,128]{1,0:T(8,128)S(1)} %get-tuple-element.19), channel_id=1, source_target_pairs={{16,0},{32,16},{48,32},{64,48},{80,64},{96,80},{112,96},{17,1},{33... | collective-permute-start | bytes 110600 | tf_op jit(solution)/shard_map/ppermute | solution.py:412
  45.8 3.0 %collective-permute-start.1 = (f32[72,128]{1,0:T(8,128)S(1)}, f32[72,128]{1,0:T(8,128)S(1)}, u32[]{:S(2)}, u32[]{:S(2)}) collective-permute-start(f32[72,128]{1,0:T(8,128)S(1)} %get-tuple-element.20), channel_id=1, source_target_pairs={{0,16},{16,32},{32,48},{48,64},{64,80},{80,96},{96,112},{1,17},{17... | collective-permute-start | bytes 110600 | tf_op jit(solution)/shard_map/ppermute | solution.py:411
  48.8 0.8 collective-permute-done.1.above_ref
  49.7 0.5 shard_map.151
  50.1 2.8 %collective-permute-start.2 = (f32[72,128]{1,0:T(8,128)S(1)}, f32[72,128]{1,0:T(8,128)S(1)}, u32[]{:S(2)}, u32[]{:S(2)}) collective-permute-start(f32[72,128]{1,0:T(8,128)S(1)} %get-tuple-element.21), channel_id=1, source_target_pairs={{0,1},{1,2},{2,3},{3,4},{4,5},{5,6},{6,7},{7,8},{8,9},{9,10},{10,1... | collective-permute-start | bytes 110600 | tf_op jit(solution)/shard_map/ppermute | solution.py:411
  52.9 1.3 %collective-permute-start.3 = (f32[72,128]{1,0:T(8,128)S(1)}, f32[72,128]{1,0:T(8,128)S(1)}, u32[]{:S(2)}, u32[]{:S(2)}) collective-permute-start(f32[72,128]{1,0:T(8,128)S(1)} %get-tuple-element.22), channel_id=1, source_target_pairs={{1,0},{2,1},{3,2},{4,3},{5,4},{6,5},{7,6},{8,7},{9,8},{10,9},{11,1... | collective-permute-start | bytes 110600 | tf_op jit(solution)/shard_map/ppermute | solution.py:412
  54.2 0.1 pad_add_fusion.place_ref
  55.0 2.7 %shard_map.152.packed_hbm = f32[256,1,2048]{2,1,0:T(1,128)} custom-call(s32[8,128]{1,0:T(8,128)S(1)} %get-tuple-element.15.plan_ref, s32[160]{0:T(256)S(1)} %copy-done.7, f32[160,1536]{1,0:T(8,128)S(1)} %get-tuple-element.23.state_ref, f32[160,1536]{1,0:T(8,128)S(1)} %copy-done.1), custom_call_target="tpu_custom_call" | custom-call | tf_op jit(solution)/shard_map/pallas_call | solution.py:473
  57.7 1.1 %collective-permute-done.3.right_ref = f32[72,128]{1,0:T(8,128)S(1)} collective-permute-done((f32[72,128]{1,0:T(8,128)S(1)}, f32[72,128]{1,0:T(8,128)S(1)}, u32[]{:S(2)}, u32[]{:S(2)}) %collective-permute-start.3) | collective-permute-done | bytes 36896 | tf_op jit(solution)/shard_map/ppermute | solution.py:412
  58.9 3.2 %shard_map.153 = (f32[6,64,128]{2,1,0:T(8,128)S(1)}, f32[256,1,2048]{2,1,0:T(1,128)}) custom-call(s32[4]{0:T(128)S(1)} %pad_add_fusion.place_ref, f32[1]{0:T(128)S(6)} %copy.21.load_ref, f32[18,64,128]{2,1,0:T(8,128)S(1)} %get-tuple-element.18.field_ref, f32[72,128]{1,0:T(8,128)S(1)} %collective-permute-done.below_ref, ...), custom_call_target="tpu_custom_call", output_to_operand_aliasing={{1}: (7, {})} | custom-call | flops 200000000 | bytes 2000000 | tf_op jit(solution)/shard_map/pallas_call | solution.py:480
  62.1 14.2 %all-to-all-start.2 = ((f32[128,1,4096]{2,1,0:T(1,128)}), f32[128,1,4096]{2,1,0:T(1,128)S(1)}, u32[]{:S(2)}, u32[]{:S(2)}) async-start(f32[128,1,4096]{2,1,0:T(1,128)} %bitcast.8), calls=%async_computation.2 | async-start | bytes 4194304 | tf_op jit(solution)/shard_map/all_to_all | solution.py:490
  76.9 29.1 %all-to-all-done.2 = f32[128,1,4096]{2,1,0:T(1,128)S(1)} async-done(((f32[128,1,4096]{2,1,0:T(1,128)}), f32[128,1,4096]{2,1,0:T(1,128)S(1)}, u32[]{:S(2)}, u32[]{:S(2)}) %all-to-all-start.2) | async-done | bytes 2097184 | tf_op jit(solution)/shard_map/all_to_all | solution.py:490
  106.1 2.4 %shard_map.154 = (f32[3,64,128]{2,1,0:T(8,128)}, f32[1]{0:T(128)}, f32[80,1536]{1,0:T(8,128)}, f32[80,1536]{1,0:T(8,128)}) custom-call(s32[8,128]{1,0:T(8,128)S(1)} %get-tuple-element.15.plan_ref, f32[1]{0:T(128)S(6)} %copy.21.load_ref, f32[1]{0:T(128)S(6)} %copy.22.radius_ref, f32[256,1,1152]{2,1,0:T(1,128)S(1)} %bitcast.11, f32[256,1,2048]{2,1,0:T(1,128)S(1)} %bitcast.10, ...), custom_call_target="tpu_custom_call" | custom-call | tf_op jit(solution)/shard_map/pallas_call | solution.py:492
  (19 shorter events, 0.0 us)
Async XLA Ops:
  0.6 0.7 copy-start.6
  1.3 21.4 %copy-start = (f32[160,1536]{1,0:T(8,128)S(1)}, f32[160,1536]{1,0:T(8,128)}, u32[]{:S(2)}) copy-start(f32[160,1536]{1,0:T(8,128)} %history_ref.3) | copy-start | bytes 2949124
  1.3 21.4 %copy-start.7 = (s32[160]{0:T(256)S(1)}, s32[160]{0:T(256)}, u32[]{:S(2)}) copy-start(s32[160]{0:T(256)} %steps_ref.3) | copy-start | bytes 1924
  2.1 27.7 %copy-start.2 = (f32[3,64,128]{2,1,0:T(8,128)S(1)}, f32[3,64,128]{2,1,0:T(8,128)}, u32[]{:S(2)}) copy-start(f32[3,64,128]{2,1,0:T(8,128)} %jump_ref.3) | copy-start | bytes 294916
  2.1 27.8 %copy-start.8 = (s32[160]{0:T(256)S(1)}, s32[160]{0:T(256)}, u32[]{:S(2)}) copy-start(s32[160]{0:T(256)} %param.23) | copy-start | bytes 1924
  2.1 27.8 %copy-start.9 = (f32[3,1536]{1,0:T(4,128)S(1)}, f32[3,1536]{1,0:T(4,128)}, u32[]{:S(2)}) copy-start(f32[3,1536]{1,0:T(4,128)} %coupling_ref.1) | copy-start | bytes 55300
  2.1 20.6 %all-to-all-start = ((f32[128,1,128]{2,1,0:T(1,128)}), f32[128,1,128]{2,1,0:T(1,128)S(1)}, u32[]{:S(2)}, u32[]{:S(2)}) async-start(f32[128,1,128]{2,1,0:T(1,128)} %shard_map.147), calls=%async_computation | async-start | bytes 131072 | tf_op jit(solution)/shard_map/all_to_all | solution.py:435
  25.2 36.9 %all-to-all-start.1 = ((f32[128,1,2304]{2,1,0:T(1,128)}), f32[128,1,2304]{2,1,0:T(1,128)S(1)}, u32[]{:S(2)}, u32[]{:S(2)}) async-start(f32[128,1,2304]{2,1,0:T(1,128)} %bitcast.3), calls=%async_computation.1 | async-start | bytes 2359296 | tf_op jit(solution)/shard_map/all_to_all | solution.py:443
  29.8 14.5 %copy-start.3 = (f32[3,64,128]{2,1,0:T(8,128)S(1)}, f32[3,64,128]{2,1,0:T(8,128)}, u32[]{:S(2)}) copy-start(f32[3,64,128]{2,1,0:T(8,128)} %external_ref.1) | copy-start | bytes 294916
  29.8 14.5 %copy-start.4 = (s32[2,64,128]{2,1,0:T(8,128)S(1)}, s32[2,64,128]{2,1,0:T(8,128)}, u32[]{:S(2)}) copy-start(s32[2,64,128]{2,1,0:T(8,128)} %mask_ref.1) | copy-start | bytes 196612
  29.9 14.5 %copy-start.5 = (f32[64,128]{1,0:T(8,128)S(1)}, f32[64,128]{1,0:T(8,128)}, u32[]{:S(2)}) copy-start(f32[64,128]{1,0:T(8,128)} %cohesive_ref.1) | copy-start | bytes 98308
  29.9 25.1 %copy-start.1 = (f32[160,1536]{1,0:T(8,128)S(1)}, f32[160,1536]{1,0:T(8,128)}, u32[]{:S(2)}) copy-start(f32[160,1536]{1,0:T(8,128)} %history_ref.3) | copy-start | bytes 2949124
  44.5 4.3 %collective-permute-start = (f32[72,128]{1,0:T(8,128)S(1)}, f32[72,128]{1,0:T(8,128)S(1)}, u32[]{:S(2)}, u32[]{:S(2)}) collective-permute-start(f32[72,128]{1,0:T(8,128)S(1)} %get-tuple-element.19), channel_id=1, source_target_pairs={{16,0},{32,16},{48,32},{64,48},{80,64},{96,80},{112,96},{17,1},{33... | collective-permute-start | bytes 110600 | tf_op jit(solution)/shard_map/ppermute | solution.py:412
  45.8 3.9 %collective-permute-start.1 = (f32[72,128]{1,0:T(8,128)S(1)}, f32[72,128]{1,0:T(8,128)S(1)}, u32[]{:S(2)}, u32[]{:S(2)}) collective-permute-start(f32[72,128]{1,0:T(8,128)S(1)} %get-tuple-element.20), channel_id=1, source_target_pairs={{0,16},{16,32},{32,48},{48,64},{64,80},{80,96},{96,112},{1,17},{17... | collective-permute-start | bytes 110600 | tf_op jit(solution)/shard_map/ppermute | solution.py:411
  50.1 7.6 %collective-permute-start.2 = (f32[72,128]{1,0:T(8,128)S(1)}, f32[72,128]{1,0:T(8,128)S(1)}, u32[]{:S(2)}, u32[]{:S(2)}) collective-permute-start(f32[72,128]{1,0:T(8,128)S(1)} %get-tuple-element.21), channel_id=1, source_target_pairs={{0,1},{1,2},{2,3},{3,4},{4,5},{5,6},{6,7},{7,8},{8,9},{9,10},{10,1... | collective-permute-start | bytes 110600 | tf_op jit(solution)/shard_map/ppermute | solution.py:411
  52.9 5.9 %collective-permute-start.3 = (f32[72,128]{1,0:T(8,128)S(1)}, f32[72,128]{1,0:T(8,128)S(1)}, u32[]{:S(2)}, u32[]{:S(2)}) collective-permute-start(f32[72,128]{1,0:T(8,128)S(1)} %get-tuple-element.22), channel_id=1, source_target_pairs={{1,0},{2,1},{3,2},{4,3},{5,4},{6,5},{7,6},{8,7},{9,8},{10,9},{11,1... | collective-permute-start | bytes 110600 | tf_op jit(solution)/shard_map/ppermute | solution.py:412
  62.1 44.0 %all-to-all-start.2 = ((f32[128,1,4096]{2,1,0:T(1,128)}), f32[128,1,4096]{2,1,0:T(1,128)S(1)}, u32[]{:S(2)}, u32[]{:S(2)}) async-start(f32[128,1,4096]{2,1,0:T(1,128)} %bitcast.8), calls=%async_computation.2 | async-start | bytes 4194304 | tf_op jit(solution)/shard_map/all_to_all | solution.py:490

commit v4 on v2

--- a/solution.py
+++ b/solution.py
@@ -13,6 +13,7 @@
 HALO = 4
 INPUT_FIELDS = 9
 FIELDS = 18
+NEWTON_MIB = 52
 LANES = 128
 ROWS_COLS = ("row", "col")
 VMEM = pl.BlockSpec(memory_space=pltpu.VMEM)
@@ -71,10 +72,21 @@
 
 
 def newton_kernel(
-    ids_ref, steps_ref, jump_ref, stiffness_ref, coupling_ref, old_state_ref, history_ref,
+    ids_ref, steps_ref, jump_ref, stiffness_hbm, coupling_ref, old_state_hbm, history_hbm,
     state_ref, grid_ref,
-    damage_ref, load_ref, diagonal_ref, rounded_ref,
+    stiffness_ref, damage_ref, load_ref, diagonal_ref, rounded_ref, sems,
 ):
+    width = 256
+    cuts = [slice(t * width, (t + 1) * width) for t in range(stiffness_hbm.shape[1] // width)]
+    copies = [
+        pltpu.make_async_copy(stiffness_hbm.at[:, part], stiffness_ref.at[:, part], sems.at[t])
+        for t, part in enumerate(cuts)
+    ]
+    get_history = pltpu.make_async_copy(history_hbm, damage_ref, sems.at[len(cuts)])
+    get_state = pltpu.make_async_copy(old_state_hbm, state_ref, sems.at[len(cuts) + 1])
+    ahead = 3
+    for copy in (get_history, get_state):
+        copy.start()
     slots, cells = state_ref.shape
     _, rows, lanes = jump_ref.shape
     wide = 2 * lanes
@@ -102,23 +114,25 @@
     load_ref[...] = (
         drive[0] * coupling_ref[0:1, :] + drive[1] * coupling_ref[1:2, :] + drive[2] * coupling_ref[2:3, :]
     )
-    damage_ref[...] = jnp.exp(-history_ref[...])
-    first_state = old_state_ref[...]
-    state_ref[...] = first_state
-    rounded_ref[0] = first_state.astype(BF16)
-    eye = iota((LANES, LANES), 0) == iota((LANES, LANES), 1)
-    for t in range(cells // LANES):
-        part = slice(t * LANES, (t + 1) * LANES)
-        block = stiffness_ref[part, part].astype(F32)
-        diagonal_ref[:, part] = jnp.sum(jnp.where(eye, block, 0.0), axis=0, keepdims=True)
-    width = 256
-
-    def advance(count, carry):
-        now = lax.rem(count, 2)
+    get_history.wait()
+    for copy in copies[:ahead]:
+        copy.start()
+    damage_ref[...] = jnp.exp(-damage_ref[...])
+    get_state.wait()
+    rounded_ref[0] = state_ref[...].astype(BF16)
+    eye = iota((width, width), 0) == iota((width, width), 1)
+
+    def advance(count, carry, waiting=False):
+        now = count % 2 if waiting else lax.rem(count, 2)
         rounded = rounded_ref[now]
-        moving = count.astype(F32) < steps
-        for t in range(cells // width):
-            part = slice(t * width, (t + 1) * width)
+        moving = steps > jnp.asarray(count, jnp.int32).astype(F32)
+        for t, part in enumerate(cuts):
+            if waiting:
+                copies[t].wait()
+                if t + ahead < len(copies):
+                    copies[t + ahead].start()
+                block = stiffness_ref[part, part].astype(F32)
+                diagonal_ref[:, part] = jnp.sum(jnp.where(eye, block, 0.0), axis=0, keepdims=True)
             force = jnp.dot(rounded, stiffness_ref[:, part], preferred_element_type=F32)
             current = state_ref[:, part]
             bent = jnp.tanh(current)
@@ -130,7 +144,8 @@
             rounded_ref[1 - now, :, part] = current.astype(BF16)
         return carry
 
-    lax.fori_loop(0, MAX_STEPS, advance, 0)
+    advance(0, 0, waiting=True)
+    lax.fori_loop(1, MAX_STEPS, advance, 0)
     bent = jnp.tanh(state_ref[...])
     damage = damage_ref[...]
     pull = damage * bent
@@ -192,7 +207,7 @@
     source = jnp.sum(jnp.where(starts <= wanted, 1.0, 0.0), axis=0, keepdims=True) - 1.0
     index = jnp.where(wanted < total, 2.0 * source + (slot % 2).astype(F32), -1.0).astype(jnp.int32)
     plan_ref[...] = jnp.broadcast_to(index, plan_ref.shape)
-    places = out_ref.shape[0]
+    places = 2 * out_ref.shape[0]
     unused = lax.rem(2 * (start // 2) + places - 2, places)
     group = 8
 
@@ -203,8 +218,9 @@
         for k in range(group):
             alive = steps_ref[at + k] > 0
             to = jnp.where(alive, lax.rem(rank, places), unused)
-            out_ref[pl.ds(to, 1), 0, :cells] = state[k : k + 1]
-            out_ref[pl.ds(to, 1), 0, cells : 2 * cells] = history[k : k + 1]
+            at_lane = pl.multiple_of(lax.rem(to, 2) * (2 * cells), LANES)
+            out_ref[pl.ds(to // 2, 1), 0, pl.ds(at_lane, cells)] = state[k : k + 1]
+            out_ref[pl.ds(to // 2, 1), 0, pl.ds(at_lane + cells, cells)] = history[k : k + 1]
             rank = rank + alive.astype(jnp.int32)
         return rank
 
@@ -332,7 +348,7 @@
     new_jump_ref, new_load_ref, new_state_ref, new_history_ref,
 ):
     new_cap, cells = new_state_ref.shape
-    whole = 0.5 * jnp.sum(arrived_ref[:, 0, 2 * cells :], axis=0, keepdims=True)
+    whole = jnp.sum(arrived_ref[:, 0, 4 * cells :], axis=0, keepdims=True)
     half = iota(whole.shape, 1) < LANES // 2
     other = pltpu.roll(whole, LANES // 2, 1)
     cross, square = jnp.where(half, whole, other), jnp.where(half, other, whole)
@@ -349,8 +365,9 @@
             index = plan_ref[0, at + k]
             valid = index >= 0
             source = jnp.maximum(index, 0)
-            state = arrived_ref[pl.ds(source, 1), 0, :cells]
-            history = arrived_ref[pl.ds(source, 1), 0, cells : 2 * cells]
+            at_lane = pl.multiple_of(lax.rem(source, 2) * (2 * cells), LANES)
+            state = arrived_ref[pl.ds(source // 2, 1), 0, pl.ds(at_lane, cells)]
+            history = arrived_ref[pl.ds(source // 2, 1), 0, pl.ds(at_lane + cells, cells)]
             new_state_ref[pl.ds(at + k, 1), :] = jnp.where(valid, state, 0.0)
             new_history_ref[pl.ds(at + k, 1), :] = jnp.where(valid, jnp.maximum(history, jnp.abs(state)), 0.0)
         return carry
@@ -398,8 +415,7 @@
     slots, cells = old_state.shape
     _, rows, lanes = jump.shape
     edge = HALO * FIELDS
-    width = 2 * cells + LANES
-    packed_shape = shape(2 * devices, 1, width)
+    packed_shape = shape(devices, 1, 4 * cells + LANES)
     place = jnp.stack([row_at, col_at, n_row, n_col]).astype(jnp.int32)
     ids_row = point_ids.reshape(1, slots)
     steps_row = newton_steps.reshape(1, slots)
@@ -409,14 +425,16 @@
     state, grid = call(
         newton_kernel,
         (shape(slots, cells), shape(FIELDS - INPUT_FIELDS, rows, lanes)),
-        [VMEM] * 7,
+        [VMEM] * 3 + [HBM, VMEM, HBM, HBM],
         (VMEM, VMEM),
-        24,
+        NEWTON_MIB,
         scratch=(
+            pltpu.VMEM(stiffness.shape, BF16),
             pltpu.VMEM((slots, cells), F32),
             pltpu.VMEM((slots, cells), F32),
             pltpu.VMEM((1, cells), F32),
             pltpu.VMEM((2, slots, cells), BF16),
+            pltpu.SemaphoreType.DMA((cells // 256 + 2,)),
         ),
         cost=pl.CostEstimate(
             flops=2 * MAX_STEPS * slots * cells * cells,
@@ -449,12 +467,11 @@
         [SMEM, SMEM] + [VMEM] * 5 + [HBM],
         (VMEM, HBM),
         12,
-        scratch=(pltpu.VMEM((2 * devices, 1, LANES), F32), pltpu.SemaphoreType.DMA),
+        scratch=(pltpu.VMEM((devices, 1, LANES), F32), pltpu.SemaphoreType.DMA),
         cost=pl.CostEstimate(flops=200_000_000, transcendentals=0, bytes_accessed=2_000_000),
         aliases={7: 1},
     )(place, load_factor, fields, below, above, left, right, packed)
-    arrived = lax.all_to_all(packed.reshape(devices, 1, 2 * width), ROWS_COLS, 0, 0, tiled=True)
-    arrived = arrived.reshape(2 * devices, 1, width)
+    arrived = lax.all_to_all(packed, ROWS_COLS, 0, 0, tiled=True)
     new_jump, new_load, new_state, new_history = call(
         functools.partial(last_kernel, 3.0 * rows * lanes * devices),
         (shape(3, rows, lanes), shape(1), shape(slots // 2, cells), shape(slots // 2, cells)),

time: 107 us -> 104 us (0.972)
  local copies, waits for them, and re-layouts: 7.74 us -> 3 us
  Pallas kernels: 21.9 us -> 26.2 us
    unnamed x24 -> x18, local copies, waits for them, and re-layouts: 7.74 us -> 3 us
    pallas_call x1, Pallas kernels: 11.9 us -> 14.9 us  [on_device(): call(newton_kernel, (shape(slots, cells), shape(FIELDS - INPUT_FIELDS, ro...]
  transfers between devices with their start and end apart: 6 -> 6, of which waited for: 2 -> 2; matrix products, arithmetic and copies ran while one was open for 0% -> 0% of each run, Pallas kernels for 4% -> 5%
where the time goes in v4:
time: 104 us
  waiting for transfers between devices  44.5 us (43%)
  starting transfers between devices  28 us (27%)
  Pallas kernels  26.2 us (25%)
  local copies, waits for them, and re-layouts  3 us (3%)
  between operations  2.08 us (2%)
    all_to_all x1, waiting for transfers between devices, on_device(): arrived = lax.all_to_all(packed, ROWS_COLS, 0, 0, tiled=True)  40.4 us
    pallas_call x1, Pallas kernels, on_device(): call(newton_kernel, (shape(slots, cells), shape(FIELDS - INPUT_FIELDS, ro...  14.9 us
    all_to_all x1, starting transfers between devices, on_device(): lax.all_to_all(mine, ROWS_COLS, 0, 0, tiled=True).reshape(devices, LANES)  11.8 us
    all_to_all x1, starting transfers between devices, on_device(): arrived = lax.all_to_all(packed, ROWS_COLS, 0, 0, tiled=True)  7.55 us
    ppermute x2, starting transfers between devices, swap(): above = lax.ppermute(last, axis, up)  6.03 us
    pallas_call x1, Pallas kernels, on_device(): call(pack_kernel, (packed_shape, shape(8, LANES, dtype=jnp.int32)), [SMEM...  4.15 us
    all_to_all x1, waiting for transfers between devices, on_device(): lax.all_to_all(mine, ROWS_COLS, 0, 0, tiled=True).reshape(devices, LANES)  4.03 us
    pallas_call x1, Pallas kernels, on_device(): call(macro_kernel, (shape(6, rows, lanes), packed_shape), [SMEM, SMEM] +...  3.14 us
  transfers between devices with their start and end apart: 6, of which 2 were waited for; matrix products, arithmetic and copies ran while one was open for 0% of the time, Pallas kernels for 5%

profile of v4, /device:TPU:0, one launch (start us, length us, event | category | flops | bytes accessed | tf_op | source)
XLA Modules:
  0.0 103.8 jit_solution(14995230678877633934)
XLA Ops:
  0.6 0.9 copy-done.1
  1.5 0.7 copy-done.5
  2.2 0.7 copy-done.7
  2.9 0.7 copy-done.8
  3.6 14.9 %shard_map.148 = (f32[160,1536]{1,0:T(8,128)S(1)}, f32[9,64,128]{2,1,0:T(8,128)S(1)}) custom-call(s32[1,160]{1,0:T(1,128)S(1)} %bitcast.10, s32[1,160]{1,0:T(1,128)S(1)} %bitcast.7, f32[3,64,128]{2,1,0:T(8,128)S(1)} %copy-done.1, bf16[1536,1536]{1,0:T(8,128)(2,1)} %stiffness_hbm.1, f32[3,1536]{1,0:T(4,128)S(1)} %copy-done.8, f32[160,1536]{1,0:T(8,128)} %old_state_hbm.1, ...), custom_call_target="tpu_custom_call" | custom-call | flops 6794772480 | bytes 7667712 | tf_op jit(solution)/shard_map/pallas_call | solution.py:425
  18.6 0.2 shard_map.150
  18.7 1.3 %collective-permute-start = (f32[72,128]{1,0:T(8,128)S(1)}, f32[72,128]{1,0:T(8,128)S(1)}, u32[]{:S(2)}, u32[]{:S(2)}) collective-permute-start(f32[72,128]{1,0:T(8,128)S(1)} %get-tuple-element.19), channel_id=1, source_target_pairs={{16,0},{32,16},{48,32},{64,48},{80,64},{96,80},{112,96},{17,1},{33... | collective-permute-start | bytes 110600 | tf_op jit(solution)/shard_map/ppermute | solution.py:403
  20.0 0.0 copy-start
  20.0 0.0 copy-start.6
  20.1 3.2 %collective-permute-start.1 = (f32[72,128]{1,0:T(8,128)S(1)}, f32[72,128]{1,0:T(8,128)S(1)}, u32[]{:S(2)}, u32[]{:S(2)}) collective-permute-start(f32[72,128]{1,0:T(8,128)S(1)} %get-tuple-element.20), channel_id=1, source_target_pairs={{0,16},{16,32},{32,48},{48,64},{64,80},{80,96},{96,112},{1,17},{17... | collective-permute-start | bytes 110600 | tf_op jit(solution)/shard_map/ppermute | solution.py:402
  23.2 0.7 shard_map.147
  24.0 11.8 %all-to-all-start = ((f32[128,1,128]{2,1,0:T(1,128)}), f32[128,1,128]{2,1,0:T(1,128)S(1)}, u32[]{:S(2)}, u32[]{:S(2)}) async-start(f32[128,1,128]{2,1,0:T(1,128)} %shard_map.147), calls=%async_computation | async-start | bytes 131072 | tf_op jit(solution)/shard_map/all_to_all | solution.py:424
  35.8 0.0 collective-permute-done.below_ref
  35.9 0.5 shard_map.151
  36.3 2.9 %collective-permute-start.2 = (f32[72,128]{1,0:T(8,128)S(1)}, f32[72,128]{1,0:T(8,128)S(1)}, u32[]{:S(2)}, u32[]{:S(2)}) collective-permute-start(f32[72,128]{1,0:T(8,128)S(1)} %get-tuple-element.21), channel_id=1, source_target_pairs={{0,1},{1,2},{2,3},{3,4},{4,5},{5,6},{6,7},{7,8},{8,9},{9,10},{10,1... | collective-permute-start | bytes 110600 | tf_op jit(solution)/shard_map/ppermute | solution.py:402
  39.2 1.3 %collective-permute-start.3 = (f32[72,128]{1,0:T(8,128)S(1)}, f32[72,128]{1,0:T(8,128)S(1)}, u32[]{:S(2)}, u32[]{:S(2)}) collective-permute-start(f32[72,128]{1,0:T(8,128)S(1)} %get-tuple-element.22), channel_id=1, source_target_pairs={{1,0},{2,1},{3,2},{4,3},{5,4},{6,5},{7,6},{8,7},{9,8},{10,9},{11,1... | collective-permute-start | bytes 110600 | tf_op jit(solution)/shard_map/ppermute | solution.py:403
  40.5 0.1 pad_add_fusion.place_ref
  41.2 4.0 %all-to-all-done = f32[128,1,128]{2,1,0:T(1,128)S(1)} async-done(((f32[128,1,128]{2,1,0:T(1,128)}), f32[128,1,128]{2,1,0:T(1,128)S(1)}, u32[]{:S(2)}, u32[]{:S(2)}) %all-to-all-start) | async-done | bytes 65568 | tf_op jit(solution)/shard_map/all_to_all | solution.py:424
  45.3 4.2 %shard_map.149 = (f32[128,1,6272]{2,1,0:T(1,128)}, s32[8,128]{1,0:T(8,128)S(1)}) custom-call(s32[1]{0:T(128)} %bitcast.here_ref, s32[160]{0:T(256)S(1)} %copy-done.6, f32[128,128]{1,0:T(8,128)S(1)} %bitcast.6, f32[160,1536]{1,0:T(8,128)S(1)} %get-tuple-element.15.state_ref, f32[160,1536]{1,0:T(8,128)S(1)} %copy-done), custom_call_target="tpu_custom_call" | custom-call | tf_op jit(solution)/shard_map/pallas_call | solution.py:453
  49.4 0.0 collective-permute-done.2.left_ref
  49.4 3.1 %shard_map.152 = (f32[6,64,128]{2,1,0:T(8,128)S(1)}, f32[128,1,6272]{2,1,0:T(1,128)}) custom-call(s32[4]{0:T(128)S(1)} %pad_add_fusion.place_ref, f32[1]{0:T(128)S(6)} %copy.19.load_ref, f32[18,64,128]{2,1,0:T(8,128)S(1)} %get-tuple-element.18.field_ref, f32[72,128]{1,0:T(8,128)S(1)} %collective-permute-done.below_ref, ...), custom_call_target="tpu_custom_call", output_to_operand_aliasing={{1}: (7, {})} | custom-call | flops 200000000 | bytes 2000000 | tf_op jit(solution)/shard_map/pallas_call | solution.py:464
  52.6 7.5 %all-to-all-start.1 = ((f32[128,1,6272]{2,1,0:T(1,128)}), f32[128,1,6272]{2,1,0:T(1,128)S(1)}, u32[]{:S(2)}, u32[]{:S(2)}) async-start(f32[128,1,6272]{2,1,0:T(1,128)} %get-tuple-element.24), calls=%async_computation.1 | async-start | bytes 6422528 | tf_op jit(solution)/shard_map/all_to_all | solution.py:474
  60.8 40.4 %all-to-all-done.1.arrived_ref = f32[128,1,6272]{2,1,0:T(1,128)S(1)} async-done(((f32[128,1,6272]{2,1,0:T(1,128)}), f32[128,1,6272]{2,1,0:T(1,128)S(1)}, u32[]{:S(2)}, u32[]{:S(2)}) %all-to-all-start.1) | async-done | bytes 3211296 | tf_op jit(solution)/shard_map/all_to_all | solution.py:474
  101.2 2.6 %shard_map.153 = (f32[3,64,128]{2,1,0:T(8,128)}, f32[1]{0:T(128)}, f32[80,1536]{1,0:T(8,128)}, f32[80,1536]{1,0:T(8,128)}) custom-call(s32[8,128]{1,0:T(8,128)S(1)} %get-tuple-element.16.plan_ref, f32[1]{0:T(128)S(6)} %copy.19.load_ref, f32[1]{0:T(128)S(6)} %copy.20.radius_ref, f32[128,1,6272]{2,1,0:T(1,128)S(1)} %all-to-all-done.1.arrived_ref, ...), custom_call_target="tpu_custom_call" | custom-call | tf_op jit(solution)/shard_map/pallas_call | solution.py:475
  (14 shorter events, 0.0 us)
Async XLA Ops:
  0.6 0.9 copy-start.1
  1.5 0.7 copy-start.5
  2.2 0.7 copy-start.7
  2.9 0.7 copy-start.8
  3.6 14.9 %copy-start.2 = (f32[3,64,128]{2,1,0:T(8,128)S(1)}, f32[3,64,128]{2,1,0:T(8,128)}, u32[]{:S(2)}) copy-start(f32[3,64,128]{2,1,0:T(8,128)} %external_ref.1) | copy-start | bytes 294916
  3.6 14.9 %copy-start.3 = (s32[2,64,128]{2,1,0:T(8,128)S(1)}, s32[2,64,128]{2,1,0:T(8,128)}, u32[]{:S(2)}) copy-start(s32[2,64,128]{2,1,0:T(8,128)} %mask_ref.1) | copy-start | bytes 196612
  3.6 14.9 %copy-start.4 = (f32[64,128]{1,0:T(8,128)S(1)}, f32[64,128]{1,0:T(8,128)}, u32[]{:S(2)}) copy-start(f32[64,128]{1,0:T(8,128)} %cohesive_ref.1) | copy-start | bytes 98308
  18.7 17.1 %collective-permute-start = (f32[72,128]{1,0:T(8,128)S(1)}, f32[72,128]{1,0:T(8,128)S(1)}, u32[]{:S(2)}, u32[]{:S(2)}) collective-permute-start(f32[72,128]{1,0:T(8,128)S(1)} %get-tuple-element.19), channel_id=1, source_target_pairs={{16,0},{32,16},{48,32},{64,48},{80,64},{96,80},{112,96},{17,1},{33... | collective-permute-start | bytes 110600 | tf_op jit(solution)/shard_map/ppermute | solution.py:403
  20.0 25.2 %copy-start = (f32[160,1536]{1,0:T(8,128)S(1)}, f32[160,1536]{1,0:T(8,128)}, u32[]{:S(2)}) copy-start(f32[160,1536]{1,0:T(8,128)} %history_ref.1) | copy-start | bytes 2949124
  20.0 25.2 %copy-start.6 = (s32[160]{0:T(256)S(1)}, s32[160]{0:T(256)}, u32[]{:S(2)}) copy-start(s32[160]{0:T(256)} %steps_ref.1) | copy-start | bytes 1924
  20.1 15.8 %collective-permute-start.1 = (f32[72,128]{1,0:T(8,128)S(1)}, f32[72,128]{1,0:T(8,128)S(1)}, u32[]{:S(2)}, u32[]{:S(2)}) collective-permute-start(f32[72,128]{1,0:T(8,128)S(1)} %get-tuple-element.20), channel_id=1, source_target_pairs={{0,16},{16,32},{32,48},{48,64},{64,80},{80,96},{96,112},{1,17},{17... | collective-permute-start | bytes 110600 | tf_op jit(solution)/shard_map/ppermute | solution.py:402
  24.0 21.3 %all-to-all-start = ((f32[128,1,128]{2,1,0:T(1,128)}), f32[128,1,128]{2,1,0:T(1,128)S(1)}, u32[]{:S(2)}, u32[]{:S(2)}) async-start(f32[128,1,128]{2,1,0:T(1,128)} %shard_map.147), calls=%async_computation | async-start | bytes 131072 | tf_op jit(solution)/shard_map/all_to_all | solution.py:424
  36.3 13.1 %collective-permute-start.2 = (f32[72,128]{1,0:T(8,128)S(1)}, f32[72,128]{1,0:T(8,128)S(1)}, u32[]{:S(2)}, u32[]{:S(2)}) collective-permute-start(f32[72,128]{1,0:T(8,128)S(1)} %get-tuple-element.21), channel_id=1, source_target_pairs={{0,1},{1,2},{2,3},{3,4},{4,5},{5,6},{6,7},{7,8},{8,9},{9,10},{10,1... | collective-permute-start | bytes 110600 | tf_op jit(solution)/shard_map/ppermute | solution.py:402
  39.2 10.2 %collective-permute-start.3 = (f32[72,128]{1,0:T(8,128)S(1)}, f32[72,128]{1,0:T(8,128)S(1)}, u32[]{:S(2)}, u32[]{:S(2)}) collective-permute-start(f32[72,128]{1,0:T(8,128)S(1)} %get-tuple-element.22), channel_id=1, source_target_pairs={{1,0},{2,1},{3,2},{4,3},{5,4},{6,5},{7,6},{8,7},{9,8},{10,9},{11,1... | collective-permute-start | bytes 110600 | tf_op jit(solution)/shard_map/ppermute | solution.py:403
  52.6 48.6 %all-to-all-start.1 = ((f32[128,1,6272]{2,1,0:T(1,128)}), f32[128,1,6272]{2,1,0:T(1,128)S(1)}, u32[]{:S(2)}, u32[]{:S(2)}) async-start(f32[128,1,6272]{2,1,0:T(1,128)} %get-tuple-element.24), calls=%async_computation.1 | async-start | bytes 6422528 | tf_op jit(solution)/shard_map/all_to_all | solution.py:474

commit v5 on v4

--- a/solution.py
+++ b/solution.py
@@ -84,7 +84,6 @@
     ]
     get_history = pltpu.make_async_copy(history_hbm, damage_ref, sems.at[len(cuts)])
     get_state = pltpu.make_async_copy(old_state_hbm, state_ref, sems.at[len(cuts) + 1])
-    ahead = 3
     for copy in (get_history, get_state):
         copy.start()
     slots, cells = state_ref.shape
@@ -114,9 +113,9 @@
     load_ref[...] = (
         drive[0] * coupling_ref[0:1, :] + drive[1] * coupling_ref[1:2, :] + drive[2] * coupling_ref[2:3, :]
     )
+    for copy in copies:
+        copy.start()
     get_history.wait()
-    for copy in copies[:ahead]:
-        copy.start()
     damage_ref[...] = jnp.exp(-damage_ref[...])
     get_state.wait()
     rounded_ref[0] = state_ref[...].astype(BF16)
@@ -129,8 +128,6 @@
         for t, part in enumerate(cuts):
             if waiting:
                 copies[t].wait()
-                if t + ahead < len(copies):
-                    copies[t + ahead].start()
                 block = stiffness_ref[part, part].astype(F32)
                 diagonal_ref[:, part] = jnp.sum(jnp.where(eye, block, 0.0), axis=0, keepdims=True)
             force = jnp.dot(rounded, stiffness_ref[:, part], preferred_element_type=F32)
@@ -173,8 +170,12 @@
 
 
 def fields_kernel(
-    ids_ref, steps_ref, jump_ref, external_ref, cohesive_ref, mask_ref, grid_ref, field_ref, first_ref, last_ref
+    ids_ref, steps_ref, jump_ref, external_ref, cohesive_ref, mask_ref, grid_ref, counts_ref,
+    field_ref, first_ref, last_ref, line_ref,
 ):
+    counts = counts_ref[:, 0, :]
+    line = jnp.sum(jnp.where(iota(counts.shape, 0) == iota(counts.shape, 1), counts, 0.0), axis=0, keepdims=True)
+    line_ref[...] = jnp.broadcast_to(line[None], line_ref.shape)
     rows, lanes = cohesive_ref.shape
     slots = ids_ref.shape[1]
     ids = ids_ref[...]
@@ -194,9 +195,15 @@
 
 def pack_kernel(here_ref, steps_ref, counts_ref, state_ref, history_ref, out_ref, plan_ref):
     slots, cells = state_ref.shape
-    devices = counts_ref.shape[0]
+    devices = out_ref.shape[0]
     here = here_ref[0]
-    counts = counts_ref[...]
+    lines = counts_ref[:, 0, :]
+    n_row = lines.shape[0]
+    n_col = devices // n_row
+    pick = (iota((devices, n_row), 0) // n_col == iota((devices, n_row), 1)).astype(F32).astype(BF16)
+    spread = jnp.dot(pick, lines.astype(BF16), preferred_element_type=F32)
+    mine = iota(spread.shape, 0) % n_col == iota(spread.shape, 1)
+    counts = jnp.broadcast_to(jnp.sum(jnp.where(mine, spread, 0.0), axis=1, keepdims=True), (devices, LANES))
     before = (iota((devices, devices), 1) < iota((devices, devices), 0)).astype(F32).astype(BF16)
     starts = jnp.dot(before, counts.astype(BF16), preferred_element_type=F32)
     row = iota((devices, LANES), 0)
@@ -420,8 +427,8 @@
     ids_row = point_ids.reshape(1, slots)
     steps_row = newton_steps.reshape(1, slots)
 
-    mine = call(count_kernel, shape(devices, 1, LANES), [VMEM], VMEM, 2, cost=LONG)(steps_row)
-    counts = lax.all_to_all(mine, ROWS_COLS, 0, 0, tiled=True).reshape(devices, LANES)
+    mine = call(count_kernel, shape(n_col, 1, LANES), [VMEM], VMEM, 2, cost=LONG)(steps_row)
+    counts = lax.all_to_all(mine, "col", 0, 0, tiled=True)
     state, grid = call(
         newton_kernel,
         (shape(slots, cells), shape(FIELDS - INPUT_FIELDS, rows, lanes)),
@@ -442,14 +449,15 @@
             bytes_accessed=2 * cells * cells + 12 * slots * cells,
         ),
     )(ids_row, steps_row, jump, stiffness, coupling, old_state, old_history)
-    fields, first, last = call(
+    fields, first, last, line = call(
         fields_kernel,
-        (shape(FIELDS, rows, lanes), shape(edge, lanes), shape(edge, lanes)),
-        [VMEM] * 7,
-        (VMEM,) * 3,
+        (shape(FIELDS, rows, lanes), shape(edge, lanes), shape(edge, lanes), shape(n_row, 1, LANES)),
+        [VMEM] * 8,
+        (VMEM,) * 4,
         4,
-    )(ids_row, steps_row, jump, external, cohesive, bond_mask, grid)
+    )(ids_row, steps_row, jump, external, cohesive, bond_mask, grid, counts)
     below, above = swap(first, last, "row")
+    counts = lax.all_to_all(line, "row", 0, 0, tiled=True)
     packed, plan = call(
         pack_kernel,
         (packed_shape, shape(8, LANES, dtype=jnp.int32)),

time: 104 us -> 104 us (level)
  starting transfers between devices: 28 us -> 33.8 us
  waiting for transfers between devices: 44.5 us -> 40.4 us
  local copies, waits for them, and re-layouts: 3 us -> 0.71 us
    all_to_all x1 -> x2, waiting for transfers between devices: 4.03 us -> 0.01 us  [the longest x1 0.01 us: on_device(): counts = lax.all_to_all(line, 'row', 0, 0, tiled=True)]
    all_to_all x1, starting transfers between devices: 7.55 us -> 11.5 us  [on_device(): arrived = lax.all_to_all(packed, ROWS_COLS, 0, 0, tiled=True)]
    unnamed x18, local copies, waits for them, and re-layouts: 3 us -> 0.71 us
    all_to_all x1 -> x2, starting transfers between devices: 11.8 us -> 12.9 us  [the longest x1 8.16 us: on_device(): counts = lax.all_to_all(mine, 'col', 0, 0, tiled=True)]
  transfers between devices with their start and end apart: 6 -> 7, of which waited for: 2 -> 1; matrix products, arithmetic and copies ran while one was open for 0% -> 0% of each run, Pallas kernels for 5% -> 19%
where the time goes in v5:
time: 104 us; the launch traced here: 103 us
  waiting for transfers between devices  40.4 us (39%)
  starting transfers between devices  33.8 us (32%)
  Pallas kernels  26.3 us (25%)
  between operations  2.14 us (2%)
    all_to_all x1, waiting for transfers between devices, on_device(): arrived = lax.all_to_all(packed, ROWS_COLS, 0, 0, tiled=True)  40.4 us
    pallas_call x1, Pallas kernels, on_device(): call(newton_kernel, (shape(slots, cells), shape(FIELDS - INPUT_FIELDS, ro...  14.3 us
    all_to_all x1, starting transfers between devices, on_device(): arrived = lax.all_to_all(packed, ROWS_COLS, 0, 0, tiled=True)  11.5 us
    all_to_all x1, starting transfers between devices, on_device(): counts = lax.all_to_all(mine, 'col', 0, 0, tiled=True)  8.16 us
    ppermute x2, starting transfers between devices, swap(): above = lax.ppermute(last, axis, up)  6.85 us
    all_to_all x1, starting transfers between devices, on_device(): counts = lax.all_to_all(line, 'row', 0, 0, tiled=True)  4.73 us
    pallas_call x1, Pallas kernels, on_device(): call(pack_kernel, (packed_shape, shape(8, LANES, dtype=jnp.int32)), [SMEM...  4.36 us
    pallas_call x1, Pallas kernels, on_device(): call(macro_kernel, (shape(6, rows, lanes), packed_shape), [SMEM, SMEM] +...  3.16 us
  transfers between devices with their start and end apart: 7, of which 1 were waited for; matrix products, arithmetic and copies ran while one was open for 0% of the time, Pallas kernels for 19%

profile of v5, /device:TPU:0, one launch (start us, length us, event | category | flops | bytes accessed | tf_op | source)
XLA Modules:
  0.0 103.4 jit_solution(8935817802928233801)
XLA Ops:
  0.6 0.7 copy-done.5
  1.3 0.7 shard_map.148
  2.0 8.2 %all-to-all-start = ((f32[16,1,128]{2,1,0:T(1,128)}), f32[16,1,128]{2,1,0:T(1,128)S(1)}, u32[]{:S(2)}, u32[]{:S(2)}) async-start(f32[16,1,128]{2,1,0:T(1,128)} %shard_map.148), calls=%async_computation | async-start | bytes 16384 | tf_op jit(solution)/shard_map/all_to_all | solution.py:431
  10.2 0.0 copy-start.2
  10.2 0.0 copy-start.3
  10.2 0.0 copy-start.4
  10.2 0.0 copy-start
  10.3 14.3 %shard_map.147 = (f32[160,1536]{1,0:T(8,128)S(1)}, f32[9,64,128]{2,1,0:T(8,128)S(1)}) custom-call(s32[1,160]{1,0:T(1,128)S(1)} %bitcast.8, s32[1,160]{1,0:T(1,128)S(1)} %bitcast.6, f32[3,64,128]{2,1,0:T(8,128)S(1)} %copy-done.1, bf16[1536,1536]{1,0:T(8,128)(2,1)} %stiffness_hbm.1, f32[3,1536]{1,0:T(4,128)S(1)} %copy-done.8, f32[160,1536]{1,0:T(8,128)} %old_state_hbm.1, ...), custom_call_target="tpu_custom_call" | custom-call | flops 6794772480 | bytes 7667712 | tf_op jit(solution)/shard_map/pallas_call | solution.py:432
  24.7 0.7 shard_map.149
  25.3 1.3 %collective-permute-start = (f32[72,128]{1,0:T(8,128)S(1)}, f32[72,128]{1,0:T(8,128)S(1)}, u32[]{:S(2)}, u32[]{:S(2)}) collective-permute-start(f32[72,128]{1,0:T(8,128)S(1)} %get-tuple-element.21), channel_id=1, source_target_pairs={{16,0},{32,16},{48,32},{64,48},{80,64},{96,80},{112,96},{17,1},{33... | collective-permute-start | bytes 110600 | tf_op jit(solution)/shard_map/ppermute | solution.py:410
  26.6 3.0 %collective-permute-start.1 = (f32[72,128]{1,0:T(8,128)S(1)}, f32[72,128]{1,0:T(8,128)S(1)}, u32[]{:S(2)}, u32[]{:S(2)}) collective-permute-start(f32[72,128]{1,0:T(8,128)S(1)} %get-tuple-element.22), channel_id=1, source_target_pairs={{0,16},{16,32},{32,48},{48,64},{64,80},{80,96},{96,112},{1,17},{17... | collective-permute-start | bytes 110600 | tf_op jit(solution)/shard_map/ppermute | solution.py:409
  29.7 4.7 %all-to-all-start.1 = ((f32[8,1,128]{2,1,0:T(1,128)}), f32[8,1,128]{2,1,0:T(1,128)S(1)}, u32[]{:S(2)}, u32[]{:S(2)}) async-start(f32[8,1,128]{2,1,0:T(1,128)} %get-tuple-element.17), calls=%async_computation.1 | async-start | bytes 8192 | tf_op jit(solution)/shard_map/all_to_all | solution.py:460
  34.4 0.0 collective-permute-done.below_ref
  34.4 0.0 collective-permute-done.1.above_ref
  34.4 0.5 shard_map.151
  34.9 3.8 %collective-permute-start.2 = (f32[72,128]{1,0:T(8,128)S(1)}, f32[72,128]{1,0:T(8,128)S(1)}, u32[]{:S(2)}, u32[]{:S(2)}) collective-permute-start(f32[72,128]{1,0:T(8,128)S(1)} %get-tuple-element.23), channel_id=1, source_target_pairs={{0,1},{1,2},{2,3},{3,4},{4,5},{5,6},{6,7},{7,8},{8,9},{9,10},{10,1... | collective-permute-start | bytes 110600 | tf_op jit(solution)/shard_map/ppermute | solution.py:409
  38.7 1.3 %collective-permute-start.3 = (f32[72,128]{1,0:T(8,128)S(1)}, f32[72,128]{1,0:T(8,128)S(1)}, u32[]{:S(2)}, u32[]{:S(2)}) collective-permute-start(f32[72,128]{1,0:T(8,128)S(1)} %get-tuple-element.24), channel_id=1, source_target_pairs={{1,0},{2,1},{3,2},{4,3},{5,4},{6,5},{7,6},{8,7},{9,8},{10,9},{11,1... | collective-permute-start | bytes 110600 | tf_op jit(solution)/shard_map/ppermute | solution.py:410
  40.0 0.1 pad_add_fusion.place_ref
  40.7 0.0 all-to-all-done.1.counts_ref
  40.8 4.4 %shard_map.150 = (f32[128,1,6272]{2,1,0:T(1,128)}, s32[8,128]{1,0:T(8,128)S(1)}) custom-call(s32[1]{0:T(128)} %bitcast.here_ref, s32[160]{0:T(256)S(1)} %copy-done.6, f32[8,1,128]{2,1,0:T(1,128)S(1)} %all-to-all-done.1.counts_ref, f32[160,1536]{1,0:T(8,128)S(1)} %get-tuple-element.18.state_ref, f32[160,1536]{1,0:T(8,128)S(1)} %copy-done), custom_call_target="tpu_custom_call" | custom-call | tf_op jit(solution)/shard_map/pallas_call | solution.py:461
  45.1 3.2 %shard_map.152 = (f32[6,64,128]{2,1,0:T(8,128)S(1)}, f32[128,1,6272]{2,1,0:T(1,128)}) custom-call(s32[4]{0:T(128)S(1)} %pad_add_fusion.place_ref, f32[1]{0:T(128)S(6)} %copy.18.load_ref, f32[18,64,128]{2,1,0:T(8,128)S(1)} %get-tuple-element.20.field_ref, f32[72,128]{1,0:T(8,128)S(1)} %collective-permute-done.below_ref, ...), custom_call_target="tpu_custom_call", output_to_operand_aliasing={{1}: (7, {})} | custom-call | flops 200000000 | bytes 2000000 | tf_op jit(solution)/shard_map/pallas_call | solution.py:472
  48.3 11.5 %all-to-all-start.2 = ((f32[128,1,6272]{2,1,0:T(1,128)}), f32[128,1,6272]{2,1,0:T(1,128)S(1)}, u32[]{:S(2)}, u32[]{:S(2)}) async-start(f32[128,1,6272]{2,1,0:T(1,128)} %get-tuple-element.26), calls=%async_computation.2 | async-start | bytes 6422528 | tf_op jit(solution)/shard_map/all_to_all | solution.py:482
  60.4 40.4 %all-to-all-done.2.arrived_ref = f32[128,1,6272]{2,1,0:T(1,128)S(1)} async-done(((f32[128,1,6272]{2,1,0:T(1,128)}), f32[128,1,6272]{2,1,0:T(1,128)S(1)}, u32[]{:S(2)}, u32[]{:S(2)}) %all-to-all-start.2) | async-done | bytes 3211296 | tf_op jit(solution)/shard_map/all_to_all | solution.py:482
  100.8 2.6 %shard_map.153 = (f32[3,64,128]{2,1,0:T(8,128)}, f32[1]{0:T(128)}, f32[80,1536]{1,0:T(8,128)}, f32[80,1536]{1,0:T(8,128)}) custom-call(s32[8,128]{1,0:T(8,128)S(1)} %get-tuple-element.19.plan_ref, f32[1]{0:T(128)S(6)} %copy.18.load_ref, f32[1]{0:T(128)S(6)} %copy.19.radius_ref, f32[128,1,6272]{2,1,0:T(1,128)S(1)} %all-to-all-done.2.arrived_ref, ...), custom_call_target="tpu_custom_call" | custom-call | tf_op jit(solution)/shard_map/pallas_call | solution.py:483
  (16 shorter events, 0.0 us)
Async XLA Ops:
  0.6 0.7 copy-start.5
  1.3 8.9 %copy-start.1 = (f32[3,64,128]{2,1,0:T(8,128)S(1)}, f32[3,64,128]{2,1,0:T(8,128)}, u32[]{:S(2)}) copy-start(f32[3,64,128]{2,1,0:T(8,128)} %jump_ref.3) | copy-start | bytes 294916
  1.3 8.9 %copy-start.6 = (s32[160]{0:T(256)S(1)}, s32[160]{0:T(256)}, u32[]{:S(2)}) copy-start(s32[160]{0:T(256)} %steps_ref.1) | copy-start | bytes 1924
  1.3 8.9 %copy-start.7 = (s32[160]{0:T(256)S(1)}, s32[160]{0:T(256)}, u32[]{:S(2)}) copy-start(s32[160]{0:T(256)} %param.23) | copy-start | bytes 1924
  1.3 8.9 %copy-start.8 = (f32[3,1536]{1,0:T(4,128)S(1)}, f32[3,1536]{1,0:T(4,128)}, u32[]{:S(2)}) copy-start(f32[3,1536]{1,0:T(4,128)} %coupling_ref.1) | copy-start | bytes 55300
  2.0 22.6 %all-to-all-start = ((f32[16,1,128]{2,1,0:T(1,128)}), f32[16,1,128]{2,1,0:T(1,128)S(1)}, u32[]{:S(2)}, u32[]{:S(2)}) async-start(f32[16,1,128]{2,1,0:T(1,128)} %shard_map.148), calls=%async_computation | async-start | bytes 16384 | tf_op jit(solution)/shard_map/all_to_all | solution.py:431
  10.2 14.4 %copy-start.2 = (f32[3,64,128]{2,1,0:T(8,128)S(1)}, f32[3,64,128]{2,1,0:T(8,128)}, u32[]{:S(2)}) copy-start(f32[3,64,128]{2,1,0:T(8,128)} %external_ref.1) | copy-start | bytes 294916
  10.2 14.4 %copy-start.3 = (s32[2,64,128]{2,1,0:T(8,128)S(1)}, s32[2,64,128]{2,1,0:T(8,128)}, u32[]{:S(2)}) copy-start(s32[2,64,128]{2,1,0:T(8,128)} %mask_ref.1) | copy-start | bytes 196612
  10.2 14.4 %copy-start.4 = (f32[64,128]{1,0:T(8,128)S(1)}, f32[64,128]{1,0:T(8,128)}, u32[]{:S(2)}) copy-start(f32[64,128]{1,0:T(8,128)} %cohesive_ref.1) | copy-start | bytes 98308
  10.2 30.5 %copy-start = (f32[160,1536]{1,0:T(8,128)S(1)}, f32[160,1536]{1,0:T(8,128)}, u32[]{:S(2)}) copy-start(f32[160,1536]{1,0:T(8,128)} %history_ref.1) | copy-start | bytes 2949124
  25.3 9.1 %collective-permute-start = (f32[72,128]{1,0:T(8,128)S(1)}, f32[72,128]{1,0:T(8,128)S(1)}, u32[]{:S(2)}, u32[]{:S(2)}) collective-permute-start(f32[72,128]{1,0:T(8,128)S(1)} %get-tuple-element.21), channel_id=1, source_target_pairs={{16,0},{32,16},{48,32},{64,48},{80,64},{96,80},{112,96},{17,1},{33... | collective-permute-start | bytes 110600 | tf_op jit(solution)/shard_map/ppermute | solution.py:410
  26.6 7.8 %collective-permute-start.1 = (f32[72,128]{1,0:T(8,128)S(1)}, f32[72,128]{1,0:T(8,128)S(1)}, u32[]{:S(2)}, u32[]{:S(2)}) collective-permute-start(f32[72,128]{1,0:T(8,128)S(1)} %get-tuple-element.22), channel_id=1, source_target_pairs={{0,16},{16,32},{32,48},{48,64},{64,80},{80,96},{96,112},{1,17},{17... | collective-permute-start | bytes 110600 | tf_op jit(solution)/shard_map/ppermute | solution.py:409
  29.7 11.1 %all-to-all-start.1 = ((f32[8,1,128]{2,1,0:T(1,128)}), f32[8,1,128]{2,1,0:T(1,128)S(1)}, u32[]{:S(2)}, u32[]{:S(2)}) async-start(f32[8,1,128]{2,1,0:T(1,128)} %get-tuple-element.17), calls=%async_computation.1 | async-start | bytes 8192 | tf_op jit(solution)/shard_map/all_to_all | solution.py:460
  34.9 10.2 %collective-permute-start.2 = (f32[72,128]{1,0:T(8,128)S(1)}, f32[72,128]{1,0:T(8,128)S(1)}, u32[]{:S(2)}, u32[]{:S(2)}) collective-permute-start(f32[72,128]{1,0:T(8,128)S(1)} %get-tuple-element.23), channel_id=1, source_target_pairs={{0,1},{1,2},{2,3},{3,4},{4,5},{5,6},{6,7},{7,8},{8,9},{9,10},{10,1... | collective-permute-start | bytes 110600 | tf_op jit(solution)/shard_map/ppermute | solution.py:409
  38.7 6.4 %collective-permute-start.3 = (f32[72,128]{1,0:T(8,128)S(1)}, f32[72,128]{1,0:T(8,128)S(1)}, u32[]{:S(2)}, u32[]{:S(2)}) collective-permute-start(f32[72,128]{1,0:T(8,128)S(1)} %get-tuple-element.24), channel_id=1, source_target_pairs={{1,0},{2,1},{3,2},{4,3},{5,4},{6,5},{7,6},{8,7},{9,8},{10,9},{11,1... | collective-permute-start | bytes 110600 | tf_op jit(solution)/shard_map/ppermute | solution.py:410
  48.3 52.5 %all-to-all-start.2 = ((f32[128,1,6272]{2,1,0:T(1,128)}), f32[128,1,6272]{2,1,0:T(1,128)S(1)}, u32[]{:S(2)}, u32[]{:S(2)}) async-start(f32[128,1,6272]{2,1,0:T(1,128)} %get-tuple-element.26), calls=%async_computation.2 | async-start | bytes 6422528 | tf_op jit(solution)/shard_map/all_to_all | solution.py:482

commit v6 on v4

--- a/solution.py
+++ b/solution.py
@@ -72,10 +72,11 @@
 
 
 def newton_kernel(
-    ids_ref, steps_ref, jump_ref, stiffness_hbm, coupling_ref, old_state_hbm, history_hbm,
+    ids_ref, steps_ref, jump_ref, stiffness_hbm, coupling_ref, old_state_hbm, history_hbm, after_ref,
     state_ref, grid_ref,
     stiffness_ref, damage_ref, load_ref, diagonal_ref, rounded_ref, sems,
 ):
+    del after_ref
     width = 256
     cuts = [slice(t * width, (t + 1) * width) for t in range(stiffness_hbm.shape[1] // width)]
     copies = [
@@ -84,7 +85,6 @@
     ]
     get_history = pltpu.make_async_copy(history_hbm, damage_ref, sems.at[len(cuts)])
     get_state = pltpu.make_async_copy(old_state_hbm, state_ref, sems.at[len(cuts) + 1])
-    ahead = 3
     for copy in (get_history, get_state):
         copy.start()
     slots, cells = state_ref.shape
@@ -114,9 +114,9 @@
     load_ref[...] = (
         drive[0] * coupling_ref[0:1, :] + drive[1] * coupling_ref[1:2, :] + drive[2] * coupling_ref[2:3, :]
     )
+    for copy in copies:
+        copy.start()
     get_history.wait()
-    for copy in copies[:ahead]:
-        copy.start()
     damage_ref[...] = jnp.exp(-damage_ref[...])
     get_state.wait()
     rounded_ref[0] = state_ref[...].astype(BF16)
@@ -129,8 +129,6 @@
         for t, part in enumerate(cuts):
             if waiting:
                 copies[t].wait()
-                if t + ahead < len(copies):
-                    copies[t + ahead].start()
                 block = stiffness_ref[part, part].astype(F32)
                 diagonal_ref[:, part] = jnp.sum(jnp.where(eye, block, 0.0), axis=0, keepdims=True)
             force = jnp.dot(rounded, stiffness_ref[:, part], preferred_element_type=F32)
@@ -421,11 +419,10 @@
     steps_row = newton_steps.reshape(1, slots)
 
     mine = call(count_kernel, shape(devices, 1, LANES), [VMEM], VMEM, 2, cost=LONG)(steps_row)
-    counts = lax.all_to_all(mine, ROWS_COLS, 0, 0, tiled=True).reshape(devices, LANES)
     state, grid = call(
         newton_kernel,
         (shape(slots, cells), shape(FIELDS - INPUT_FIELDS, rows, lanes)),
-        [VMEM] * 3 + [HBM, VMEM, HBM, HBM],
+        [VMEM] * 3 + [HBM, VMEM, HBM, HBM, HBM],
         (VMEM, VMEM),
         NEWTON_MIB,
         scratch=(
@@ -441,7 +438,7 @@
             transcendentals=2 * MAX_STEPS * slots * cells,
             bytes_accessed=2 * cells * cells + 12 * slots * cells,
         ),
-    )(ids_row, steps_row, jump, stiffness, coupling, old_state, old_history)
+    )(ids_row, steps_row, jump, stiffness, coupling, old_state, old_history, mine)
     fields, first, last = call(
         fields_kernel,
         (shape(FIELDS, rows, lanes), shape(edge, lanes), shape(edge, lanes)),
@@ -450,6 +447,7 @@
         4,
     )(ids_row, steps_row, jump, external, cohesive, bond_mask, grid)
     below, above = swap(first, last, "row")
+    counts = lax.all_to_all(mine, ROWS_COLS, 0, 0, tiled=True).reshape(devices, LANES)
     packed, plan = call(
         pack_kernel,
         (packed_shape, shape(8, LANES, dtype=jnp.int32)),

time: 104 us -> 102 us (0.981)
  local copies, waits for them, and re-layouts: 3 us -> 0.85 us
    unnamed x18, local copies, waits for them, and re-layouts: 3 us -> 0.85 us
where the time goes in v6:
time: 102 us; the launch traced here: 101 us
  waiting for transfers between devices  44.5 us (44%)
  starting transfers between devices  27.9 us (27%)
  Pallas kernels  25.7 us (25%)
  between operations  2.09 us (2%)
    all_to_all x1, waiting for transfers between devices, on_device(): arrived = lax.all_to_all(packed, ROWS_COLS, 0, 0, tiled=True)  40.4 us
    pallas_call x1, Pallas kernels, on_device(): call(newton_kernel, (shape(slots, cells), shape(FIELDS - INPUT_FIELDS, ro...  14.4 us
    all_to_all x1, starting transfers between devices, on_device(): lax.all_to_all(mine, ROWS_COLS, 0, 0, tiled=True).reshape(devices, LANES)  11.9 us
    all_to_all x1, starting transfers between devices, on_device(): arrived = lax.all_to_all(packed, ROWS_COLS, 0, 0, tiled=True)  7.55 us
    ppermute x2, starting transfers between devices, swap(): above = lax.ppermute(last, axis, up)  5.9 us
    pallas_call x1, Pallas kernels, on_device(): call(pack_kernel, (packed_shape, shape(8, LANES, dtype=jnp.int32)), [SMEM...  4.15 us
    all_to_all x1, waiting for transfers between devices, on_device(): lax.all_to_all(mine, ROWS_COLS, 0, 0, tiled=True).reshape(devices, LANES)  4.03 us
    pallas_call x1, Pallas kernels, on_device(): call(macro_kernel, (shape(6, rows, lanes), packed_shape), [SMEM, SMEM] +...  3.14 us
  transfers between devices with their start and end apart: 6, of which 2 were waited for; matrix products, arithmetic and copies ran while one was open for 0% of the time, Pallas kernels for 5%

profile of v6, /device:TPU:0, one launch (start us, length us, event | category | flops | bytes accessed | tf_op | source)
XLA Modules:
  0.0 101.0 jit_solution(8876512758277272076)
XLA Ops:
  0.6 0.7 copy-done.5
  1.3 0.7 shard_map.147.after_ref
  2.1 0.1 copy-done.1
  2.2 0.0 copy-start.3
  2.2 0.0 copy-start.4
  2.2 0.0 copy-start
  2.3 14.4 %shard_map.148 = (f32[160,1536]{1,0:T(8,128)S(1)}, f32[9,64,128]{2,1,0:T(8,128)S(1)}) custom-call(s32[1,160]{1,0:T(1,128)S(1)} %bitcast.10, s32[1,160]{1,0:T(1,128)S(1)} %bitcast.8, f32[3,64,128]{2,1,0:T(8,128)S(1)} %copy-done.1, bf16[1536,1536]{1,0:T(8,128)(2,1)} %stiffness_hbm.1, f32[3,1536]{1,0:T(4,128)S(1)} %copy-done.8, f32[160,1536]{1,0:T(8,128)} %old_state_hbm.1, ...), custom_call_target="tpu_custom_call" | custom-call | flops 6794772480 | bytes 7667712 | tf_op jit(solution)/shard_map/pallas_call | solution.py:422
  16.7 0.2 shard_map.150
  16.9 1.3 %collective-permute-start = (f32[72,128]{1,0:T(8,128)S(1)}, f32[72,128]{1,0:T(8,128)S(1)}, u32[]{:S(2)}, u32[]{:S(2)}) collective-permute-start(f32[72,128]{1,0:T(8,128)S(1)} %get-tuple-element.19), channel_id=1, source_target_pairs={{16,0},{32,16},{48,32},{64,48},{80,64},{96,80},{112,96},{17,1},{33... | collective-permute-start | bytes 110600 | tf_op jit(solution)/shard_map/ppermute | solution.py:401
  18.2 3.0 %collective-permute-start.1 = (f32[72,128]{1,0:T(8,128)S(1)}, f32[72,128]{1,0:T(8,128)S(1)}, u32[]{:S(2)}, u32[]{:S(2)}) collective-permute-start(f32[72,128]{1,0:T(8,128)S(1)} %get-tuple-element.20), channel_id=1, source_target_pairs={{0,16},{16,32},{32,48},{48,64},{64,80},{80,96},{96,112},{1,17},{17... | collective-permute-start | bytes 110600 | tf_op jit(solution)/shard_map/ppermute | solution.py:400
  21.2 11.9 %all-to-all-start = ((f32[128,1,128]{2,1,0:T(1,128)}), f32[128,1,128]{2,1,0:T(1,128)S(1)}, u32[]{:S(2)}, u32[]{:S(2)}) async-start(f32[128,1,128]{2,1,0:T(1,128)} %shard_map.147.after_ref), calls=%async_computation | async-start | bytes 131072 | tf_op jit(solution)/shard_map/all_to_all | solution.py:450
  33.1 0.0 collective-permute-done.below_ref
  33.1 0.0 collective-permute-done.1.above_ref
  33.1 0.5 shard_map.151
  33.6 2.9 %collective-permute-start.2 = (f32[72,128]{1,0:T(8,128)S(1)}, f32[72,128]{1,0:T(8,128)S(1)}, u32[]{:S(2)}, u32[]{:S(2)}) collective-permute-start(f32[72,128]{1,0:T(8,128)S(1)} %get-tuple-element.21), channel_id=1, source_target_pairs={{0,1},{1,2},{2,3},{3,4},{4,5},{5,6},{6,7},{7,8},{8,9},{9,10},{10,1... | collective-permute-start | bytes 110600 | tf_op jit(solution)/shard_map/ppermute | solution.py:400
  36.4 1.3 %collective-permute-start.3 = (f32[72,128]{1,0:T(8,128)S(1)}, f32[72,128]{1,0:T(8,128)S(1)}, u32[]{:S(2)}, u32[]{:S(2)}) collective-permute-start(f32[72,128]{1,0:T(8,128)S(1)} %get-tuple-element.22), channel_id=1, source_target_pairs={{1,0},{2,1},{3,2},{4,3},{5,4},{6,5},{7,6},{8,7},{9,8},{10,9},{11,1... | collective-permute-start | bytes 110600 | tf_op jit(solution)/shard_map/ppermute | solution.py:401
  37.7 0.1 pad_add_fusion.place_ref
  38.5 4.0 %all-to-all-done = f32[128,1,128]{2,1,0:T(1,128)S(1)} async-done(((f32[128,1,128]{2,1,0:T(1,128)}), f32[128,1,128]{2,1,0:T(1,128)S(1)}, u32[]{:S(2)}, u32[]{:S(2)}) %all-to-all-start) | async-done | bytes 65568 | tf_op jit(solution)/shard_map/all_to_all | solution.py:450
  42.5 4.1 %shard_map.149 = (f32[128,1,6272]{2,1,0:T(1,128)}, s32[8,128]{1,0:T(8,128)S(1)}) custom-call(s32[1]{0:T(128)} %bitcast.here_ref, s32[160]{0:T(256)S(1)} %copy-done.6, f32[128,128]{1,0:T(8,128)S(1)} %bitcast.6, f32[160,1536]{1,0:T(8,128)S(1)} %get-tuple-element.15.state_ref, f32[160,1536]{1,0:T(8,128)S(1)} %copy-done), custom_call_target="tpu_custom_call" | custom-call | tf_op jit(solution)/shard_map/pallas_call | solution.py:451
  46.7 0.0 collective-permute-done.3.right_ref
  46.7 3.1 %shard_map.152 = (f32[6,64,128]{2,1,0:T(8,128)S(1)}, f32[128,1,6272]{2,1,0:T(1,128)}) custom-call(s32[4]{0:T(128)S(1)} %pad_add_fusion.place_ref, f32[1]{0:T(128)S(6)} %copy.19.load_ref, f32[18,64,128]{2,1,0:T(8,128)S(1)} %get-tuple-element.18.field_ref, f32[72,128]{1,0:T(8,128)S(1)} %collective-permute-done.below_ref, ...), custom_call_target="tpu_custom_call", output_to_operand_aliasing={{1}: (7, {})} | custom-call | flops 200000000 | bytes 2000000 | tf_op jit(solution)/shard_map/pallas_call | solution.py:462
  49.8 7.5 %all-to-all-start.1 = ((f32[128,1,6272]{2,1,0:T(1,128)}), f32[128,1,6272]{2,1,0:T(1,128)S(1)}, u32[]{:S(2)}, u32[]{:S(2)}) async-start(f32[128,1,6272]{2,1,0:T(1,128)} %get-tuple-element.24), calls=%async_computation.1 | async-start | bytes 6422528 | tf_op jit(solution)/shard_map/all_to_all | solution.py:472
  58.0 40.4 %all-to-all-done.1.arrived_ref = f32[128,1,6272]{2,1,0:T(1,128)S(1)} async-done(((f32[128,1,6272]{2,1,0:T(1,128)}), f32[128,1,6272]{2,1,0:T(1,128)S(1)}, u32[]{:S(2)}, u32[]{:S(2)}) %all-to-all-start.1) | async-done | bytes 3211296 | tf_op jit(solution)/shard_map/all_to_all | solution.py:472
  98.4 2.6 %shard_map.153 = (f32[3,64,128]{2,1,0:T(8,128)}, f32[1]{0:T(128)}, f32[80,1536]{1,0:T(8,128)}, f32[80,1536]{1,0:T(8,128)}) custom-call(s32[8,128]{1,0:T(8,128)S(1)} %get-tuple-element.16.plan_ref, f32[1]{0:T(128)S(6)} %copy.19.load_ref, f32[1]{0:T(128)S(6)} %copy.20.radius_ref, f32[128,1,6272]{2,1,0:T(1,128)S(1)} %all-to-all-done.1.arrived_ref, ...), custom_call_target="tpu_custom_call" | custom-call | tf_op jit(solution)/shard_map/pallas_call | solution.py:473
  (14 shorter events, 0.0 us)
Async XLA Ops:
  0.6 0.7 copy-start.5
  1.3 0.9 copy-start.1
  1.3 0.9 copy-start.6
  1.3 0.9 copy-start.7
  1.3 0.9 copy-start.8
  2.2 14.5 %copy-start.2 = (f32[3,64,128]{2,1,0:T(8,128)S(1)}, f32[3,64,128]{2,1,0:T(8,128)}, u32[]{:S(2)}) copy-start(f32[3,64,128]{2,1,0:T(8,128)} %external_ref.1) | copy-start | bytes 294916
  2.2 14.5 %copy-start.3 = (s32[2,64,128]{2,1,0:T(8,128)S(1)}, s32[2,64,128]{2,1,0:T(8,128)}, u32[]{:S(2)}) copy-start(s32[2,64,128]{2,1,0:T(8,128)} %mask_ref.1) | copy-start | bytes 196612
  2.2 14.5 %copy-start.4 = (f32[64,128]{1,0:T(8,128)S(1)}, f32[64,128]{1,0:T(8,128)}, u32[]{:S(2)}) copy-start(f32[64,128]{1,0:T(8,128)} %cohesive_ref.1) | copy-start | bytes 98308
  2.2 40.3 %copy-start = (f32[160,1536]{1,0:T(8,128)S(1)}, f32[160,1536]{1,0:T(8,128)}, u32[]{:S(2)}) copy-start(f32[160,1536]{1,0:T(8,128)} %history_ref.1) | copy-start | bytes 2949124
  16.9 16.2 %collective-permute-start = (f32[72,128]{1,0:T(8,128)S(1)}, f32[72,128]{1,0:T(8,128)S(1)}, u32[]{:S(2)}, u32[]{:S(2)}) collective-permute-start(f32[72,128]{1,0:T(8,128)S(1)} %get-tuple-element.19), channel_id=1, source_target_pairs={{16,0},{32,16},{48,32},{64,48},{80,64},{96,80},{112,96},{17,1},{33... | collective-permute-start | bytes 110600 | tf_op jit(solution)/shard_map/ppermute | solution.py:401
  18.2 14.9 %collective-permute-start.1 = (f32[72,128]{1,0:T(8,128)S(1)}, f32[72,128]{1,0:T(8,128)S(1)}, u32[]{:S(2)}, u32[]{:S(2)}) collective-permute-start(f32[72,128]{1,0:T(8,128)S(1)} %get-tuple-element.20), channel_id=1, source_target_pairs={{0,16},{16,32},{32,48},{48,64},{64,80},{80,96},{96,112},{1,17},{17... | collective-permute-start | bytes 110600 | tf_op jit(solution)/shard_map/ppermute | solution.py:400
  21.2 21.3 %all-to-all-start = ((f32[128,1,128]{2,1,0:T(1,128)}), f32[128,1,128]{2,1,0:T(1,128)S(1)}, u32[]{:S(2)}, u32[]{:S(2)}) async-start(f32[128,1,128]{2,1,0:T(1,128)} %shard_map.147.after_ref), calls=%async_computation | async-start | bytes 131072 | tf_op jit(solution)/shard_map/all_to_all | solution.py:450
  33.6 13.1 %collective-permute-start.2 = (f32[72,128]{1,0:T(8,128)S(1)}, f32[72,128]{1,0:T(8,128)S(1)}, u32[]{:S(2)}, u32[]{:S(2)}) collective-permute-start(f32[72,128]{1,0:T(8,128)S(1)} %get-tuple-element.21), channel_id=1, source_target_pairs={{0,1},{1,2},{2,3},{3,4},{4,5},{5,6},{6,7},{7,8},{8,9},{9,10},{10,1... | collective-permute-start | bytes 110600 | tf_op jit(solution)/shard_map/ppermute | solution.py:400
  36.4 10.2 %collective-permute-start.3 = (f32[72,128]{1,0:T(8,128)S(1)}, f32[72,128]{1,0:T(8,128)S(1)}, u32[]{:S(2)}, u32[]{:S(2)}) collective-permute-start(f32[72,128]{1,0:T(8,128)S(1)} %get-tuple-element.22), channel_id=1, source_target_pairs={{1,0},{2,1},{3,2},{4,3},{5,4},{6,5},{7,6},{8,7},{9,8},{10,9},{11,1... | collective-permute-start | bytes 110600 | tf_op jit(solution)/shard_map/ppermute | solution.py:401
  49.8 48.6 %all-to-all-start.1 = ((f32[128,1,6272]{2,1,0:T(1,128)}), f32[128,1,6272]{2,1,0:T(1,128)S(1)}, u32[]{:S(2)}, u32[]{:S(2)}) async-start(f32[128,1,6272]{2,1,0:T(1,128)} %get-tuple-element.24), calls=%async_computation.1 | async-start | bytes 6422528 | tf_op jit(solution)/shard_map/all_to_all | solution.py:472

commit v7 on v6

--- a/solution.py
+++ b/solution.py
@@ -72,11 +72,11 @@
 
 
 def newton_kernel(
-    ids_ref, steps_ref, jump_ref, stiffness_hbm, coupling_ref, old_state_hbm, history_hbm, after_ref,
-    state_ref, grid_ref,
+    ids_ref, steps_ref, jump_ref, stiffness_hbm, coupling_ref, old_state_hbm, history_hbm, count_in,
+    state_ref, grid_ref, count_out,
     stiffness_ref, damage_ref, load_ref, diagonal_ref, rounded_ref, sems,
 ):
-    del after_ref
+    del count_in, count_out
     width = 256
     cuts = [slice(t * width, (t + 1) * width) for t in range(stiffness_hbm.shape[1] // width)]
     copies = [
@@ -419,11 +419,11 @@
     steps_row = newton_steps.reshape(1, slots)
 
     mine = call(count_kernel, shape(devices, 1, LANES), [VMEM], VMEM, 2, cost=LONG)(steps_row)
-    state, grid = call(
+    state, grid, mine = call(
         newton_kernel,
-        (shape(slots, cells), shape(FIELDS - INPUT_FIELDS, rows, lanes)),
+        (shape(slots, cells), shape(FIELDS - INPUT_FIELDS, rows, lanes), shape(devices, 1, LANES)),
         [VMEM] * 3 + [HBM, VMEM, HBM, HBM, HBM],
-        (VMEM, VMEM),
+        (VMEM, VMEM, HBM),
         NEWTON_MIB,
         scratch=(
             pltpu.VMEM(stiffness.shape, BF16),
@@ -438,6 +438,7 @@
             transcendentals=2 * MAX_STEPS * slots * cells,
             bytes_accessed=2 * cells * cells + 12 * slots * cells,
         ),
+        aliases={7: 2},
     )(ids_row, steps_row, jump, stiffness, coupling, old_state, old_history, mine)
     fields, first, last = call(
         fields_kernel,

time: 102 us -> 102 us (level)
  no operation moved by 1% of the time
where the time goes in v7:
time: 102 us; the launch traced here: 101 us
  waiting for transfers between devices  44.5 us (44%)
  starting transfers between devices  27.9 us (27%)
  Pallas kernels  25.7 us (25%)
  between operations  2.09 us (2%)
    all_to_all x1, waiting for transfers between devices, on_device(): arrived = lax.all_to_all(packed, ROWS_COLS, 0, 0, tiled=True)  40.4 us
    pallas_call x1, Pallas kernels, on_device(): call(newton_kernel, (shape(slots, cells), shape(FIELDS - INPUT_FIELDS, ro...  14.4 us
    all_to_all x1, starting transfers between devices, on_device(): lax.all_to_all(mine, ROWS_COLS, 0, 0, tiled=True).reshape(devices, LANES)  11.9 us
    all_to_all x1, starting transfers between devices, on_device(): arrived = lax.all_to_all(packed, ROWS_COLS, 0, 0, tiled=True)  7.55 us
    ppermute x2, starting transfers between devices, swap(): above = lax.ppermute(last, axis, up)  5.9 us
    pallas_call x1, Pallas kernels, on_device(): call(pack_kernel, (packed_shape, shape(8, LANES, dtype=jnp.int32)), [SMEM...  4.15 us
    all_to_all x1, waiting for transfers between devices, on_device(): lax.all_to_all(mine, ROWS_COLS, 0, 0, tiled=True).reshape(devices, LANES)  4.03 us
    pallas_call x1, Pallas kernels, on_device(): call(macro_kernel, (shape(6, rows, lanes), packed_shape), [SMEM, SMEM] +...  3.14 us
  transfers between devices with their start and end apart: 6, of which 2 were waited for; matrix products, arithmetic and copies ran while one was open for 0% of the time, Pallas kernels for 5%

profile of v7, /device:TPU:0, one launch (start us, length us, event | category | flops | bytes accessed | tf_op | source)
XLA Modules:
  0.0 101.0 jit_solution(16343435630894849170)
XLA Ops:
  0.6 0.7 copy-done.5
  1.3 0.7 shard_map.147.count_in
  2.1 0.1 copy-done.1
  2.2 0.0 copy-start.3
  2.2 0.0 copy-start.4
  2.2 0.0 copy-start
  2.3 14.4 %shard_map.148 = (f32[160,1536]{1,0:T(8,128)S(1)}, f32[9,64,128]{2,1,0:T(8,128)S(1)}, f32[128,1,128]{2,1,0:T(1,128)}) custom-call(s32[1,160]{1,0:T(1,128)S(1)} %bitcast.10, s32[1,160]{1,0:T(1,128)S(1)} %bitcast.8, f32[3,64,128]{2,1,0:T(8,128)S(1)} %copy-done.1, bf16[1536,1536]{1,0:T(8,128)(2,1)} %stiffness_hbm.1, ...), custom_call_target="tpu_custom_call", output_to_operand_aliasing={{2}: (7, {})} | custom-call | flops 6794772480 | bytes 7667712 | tf_op jit(solution)/shard_map/pallas_call | solution.py:422
  16.7 0.2 shard_map.150
  16.9 1.3 %collective-permute-start = (f32[72,128]{1,0:T(8,128)S(1)}, f32[72,128]{1,0:T(8,128)S(1)}, u32[]{:S(2)}, u32[]{:S(2)}) collective-permute-start(f32[72,128]{1,0:T(8,128)S(1)} %get-tuple-element.21), channel_id=1, source_target_pairs={{16,0},{32,16},{48,32},{64,48},{80,64},{96,80},{112,96},{17,1},{33... | collective-permute-start | bytes 110600 | tf_op jit(solution)/shard_map/ppermute | solution.py:401
  18.2 3.0 %collective-permute-start.1 = (f32[72,128]{1,0:T(8,128)S(1)}, f32[72,128]{1,0:T(8,128)S(1)}, u32[]{:S(2)}, u32[]{:S(2)}) collective-permute-start(f32[72,128]{1,0:T(8,128)S(1)} %get-tuple-element.22), channel_id=1, source_target_pairs={{0,16},{16,32},{32,48},{48,64},{64,80},{80,96},{96,112},{1,17},{17... | collective-permute-start | bytes 110600 | tf_op jit(solution)/shard_map/ppermute | solution.py:400
  21.2 11.9 %all-to-all-start = ((f32[128,1,128]{2,1,0:T(1,128)}), f32[128,1,128]{2,1,0:T(1,128)S(1)}, u32[]{:S(2)}, u32[]{:S(2)}) async-start(f32[128,1,128]{2,1,0:T(1,128)} %get-tuple-element.16), calls=%async_computation | async-start | bytes 131072 | tf_op jit(solution)/shard_map/all_to_all | solution.py:451
  33.1 0.0 collective-permute-done.below_ref
  33.1 0.0 collective-permute-done.1.above_ref
  33.1 0.5 shard_map.151
  33.6 2.9 %collective-permute-start.2 = (f32[72,128]{1,0:T(8,128)S(1)}, f32[72,128]{1,0:T(8,128)S(1)}, u32[]{:S(2)}, u32[]{:S(2)}) collective-permute-start(f32[72,128]{1,0:T(8,128)S(1)} %get-tuple-element.23), channel_id=1, source_target_pairs={{0,1},{1,2},{2,3},{3,4},{4,5},{5,6},{6,7},{7,8},{8,9},{9,10},{10,1... | collective-permute-start | bytes 110600 | tf_op jit(solution)/shard_map/ppermute | solution.py:400
  36.4 1.3 %collective-permute-start.3 = (f32[72,128]{1,0:T(8,128)S(1)}, f32[72,128]{1,0:T(8,128)S(1)}, u32[]{:S(2)}, u32[]{:S(2)}) collective-permute-start(f32[72,128]{1,0:T(8,128)S(1)} %get-tuple-element.24), channel_id=1, source_target_pairs={{1,0},{2,1},{3,2},{4,3},{5,4},{6,5},{7,6},{8,7},{9,8},{10,9},{11,1... | collective-permute-start | bytes 110600 | tf_op jit(solution)/shard_map/ppermute | solution.py:401
  37.7 0.1 pad_add_fusion.place_ref
  38.5 4.0 %all-to-all-done = f32[128,1,128]{2,1,0:T(1,128)S(1)} async-done(((f32[128,1,128]{2,1,0:T(1,128)}), f32[128,1,128]{2,1,0:T(1,128)S(1)}, u32[]{:S(2)}, u32[]{:S(2)}) %all-to-all-start) | async-done | bytes 65568 | tf_op jit(solution)/shard_map/all_to_all | solution.py:451
  42.5 4.1 %shard_map.149 = (f32[128,1,6272]{2,1,0:T(1,128)}, s32[8,128]{1,0:T(8,128)S(1)}) custom-call(s32[1]{0:T(128)} %bitcast.here_ref, s32[160]{0:T(256)S(1)} %copy-done.6, f32[128,128]{1,0:T(8,128)S(1)} %bitcast.6, f32[160,1536]{1,0:T(8,128)S(1)} %get-tuple-element.17.state_ref, f32[160,1536]{1,0:T(8,128)S(1)} %copy-done), custom_call_target="tpu_custom_call" | custom-call | tf_op jit(solution)/shard_map/pallas_call | solution.py:452
  46.7 0.0 collective-permute-done.3.right_ref
  46.7 3.1 %shard_map.152 = (f32[6,64,128]{2,1,0:T(8,128)S(1)}, f32[128,1,6272]{2,1,0:T(1,128)}) custom-call(s32[4]{0:T(128)S(1)} %pad_add_fusion.place_ref, f32[1]{0:T(128)S(6)} %copy.21.load_ref, f32[18,64,128]{2,1,0:T(8,128)S(1)} %get-tuple-element.20.field_ref, f32[72,128]{1,0:T(8,128)S(1)} %collective-permute-done.below_ref, ...), custom_call_target="tpu_custom_call", output_to_operand_aliasing={{1}: (7, {})} | custom-call | flops 200000000 | bytes 2000000 | tf_op jit(solution)/shard_map/pallas_call | solution.py:463
  49.8 7.5 %all-to-all-start.1 = ((f32[128,1,6272]{2,1,0:T(1,128)}), f32[128,1,6272]{2,1,0:T(1,128)S(1)}, u32[]{:S(2)}, u32[]{:S(2)}) async-start(f32[128,1,6272]{2,1,0:T(1,128)} %get-tuple-element.26), calls=%async_computation.1 | async-start | bytes 6422528 | tf_op jit(solution)/shard_map/all_to_all | solution.py:473
  58.0 40.4 %all-to-all-done.1.arrived_ref = f32[128,1,6272]{2,1,0:T(1,128)S(1)} async-done(((f32[128,1,6272]{2,1,0:T(1,128)}), f32[128,1,6272]{2,1,0:T(1,128)S(1)}, u32[]{:S(2)}, u32[]{:S(2)}) %all-to-all-start.1) | async-done | bytes 3211296 | tf_op jit(solution)/shard_map/all_to_all | solution.py:473
  98.4 2.6 %shard_map.153 = (f32[3,64,128]{2,1,0:T(8,128)}, f32[1]{0:T(128)}, f32[80,1536]{1,0:T(8,128)}, f32[80,1536]{1,0:T(8,128)}) custom-call(s32[8,128]{1,0:T(8,128)S(1)} %get-tuple-element.18.plan_ref, f32[1]{0:T(128)S(6)} %copy.21.load_ref, f32[1]{0:T(128)S(6)} %copy.22.radius_ref, f32[128,1,6272]{2,1,0:T(1,128)S(1)} %all-to-all-done.1.arrived_ref, ...), custom_call_target="tpu_custom_call" | custom-call | tf_op jit(solution)/shard_map/pallas_call | solution.py:474
  (14 shorter events, 0.0 us)
Async XLA Ops:
  0.6 0.7 copy-start.5
  1.3 0.9 copy-start.1
  1.3 0.9 copy-start.6
  1.3 0.9 copy-start.7
  1.3 0.9 copy-start.8
  2.2 14.5 %copy-start.2 = (f32[3,64,128]{2,1,0:T(8,128)S(1)}, f32[3,64,128]{2,1,0:T(8,128)}, u32[]{:S(2)}) copy-start(f32[3,64,128]{2,1,0:T(8,128)} %external_ref.1) | copy-start | bytes 294916
  2.2 14.5 %copy-start.3 = (s32[2,64,128]{2,1,0:T(8,128)S(1)}, s32[2,64,128]{2,1,0:T(8,128)}, u32[]{:S(2)}) copy-start(s32[2,64,128]{2,1,0:T(8,128)} %mask_ref.1) | copy-start | bytes 196612
  2.2 14.5 %copy-start.4 = (f32[64,128]{1,0:T(8,128)S(1)}, f32[64,128]{1,0:T(8,128)}, u32[]{:S(2)}) copy-start(f32[64,128]{1,0:T(8,128)} %cohesive_ref.1) | copy-start | bytes 98308
  2.2 40.3 %copy-start = (f32[160,1536]{1,0:T(8,128)S(1)}, f32[160,1536]{1,0:T(8,128)}, u32[]{:S(2)}) copy-start(f32[160,1536]{1,0:T(8,128)} %history_ref.1) | copy-start | bytes 2949124
  16.9 16.2 %collective-permute-start = (f32[72,128]{1,0:T(8,128)S(1)}, f32[72,128]{1,0:T(8,128)S(1)}, u32[]{:S(2)}, u32[]{:S(2)}) collective-permute-start(f32[72,128]{1,0:T(8,128)S(1)} %get-tuple-element.21), channel_id=1, source_target_pairs={{16,0},{32,16},{48,32},{64,48},{80,64},{96,80},{112,96},{17,1},{33... | collective-permute-start | bytes 110600 | tf_op jit(solution)/shard_map/ppermute | solution.py:401
  18.2 14.9 %collective-permute-start.1 = (f32[72,128]{1,0:T(8,128)S(1)}, f32[72,128]{1,0:T(8,128)S(1)}, u32[]{:S(2)}, u32[]{:S(2)}) collective-permute-start(f32[72,128]{1,0:T(8,128)S(1)} %get-tuple-element.22), channel_id=1, source_target_pairs={{0,16},{16,32},{32,48},{48,64},{64,80},{80,96},{96,112},{1,17},{17... | collective-permute-start | bytes 110600 | tf_op jit(solution)/shard_map/ppermute | solution.py:400
  21.2 21.3 %all-to-all-start = ((f32[128,1,128]{2,1,0:T(1,128)}), f32[128,1,128]{2,1,0:T(1,128)S(1)}, u32[]{:S(2)}, u32[]{:S(2)}) async-start(f32[128,1,128]{2,1,0:T(1,128)} %get-tuple-element.16), calls=%async_computation | async-start | bytes 131072 | tf_op jit(solution)/shard_map/all_to_all | solution.py:451
  33.6 13.1 %collective-permute-start.2 = (f32[72,128]{1,0:T(8,128)S(1)}, f32[72,128]{1,0:T(8,128)S(1)}, u32[]{:S(2)}, u32[]{:S(2)}) collective-permute-start(f32[72,128]{1,0:T(8,128)S(1)} %get-tuple-element.23), channel_id=1, source_target_pairs={{0,1},{1,2},{2,3},{3,4},{4,5},{5,6},{6,7},{7,8},{8,9},{9,10},{10,1... | collective-permute-start | bytes 110600 | tf_op jit(solution)/shard_map/ppermute | solution.py:400
  36.4 10.2 %collective-permute-start.3 = (f32[72,128]{1,0:T(8,128)S(1)}, f32[72,128]{1,0:T(8,128)S(1)}, u32[]{:S(2)}, u32[]{:S(2)}) collective-permute-start(f32[72,128]{1,0:T(8,128)S(1)} %get-tuple-element.24), channel_id=1, source_target_pairs={{1,0},{2,1},{3,2},{4,3},{5,4},{6,5},{7,6},{8,7},{9,8},{10,9},{11,1... | collective-permute-start | bytes 110600 | tf_op jit(solution)/shard_map/ppermute | solution.py:401
  49.8 48.6 %all-to-all-start.1 = ((f32[128,1,6272]{2,1,0:T(1,128)}), f32[128,1,6272]{2,1,0:T(1,128)S(1)}, u32[]{:S(2)}, u32[]{:S(2)}) async-start(f32[128,1,6272]{2,1,0:T(1,128)} %get-tuple-element.26), calls=%async_computation.1 | async-start | bytes 6422528 | tf_op jit(solution)/shard_map/all_to_all | solution.py:473

commit v8 on v6

--- a/solution.py
+++ b/solution.py
@@ -120,7 +120,7 @@
     damage_ref[...] = jnp.exp(-damage_ref[...])
     get_state.wait()
     rounded_ref[0] = state_ref[...].astype(BF16)
-    eye = iota((width, width), 0) == iota((width, width), 1)
+    eye = iota((LANES, LANES), 0) == iota((LANES, LANES), 1)
 
     def advance(count, carry, waiting=False):
         now = count % 2 if waiting else lax.rem(count, 2)
@@ -129,8 +129,10 @@
         for t, part in enumerate(cuts):
             if waiting:
                 copies[t].wait()
-                block = stiffness_ref[part, part].astype(F32)
-                diagonal_ref[:, part] = jnp.sum(jnp.where(eye, block, 0.0), axis=0, keepdims=True)
+                for low in range(part.start, part.stop, LANES):
+                    near = slice(low, low + LANES)
+                    block = stiffness_ref[near, near].astype(F32)
+                    diagonal_ref[:, near] = jnp.sum(jnp.where(eye, block, 0.0), axis=0, keepdims=True)
             force = jnp.dot(rounded, stiffness_ref[:, part], preferred_element_type=F32)
             current = state_ref[:, part]
             bent = jnp.tanh(current)
@@ -190,23 +192,28 @@
     put_row_edges(field_ref, first_ref, last_ref)
 
 
-def pack_kernel(here_ref, steps_ref, counts_ref, state_ref, history_ref, out_ref, plan_ref):
-    slots, cells = state_ref.shape
+def plan_kernel(here_ref, counts_ref, plan_ref):
     devices = counts_ref.shape[0]
-    here = here_ref[0]
     counts = counts_ref[...]
     before = (iota((devices, devices), 1) < iota((devices, devices), 0)).astype(F32).astype(BF16)
     starts = jnp.dot(before, counts.astype(BF16), preferred_element_type=F32)
-    row = iota((devices, LANES), 0)
-    start = jnp.sum(jnp.where(row < here, counts, 0.0)[:, 0:1]).astype(jnp.int32)
     total = jnp.sum(counts, axis=0, keepdims=True)
     slot = iota((1, LANES), 1)
-    wanted = (2 * (here + devices * (slot // 2)) + slot % 2).astype(F32)
+    wanted = (2 * (here_ref[0] + devices * (slot // 2)) + slot % 2).astype(F32)
     source = jnp.sum(jnp.where(starts <= wanted, 1.0, 0.0), axis=0, keepdims=True) - 1.0
     index = jnp.where(wanted < total, 2.0 * source + (slot % 2).astype(F32), -1.0).astype(jnp.int32)
     plan_ref[...] = jnp.broadcast_to(index, plan_ref.shape)
+
+
+def pack_kernel(here_ref, steps_ref, counts_ref, state_ref, history_ref, out_ref):
+    slots, cells = state_ref.shape
+    counts = counts_ref[...]
+    row = iota(counts.shape, 0)
+    start = jnp.sum(jnp.where(row < here_ref[0], counts, 0.0)[:, 0:1]).astype(jnp.int32)
     places = 2 * out_ref.shape[0]
-    unused = lax.rem(2 * (start // 2) + places - 2, places)
+    assert places & (places - 1) == 0
+    last = places - 1
+    unused = (start - 2) & last & -2
     group = 8
 
     def one(block, rank):
@@ -215,10 +222,10 @@
         history = history_ref[pl.ds(at, group), :]
         for k in range(group):
             alive = steps_ref[at + k] > 0
-            to = jnp.where(alive, lax.rem(rank, places), unused)
-            at_lane = pl.multiple_of(lax.rem(to, 2) * (2 * cells), LANES)
-            out_ref[pl.ds(to // 2, 1), 0, pl.ds(at_lane, cells)] = state[k : k + 1]
-            out_ref[pl.ds(to // 2, 1), 0, pl.ds(at_lane + cells, cells)] = history[k : k + 1]
+            to = jnp.where(alive, rank & last, unused)
+            at_lane = pl.multiple_of((to & 1) * (2 * cells), LANES)
+            out_ref[pl.ds(to >> 1, 1), 0, pl.ds(at_lane, cells)] = state[k : k + 1]
+            out_ref[pl.ds(to >> 1, 1), 0, pl.ds(at_lane + cells, cells)] = history[k : k + 1]
             rank = rank + alive.astype(jnp.int32)
         return rank
 
@@ -363,9 +370,9 @@
             index = plan_ref[0, at + k]
             valid = index >= 0
             source = jnp.maximum(index, 0)
-            at_lane = pl.multiple_of(lax.rem(source, 2) * (2 * cells), LANES)
-            state = arrived_ref[pl.ds(source // 2, 1), 0, pl.ds(at_lane, cells)]
-            history = arrived_ref[pl.ds(source // 2, 1), 0, pl.ds(at_lane + cells, cells)]
+            at_lane = pl.multiple_of((source & 1) * (2 * cells), LANES)
+            state = arrived_ref[pl.ds(source >> 1, 1), 0, pl.ds(at_lane, cells)]
+            history = arrived_ref[pl.ds(source >> 1, 1), 0, pl.ds(at_lane + cells, cells)]
             new_state_ref[pl.ds(at + k, 1), :] = jnp.where(valid, state, 0.0)
             new_history_ref[pl.ds(at + k, 1), :] = jnp.where(valid, jnp.maximum(history, jnp.abs(state)), 0.0)
         return carry
@@ -448,13 +455,9 @@
     )(ids_row, steps_row, jump, external, cohesive, bond_mask, grid)
     below, above = swap(first, last, "row")
     counts = lax.all_to_all(mine, ROWS_COLS, 0, 0, tiled=True).reshape(devices, LANES)
-    packed, plan = call(
-        pack_kernel,
-        (packed_shape, shape(8, LANES, dtype=jnp.int32)),
-        [SMEM, SMEM, VMEM, VMEM, VMEM],
-        (VMEM, VMEM),
-        12,
-    )(here[None], newton_steps, counts, state, old_history)
+    packed = call(pack_kernel, packed_shape, [SMEM, SMEM, VMEM, VMEM, VMEM], VMEM, 12)(
+        here[None], newton_steps, counts, state, old_history
+    )
     to_left, to_right = call(
         lane_edges_kernel, (shape(edge, lanes), shape(edge, lanes)), [VMEM] * 3, (VMEM, VMEM), 4
     )(fields, below, above)
@@ -470,6 +473,7 @@
         aliases={7: 1},
     )(place, load_factor, fields, below, above, left, right, packed)
     arrived = lax.all_to_all(packed, ROWS_COLS, 0, 0, tiled=True)
+    plan = call(plan_kernel, shape(8, LANES, dtype=jnp.int32), [SMEM, VMEM], VMEM, 2)(here[None], counts)
     new_jump, new_load, new_state, new_history = call(
         functools.partial(last_kernel, 3.0 * rows * lanes * devices),
         (shape(3, rows, lanes), shape(1), shape(slots // 2, cells), shape(slots // 2, cells)),

time: 102 us -> 101 us (level)
    pallas_call x1 -> x2, Pallas kernels: 4.15 us -> 3.48 us  [the longest x1 3.31 us: on_device(): call(pack_kernel, packed_shape, [SMEM, SMEM, VMEM, VMEM, VMEM], VMEM, 12)]
  transfers between devices with their start and end apart: 6 -> 6, of which waited for: 2 -> 2; matrix products, arithmetic and copies ran while one was open for 0% -> 0% of each run, Pallas kernels for 5% -> 4%
where the time goes in v8:
time: 101 us
  waiting for transfers between devices  44.3 us (44%)
  starting transfers between devices  28.7 us (28%)
  Pallas kernels  24.8 us (25%)
  between operations  2.09 us (2%)
    all_to_all x1, waiting for transfers between devices, on_device(): arrived = lax.all_to_all(packed, ROWS_COLS, 0, 0, tiled=True)  40.2 us
    pallas_call x1, Pallas kernels, on_device(): call(newton_kernel, (shape(slots, cells), shape(FIELDS - INPUT_FIELDS, ro...  14.4 us
    all_to_all x1, starting transfers between devices, on_device(): lax.all_to_all(mine, ROWS_COLS, 0, 0, tiled=True).reshape(devices, LANES)  11.9 us
    all_to_all x1, starting transfers between devices, on_device(): arrived = lax.all_to_all(packed, ROWS_COLS, 0, 0, tiled=True)  8.39 us
    ppermute x2, starting transfers between devices, swap(): above = lax.ppermute(last, axis, up)  5.9 us
    all_to_all x1, waiting for transfers between devices, on_device(): lax.all_to_all(mine, ROWS_COLS, 0, 0, tiled=True).reshape(devices, LANES)  4.03 us
    pallas_call x1, Pallas kernels, on_device(): call(pack_kernel, packed_shape, [SMEM, SMEM, VMEM, VMEM, VMEM], VMEM, 12)  3.31 us
    pallas_call x1, Pallas kernels, on_device(): call(macro_kernel, (shape(6, rows, lanes), packed_shape), [SMEM, SMEM] +...  3.12 us
  transfers between devices with their start and end apart: 6, of which 2 were waited for; matrix products, arithmetic and copies ran while one was open for 0% of the time, Pallas kernels for 4%

profile of v8, /device:TPU:0, one launch (start us, length us, event | category | flops | bytes accessed | tf_op | source)
XLA Modules:
  0.0 100.9 jit_solution(16788312044399046530)
XLA Ops:
  0.6 0.7 copy-done.5
  1.3 0.7 shard_map.147.after_ref
  2.1 0.1 copy-done.1
  2.2 0.0 copy-start.3
  2.2 0.0 copy-start.4
  2.2 0.0 copy-start
  2.3 14.4 %shard_map.149 = (f32[160,1536]{1,0:T(8,128)S(1)}, f32[9,64,128]{2,1,0:T(8,128)S(1)}) custom-call(s32[1,160]{1,0:T(1,128)S(1)} %bitcast.11, s32[1,160]{1,0:T(1,128)S(1)} %bitcast.9, f32[3,64,128]{2,1,0:T(8,128)S(1)} %copy-done.1, bf16[1536,1536]{1,0:T(8,128)(2,1)} %stiffness_hbm.1, f32[3,1536]{1,0:T(4,128)S(1)} %copy-done.8, f32[160,1536]{1,0:T(8,128)} %old_state_hbm.1, ...), custom_call_target="tpu_custom_call" | custom-call | flops 6794772480 | bytes 7667712 | tf_op jit(solution)/shard_map/pallas_call | solution.py:429
  16.7 0.2 shard_map.150
  16.9 1.3 %collective-permute-start = (f32[72,128]{1,0:T(8,128)S(1)}, f32[72,128]{1,0:T(8,128)S(1)}, u32[]{:S(2)}, u32[]{:S(2)}) collective-permute-start(f32[72,128]{1,0:T(8,128)S(1)} %get-tuple-element.15), channel_id=1, source_target_pairs={{16,0},{32,16},{48,32},{64,48},{80,64},{96,80},{112,96},{17,1},{33... | collective-permute-start | bytes 110600 | tf_op jit(solution)/shard_map/ppermute | solution.py:408
  18.2 3.0 %collective-permute-start.1 = (f32[72,128]{1,0:T(8,128)S(1)}, f32[72,128]{1,0:T(8,128)S(1)}, u32[]{:S(2)}, u32[]{:S(2)}) collective-permute-start(f32[72,128]{1,0:T(8,128)S(1)} %get-tuple-element.16), channel_id=1, source_target_pairs={{0,16},{16,32},{32,48},{48,64},{64,80},{80,96},{96,112},{1,17},{17... | collective-permute-start | bytes 110600 | tf_op jit(solution)/shard_map/ppermute | solution.py:407
  21.2 11.9 %all-to-all-start = ((f32[128,1,128]{2,1,0:T(1,128)}), f32[128,1,128]{2,1,0:T(1,128)S(1)}, u32[]{:S(2)}, u32[]{:S(2)}) async-start(f32[128,1,128]{2,1,0:T(1,128)} %shard_map.147.after_ref), calls=%async_computation | async-start | bytes 131072 | tf_op jit(solution)/shard_map/all_to_all | solution.py:457
  33.1 0.0 collective-permute-done.below_ref
  33.1 0.0 collective-permute-done.1.above_ref
  33.1 0.5 shard_map.151
  33.6 2.9 %collective-permute-start.2 = (f32[72,128]{1,0:T(8,128)S(1)}, f32[72,128]{1,0:T(8,128)S(1)}, u32[]{:S(2)}, u32[]{:S(2)}) collective-permute-start(f32[72,128]{1,0:T(8,128)S(1)} %get-tuple-element.17), channel_id=1, source_target_pairs={{0,1},{1,2},{2,3},{3,4},{4,5},{5,6},{6,7},{7,8},{8,9},{9,10},{10,1... | collective-permute-start | bytes 110600 | tf_op jit(solution)/shard_map/ppermute | solution.py:407
  36.4 1.3 %collective-permute-start.3 = (f32[72,128]{1,0:T(8,128)S(1)}, f32[72,128]{1,0:T(8,128)S(1)}, u32[]{:S(2)}, u32[]{:S(2)}) collective-permute-start(f32[72,128]{1,0:T(8,128)S(1)} %get-tuple-element.18), channel_id=1, source_target_pairs={{1,0},{2,1},{3,2},{4,3},{5,4},{6,5},{7,6},{8,7},{9,8},{10,9},{11,1... | collective-permute-start | bytes 110600 | tf_op jit(solution)/shard_map/ppermute | solution.py:408
  37.7 0.1 pad_add_fusion.place_ref
  38.5 4.0 %all-to-all-done = f32[128,1,128]{2,1,0:T(1,128)S(1)} async-done(((f32[128,1,128]{2,1,0:T(1,128)}), f32[128,1,128]{2,1,0:T(1,128)S(1)}, u32[]{:S(2)}, u32[]{:S(2)}) %all-to-all-start) | async-done | bytes 65568 | tf_op jit(solution)/shard_map/all_to_all | solution.py:457
  42.5 3.3 %shard_map.152.packed_hbm = f32[128,1,6272]{2,1,0:T(1,128)} custom-call(s32[1]{0:T(128)} %bitcast.here_ref, s32[160]{0:T(256)S(1)} %copy-done.6, f32[128,128]{1,0:T(8,128)S(1)} %bitcast.6, f32[160,1536]{1,0:T(8,128)S(1)} %get-tuple-element.19.state_ref, f32[160,1536]{1,0:T(8,128)S(1)} %copy-done), custom_call_target="tpu_custom_call" | custom-call | tf_op jit(solution)/shard_map/pallas_call | solution.py:458
  45.8 3.1 %shard_map.153 = (f32[6,64,128]{2,1,0:T(8,128)S(1)}, f32[128,1,6272]{2,1,0:T(1,128)}) custom-call(s32[4]{0:T(128)S(1)} %pad_add_fusion.place_ref, f32[1]{0:T(128)S(6)} %copy.19.load_ref, f32[18,64,128]{2,1,0:T(8,128)S(1)} %get-tuple-element.14.field_ref, f32[72,128]{1,0:T(8,128)S(1)} %collective-permute-done.below_ref, ...), custom_call_target="tpu_custom_call", output_to_operand_aliasing={{1}: (7, {})} | custom-call | flops 200000000 | bytes 2000000 | tf_op jit(solution)/shard_map/pallas_call | solution.py:465
  49.0 8.4 %all-to-all-start.1 = ((f32[128,1,6272]{2,1,0:T(1,128)}), f32[128,1,6272]{2,1,0:T(1,128)S(1)}, u32[]{:S(2)}, u32[]{:S(2)}) async-start(f32[128,1,6272]{2,1,0:T(1,128)} %get-tuple-element.20), calls=%async_computation.1 | async-start | bytes 6422528 | tf_op jit(solution)/shard_map/all_to_all | solution.py:475
  58.0 0.2 shard_map.148.plan_ref
  58.2 40.2 %all-to-all-done.1.arrived_ref = f32[128,1,6272]{2,1,0:T(1,128)S(1)} async-done(((f32[128,1,6272]{2,1,0:T(1,128)}), f32[128,1,6272]{2,1,0:T(1,128)S(1)}, u32[]{:S(2)}, u32[]{:S(2)}) %all-to-all-start.1) | async-done | bytes 3211296 | tf_op jit(solution)/shard_map/all_to_all | solution.py:475
  98.4 2.4 %shard_map.154 = (f32[3,64,128]{2,1,0:T(8,128)}, f32[1]{0:T(128)}, f32[80,1536]{1,0:T(8,128)}, f32[80,1536]{1,0:T(8,128)}) custom-call(s32[8,128]{1,0:T(8,128)S(1)} %shard_map.148.plan_ref, f32[1]{0:T(128)S(6)} %copy.19.load_ref, f32[1]{0:T(128)S(6)} %copy.20.radius_ref, f32[128,1,6272]{2,1,0:T(1,128)S(1)} %all-to-all-done.1.arrived_ref, ...), custom_call_target="tpu_custom_call" | custom-call | tf_op jit(solution)/shard_map/pallas_call | solution.py:477
  (15 shorter events, 0.0 us)
Async XLA Ops:
  0.6 0.7 copy-start.5
  1.3 0.9 copy-start.1
  1.3 0.9 copy-start.6
  1.3 0.9 copy-start.7
  1.3 0.9 copy-start.8
  2.2 14.4 %copy-start.2 = (f32[3,64,128]{2,1,0:T(8,128)S(1)}, f32[3,64,128]{2,1,0:T(8,128)}, u32[]{:S(2)}) copy-start(f32[3,64,128]{2,1,0:T(8,128)} %external_ref.1) | copy-start | bytes 294916
  2.2 14.5 %copy-start.3 = (s32[2,64,128]{2,1,0:T(8,128)S(1)}, s32[2,64,128]{2,1,0:T(8,128)}, u32[]{:S(2)}) copy-start(s32[2,64,128]{2,1,0:T(8,128)} %mask_ref.1) | copy-start | bytes 196612
  2.2 14.4 %copy-start.4 = (f32[64,128]{1,0:T(8,128)S(1)}, f32[64,128]{1,0:T(8,128)}, u32[]{:S(2)}) copy-start(f32[64,128]{1,0:T(8,128)} %cohesive_ref.1) | copy-start | bytes 98308
  2.2 40.3 %copy-start = (f32[160,1536]{1,0:T(8,128)S(1)}, f32[160,1536]{1,0:T(8,128)}, u32[]{:S(2)}) copy-start(f32[160,1536]{1,0:T(8,128)} %history_ref.1) | copy-start | bytes 2949124
  16.9 16.2 %collective-permute-start = (f32[72,128]{1,0:T(8,128)S(1)}, f32[72,128]{1,0:T(8,128)S(1)}, u32[]{:S(2)}, u32[]{:S(2)}) collective-permute-start(f32[72,128]{1,0:T(8,128)S(1)} %get-tuple-element.15), channel_id=1, source_target_pairs={{16,0},{32,16},{48,32},{64,48},{80,64},{96,80},{112,96},{17,1},{33... | collective-permute-start | bytes 110600 | tf_op jit(solution)/shard_map/ppermute | solution.py:408
  18.2 14.9 %collective-permute-start.1 = (f32[72,128]{1,0:T(8,128)S(1)}, f32[72,128]{1,0:T(8,128)S(1)}, u32[]{:S(2)}, u32[]{:S(2)}) collective-permute-start(f32[72,128]{1,0:T(8,128)S(1)} %get-tuple-element.16), channel_id=1, source_target_pairs={{0,16},{16,32},{32,48},{48,64},{64,80},{80,96},{96,112},{1,17},{17... | collective-permute-start | bytes 110600 | tf_op jit(solution)/shard_map/ppermute | solution.py:407
  21.2 21.3 %all-to-all-start = ((f32[128,1,128]{2,1,0:T(1,128)}), f32[128,1,128]{2,1,0:T(1,128)S(1)}, u32[]{:S(2)}, u32[]{:S(2)}) async-start(f32[128,1,128]{2,1,0:T(1,128)} %shard_map.147.after_ref), calls=%async_computation | async-start | bytes 131072 | tf_op jit(solution)/shard_map/all_to_all | solution.py:457
  33.6 12.3 %collective-permute-start.2 = (f32[72,128]{1,0:T(8,128)S(1)}, f32[72,128]{1,0:T(8,128)S(1)}, u32[]{:S(2)}, u32[]{:S(2)}) collective-permute-start(f32[72,128]{1,0:T(8,128)S(1)} %get-tuple-element.17), channel_id=1, source_target_pairs={{0,1},{1,2},{2,3},{3,4},{4,5},{5,6},{6,7},{7,8},{8,9},{9,10},{10,1... | collective-permute-start | bytes 110600 | tf_op jit(solution)/shard_map/ppermute | solution.py:407
  36.4 9.4 %collective-permute-start.3 = (f32[72,128]{1,0:T(8,128)S(1)}, f32[72,128]{1,0:T(8,128)S(1)}, u32[]{:S(2)}, u32[]{:S(2)}) collective-permute-start(f32[72,128]{1,0:T(8,128)S(1)} %get-tuple-element.18), channel_id=1, source_target_pairs={{1,0},{2,1},{3,2},{4,3},{5,4},{6,5},{7,6},{8,7},{9,8},{10,9},{11,1... | collective-permute-start | bytes 110600 | tf_op jit(solution)/shard_map/ppermute | solution.py:408
  49.0 49.5 %all-to-all-start.1 = ((f32[128,1,6272]{2,1,0:T(1,128)}), f32[128,1,6272]{2,1,0:T(1,128)S(1)}, u32[]{:S(2)}, u32[]{:S(2)}) async-start(f32[128,1,6272]{2,1,0:T(1,128)} %get-tuple-element.20), calls=%async_computation.1 | async-start | bytes 6422528 | tf_op jit(solution)/shard_map/all_to_all | solution.py:475

commit v9 on v8

--- a/solution.py
+++ b/solution.py
@@ -39,11 +39,20 @@
     return lax.dot_general(a, b, (((1,), (1,)), ((), ())), preferred_element_type=F32)
 
 
-def put_row_edges(field_ref, first_ref, last_ref):
+def even_on(axis):
+    return lax.rem(lax.axis_index(axis), 2) == 0
+
+
+def by_parity(even, first, second):
+    return jnp.where(even, first, second), jnp.where(even, second, first)
+
+
+def put_row_edges(field_ref, near_ref, far_ref):
     fields, rows, _ = field_ref.shape
+    even = even_on("row")
     for c in range(fields):
-        first_ref[HALO * c : HALO * (c + 1), :] = field_ref[c, :HALO, :]
-        last_ref[HALO * c : HALO * (c + 1), :] = field_ref[c, rows - HALO :, :]
+        part = slice(HALO * c, HALO * (c + 1))
+        near_ref[part, :], far_ref[part, :] = by_parity(even, field_ref[c, rows - HALO :, :], field_ref[c, :HALO, :])
 
 
 def with_row_halo(field, below, above, c):
@@ -56,8 +65,8 @@
     out_ref[...] = jnp.broadcast_to(live[None], out_ref.shape)
 
 
-def lane_edges_kernel(field_ref, below_ref, above_ref, to_left_ref, to_right_ref):
-    below, above = below_ref[...], above_ref[...]
+def lane_edges_kernel(field_ref, row_near_ref, row_far_ref, near_ref, far_ref):
+    below, above = by_parity(even_on("row"), row_near_ref[...], row_far_ref[...])
     fields, rows, lanes = field_ref.shape
     tall = rows + 2 * HALO
     group = iota((tall, lanes), 1) // HALO
@@ -67,8 +76,9 @@
         heads = jnp.where(group == c, pltpu.roll(whole, HALO * c, 1) if c else whole, heads)
         tails = jnp.where(group == c, pltpu.roll(whole, HALO * (c + 1), 1), tails)
     fill = jnp.zeros((lanes - tall, lanes), F32)
-    to_left_ref[...] = jnp.concatenate([heads, fill], axis=0).T[: HALO * fields]
-    to_right_ref[...] = jnp.concatenate([tails, fill], axis=0).T[: HALO * fields]
+    to_left = jnp.concatenate([heads, fill], axis=0).T[: HALO * fields]
+    to_right = jnp.concatenate([tails, fill], axis=0).T[: HALO * fields]
+    near_ref[...], far_ref[...] = by_parity(even_on("col"), to_right, to_left)
 
 
 def newton_kernel(
@@ -173,7 +183,7 @@
 
 
 def fields_kernel(
-    ids_ref, steps_ref, jump_ref, external_ref, cohesive_ref, mask_ref, grid_ref, field_ref, first_ref, last_ref
+    ids_ref, steps_ref, jump_ref, external_ref, cohesive_ref, mask_ref, grid_ref, field_ref, near_ref, far_ref
 ):
     rows, lanes = cohesive_ref.shape
     slots = ids_ref.shape[1]
@@ -189,7 +199,7 @@
     field_ref[8] = 0.25 + 0.75 * mask_ref[1].astype(F32)
     for c in range(FIELDS - INPUT_FIELDS):
         field_ref[INPUT_FIELDS + c] = grid_ref[c]
-    put_row_edges(field_ref, first_ref, last_ref)
+    put_row_edges(field_ref, near_ref, far_ref)
 
 
 def plan_kernel(here_ref, counts_ref, plan_ref):
@@ -233,7 +243,7 @@
 
 
 def macro_kernel(
-    place_ref, load_ref, field_ref, below_ref, above_ref, left_ref, right_ref, packed_hbm,
+    place_ref, load_ref, field_ref, row_near_ref, row_far_ref, col_near_ref, col_far_ref, packed_hbm,
     moved_ref, packed_out, sums_ref, sem,
 ):
     del packed_hbm
@@ -249,10 +259,11 @@
     row_ok = jnp.where(line < rows, 1, jnp.where(line < rows + HALO, has_below, has_above)) > 0
     side_ok = jnp.where(lane < HALO, has_right, jnp.where(lane >= LANES - HALO, has_left, 0)) > 0
     valid = (row_ok, row_ok & side_ok)
-    below, above = below_ref[...], above_ref[...]
-    fill = jnp.zeros((LANES - left_ref.shape[0], LANES), F32)
-    left = jnp.concatenate([left_ref[...], fill], axis=0).T[:tall]
-    right = jnp.concatenate([right_ref[...], fill], axis=0).T[:tall]
+    below, above = by_parity(even_on("row"), row_near_ref[...], row_far_ref[...])
+    right, left = by_parity(even_on("col"), col_near_ref[...], col_far_ref[...])
+    fill = jnp.zeros((LANES - left.shape[0], LANES), F32)
+    left = jnp.concatenate([left, fill], axis=0).T[:tall]
+    right = jnp.concatenate([right, fill], axis=0).T[:tall]
 
     def field(c):
         middle = with_row_halo(field_ref[c], below, above, c)
@@ -400,13 +411,11 @@
     )
 
 
-def swap(first, last, axis):
+def swap(near, far, axis):
     size = lax.axis_size(axis)
-    up = [(i, i + 1) for i in range(size - 1)]
-    down = [(i + 1, i) for i in range(size - 1)]
-    above = lax.ppermute(last, axis, up)
-    below = lax.ppermute(first, axis, down)
-    return below, above
+    pairs = [(i, i + 1) for i in range(size - 1)]
+    both = [pairs[k::2] + [(b, a) for a, b in pairs[k::2]] for k in range(2)]
+    return lax.ppermute(near, axis, both[0]), lax.ppermute(far, axis, both[1])
 
 
 def on_device(
@@ -446,22 +455,22 @@
             bytes_accessed=2 * cells * cells + 12 * slots * cells,
         ),
     )(ids_row, steps_row, jump, stiffness, coupling, old_state, old_history, mine)
-    fields, first, last = call(
+    fields, near, far = call(
         fields_kernel,
         (shape(FIELDS, rows, lanes), shape(edge, lanes), shape(edge, lanes)),
         [VMEM] * 7,
         (VMEM,) * 3,
         4,
     )(ids_row, steps_row, jump, external, cohesive, bond_mask, grid)
-    below, above = swap(first, last, "row")
+    row_near, row_far = swap(near, far, "row")
     counts = lax.all_to_all(mine, ROWS_COLS, 0, 0, tiled=True).reshape(devices, LANES)
     packed = call(pack_kernel, packed_shape, [SMEM, SMEM, VMEM, VMEM, VMEM], VMEM, 12)(
         here[None], newton_steps, counts, state, old_history
     )
-    to_left, to_right = call(
+    near, far = call(
         lane_edges_kernel, (shape(edge, lanes), shape(edge, lanes)), [VMEM] * 3, (VMEM, VMEM), 4
-    )(fields, below, above)
-    right, left = swap(to_left, to_right, "col")
+    )(fields, row_near, row_far)
+    col_near, col_far = swap(near, far, "col")
     moved, packed = call(
         macro_kernel,
         (shape(6, rows, lanes), packed_shape),
@@ -471,7 +480,7 @@
         scratch=(pltpu.VMEM((devices, 1, LANES), F32), pltpu.SemaphoreType.DMA),
         cost=pl.CostEstimate(flops=200_000_000, transcendentals=0, bytes_accessed=2_000_000),
         aliases={7: 1},
-    )(place, load_factor, fields, below, above, left, right, packed)
+    )(place, load_factor, fields, row_near, row_far, col_near, col_far, packed)
     arrived = lax.all_to_all(packed, ROWS_COLS, 0, 0, tiled=True)
     plan = call(plan_kernel, shape(8, LANES, dtype=jnp.int32), [SMEM, VMEM], VMEM, 2)(here[None], counts)
     new_jump, new_load, new_state, new_history = call(

time: 101 us -> 97 us (0.960)
  starting transfers between devices: 28.7 us -> 21.9 us
  waiting for transfers between devices: 44.3 us -> 46.8 us
    ppermute x4, starting transfers between devices: 8.49 us -> 2.41 us  [swap(): return (lax.ppermute(near, axis, both[0]), lax.ppermute(far, axis, both[1]))]
    all_to_all x1, waiting for transfers between devices: 4.03 us -> 6.5 us  [on_device(): lax.all_to_all(mine, ROWS_COLS, 0, 0, tiled=True).reshape(devices, LANES)]
    all_to_all x1, starting transfers between devices: 8.39 us -> 6.11 us  [on_device(): arrived = lax.all_to_all(packed, ROWS_COLS, 0, 0, tiled=True)]
    all_to_all x1, starting transfers between devices: 11.9 us -> 13.3 us  [on_device(): lax.all_to_all(mine, ROWS_COLS, 0, 0, tiled=True).reshape(devices, LANES)]
where the time goes in v9:
time: 97 us; the launch traced here: 96.5 us
  waiting for transfers between devices  46.8 us (48%)
  Pallas kernels  24.9 us (26%)
  starting transfers between devices  21.9 us (23%)
  between operations  2.09 us (2%)
    all_to_all x1, waiting for transfers between devices, on_device(): arrived = lax.all_to_all(packed, ROWS_COLS, 0, 0, tiled=True)  40.2 us
    pallas_call x1, Pallas kernels, on_device(): call(newton_kernel, (shape(slots, cells), shape(FIELDS - INPUT_FIELDS, ro...  14.4 us
    all_to_all x1, starting transfers between devices, on_device(): lax.all_to_all(mine, ROWS_COLS, 0, 0, tiled=True).reshape(devices, LANES)  13.3 us
    all_to_all x1, waiting for transfers between devices, on_device(): lax.all_to_all(mine, ROWS_COLS, 0, 0, tiled=True).reshape(devices, LANES)  6.5 us
    all_to_all x1, starting transfers between devices, on_device(): arrived = lax.all_to_all(packed, ROWS_COLS, 0, 0, tiled=True)  6.11 us
    pallas_call x1, Pallas kernels, on_device(): call(pack_kernel, packed_shape, [SMEM, SMEM, VMEM, VMEM, VMEM], VMEM, 12)  3.31 us
    pallas_call x1, Pallas kernels, on_device(): call(macro_kernel, (shape(6, rows, lanes), packed_shape), [SMEM, SMEM] +...  3.18 us
    pallas_call x1, Pallas kernels, on_device(): call(functools.partial(last_kernel, 3.0 * rows * lanes * devices), (shape...  2.45 us
  transfers between devices with their start and end apart: 6, of which 2 were waited for; matrix products, arithmetic and copies ran while one was open for 0% of the time, Pallas kernels for 4%

profile of v9, /device:TPU:0, one launch (start us, length us, event | category | flops | bytes accessed | tf_op | source)
XLA Modules:
  0.0 96.5 jit_solution(11217737169042632959)
XLA Ops:
  0.6 0.7 copy-done.5
  1.3 0.7 shard_map.147.after_ref
  2.1 0.1 copy-done.1
  2.2 0.0 copy-start.3
  2.2 0.0 copy-start.4
  2.2 0.0 copy-start
  2.3 14.4 %shard_map.149 = (f32[160,1536]{1,0:T(8,128)S(1)}, f32[9,64,128]{2,1,0:T(8,128)S(1)}) custom-call(s32[1,160]{1,0:T(1,128)S(1)} %bitcast.11, s32[1,160]{1,0:T(1,128)S(1)} %bitcast.9, f32[3,64,128]{2,1,0:T(8,128)S(1)} %copy-done.1, bf16[1536,1536]{1,0:T(8,128)(2,1)} %stiffness_hbm.1, f32[3,1536]{1,0:T(4,128)S(1)} %copy-done.8, f32[160,1536]{1,0:T(8,128)} %old_state_hbm.1, ...), custom_call_target="tpu_custom_call" | custom-call | flops 6794772480 | bytes 7667712 | tf_op jit(solution)/shard_map/pallas_call | solution.py:438
  16.7 0.2 shard_map.150
  16.9 0.0 collective-permute-start
  16.9 0.7 collective-permute-start.1
  17.6 13.3 %all-to-all-start = ((f32[128,1,128]{2,1,0:T(1,128)}), f32[128,1,128]{2,1,0:T(1,128)S(1)}, u32[]{:S(2)}, u32[]{:S(2)}) async-start(f32[128,1,128]{2,1,0:T(1,128)} %shard_map.147.after_ref), calls=%async_computation | async-start | bytes 131072 | tf_op jit(solution)/shard_map/all_to_all | solution.py:466
  30.9 0.0 collective-permute-done.row_near_ref
  30.9 0.0 collective-permute-done.1.row_far_ref
  31.0 0.5 shard_map.151
  31.4 1.0 %collective-permute-start.2 = (f32[72,128]{1,0:T(8,128)S(1)}, f32[72,128]{1,0:T(8,128)S(1)}, u32[]{:S(2)}, u32[]{:S(2)}) collective-permute-start(f32[72,128]{1,0:T(8,128)S(1)} %get-tuple-element.17), channel_id=1, source_target_pairs={{0,1},{2,3},{4,5},{6,7},{8,9},{10,11},{12,13},{14,15},{1,0},{3,2},... | collective-permute-start | bytes 110600 | tf_op jit(solution)/shard_map/ppermute | solution.py:418
  32.5 0.7 collective-permute-start.3
  33.1 0.1 pad_add_fusion.place_ref
  33.9 6.5 %all-to-all-done = f32[128,1,128]{2,1,0:T(1,128)S(1)} async-done(((f32[128,1,128]{2,1,0:T(1,128)}), f32[128,1,128]{2,1,0:T(1,128)S(1)}, u32[]{:S(2)}, u32[]{:S(2)}) %all-to-all-start) | async-done | bytes 65568 | tf_op jit(solution)/shard_map/all_to_all | solution.py:466
  40.4 3.3 %shard_map.152.packed_hbm = f32[128,1,6272]{2,1,0:T(1,128)} custom-call(s32[1]{0:T(128)} %bitcast.here_ref, s32[160]{0:T(256)S(1)} %copy-done.6, f32[128,128]{1,0:T(8,128)S(1)} %bitcast.6, f32[160,1536]{1,0:T(8,128)S(1)} %get-tuple-element.19.state_ref, f32[160,1536]{1,0:T(8,128)S(1)} %copy-done), custom_call_target="tpu_custom_call" | custom-call | tf_op jit(solution)/shard_map/pallas_call | solution.py:467
  43.7 3.2 %shard_map.153 = (f32[6,64,128]{2,1,0:T(8,128)S(1)}, f32[128,1,6272]{2,1,0:T(1,128)}) custom-call(s32[4]{0:T(128)S(1)} %pad_add_fusion.place_ref, f32[1]{0:T(128)S(6)} %copy.19.load_ref, f32[18,64,128]{2,1,0:T(8,128)S(1)} %get-tuple-element.14.field_ref, f32[72,128]{1,0:T(8,128)S(1)} %collective-permute-done.row_near_ref, ...), custom_call_target="tpu_custom_call", output_to_operand_aliasing={{1}: (7, {})} | custom-call | flops 200000000 | bytes 2000000 | tf_op jit(solution)/shard_map/pallas_call | solution.py:474
  46.9 6.1 %all-to-all-start.1 = ((f32[128,1,6272]{2,1,0:T(1,128)}), f32[128,1,6272]{2,1,0:T(1,128)S(1)}, u32[]{:S(2)}, u32[]{:S(2)}) async-start(f32[128,1,6272]{2,1,0:T(1,128)} %get-tuple-element.20), calls=%async_computation.1 | async-start | bytes 6422528 | tf_op jit(solution)/shard_map/all_to_all | solution.py:484
  53.6 0.2 shard_map.148.plan_ref
  53.8 40.2 %all-to-all-done.1.arrived_ref = f32[128,1,6272]{2,1,0:T(1,128)S(1)} async-done(((f32[128,1,6272]{2,1,0:T(1,128)}), f32[128,1,6272]{2,1,0:T(1,128)S(1)}, u32[]{:S(2)}, u32[]{:S(2)}) %all-to-all-start.1) | async-done | bytes 3211296 | tf_op jit(solution)/shard_map/all_to_all | solution.py:484
  94.0 2.4 %shard_map.154 = (f32[3,64,128]{2,1,0:T(8,128)}, f32[1]{0:T(128)}, f32[80,1536]{1,0:T(8,128)}, f32[80,1536]{1,0:T(8,128)}) custom-call(s32[8,128]{1,0:T(8,128)S(1)} %shard_map.148.plan_ref, f32[1]{0:T(128)S(6)} %copy.19.load_ref, f32[1]{0:T(128)S(6)} %copy.20.radius_ref, f32[128,1,6272]{2,1,0:T(1,128)S(1)} %all-to-all-done.1.arrived_ref, ...), custom_call_target="tpu_custom_call" | custom-call | tf_op jit(solution)/shard_map/pallas_call | solution.py:486
  (15 shorter events, 0.0 us)
Async XLA Ops:
  0.6 0.7 copy-start.5
  1.3 0.9 copy-start.1
  1.3 0.9 copy-start.6
  1.3 0.9 copy-start.7
  1.3 0.9 copy-start.8
  2.2 14.4 %copy-start.2 = (f32[3,64,128]{2,1,0:T(8,128)S(1)}, f32[3,64,128]{2,1,0:T(8,128)}, u32[]{:S(2)}) copy-start(f32[3,64,128]{2,1,0:T(8,128)} %external_ref.1) | copy-start | bytes 294916
  2.2 14.5 %copy-start.3 = (s32[2,64,128]{2,1,0:T(8,128)S(1)}, s32[2,64,128]{2,1,0:T(8,128)}, u32[]{:S(2)}) copy-start(s32[2,64,128]{2,1,0:T(8,128)} %mask_ref.1) | copy-start | bytes 196612
  2.2 14.4 %copy-start.4 = (f32[64,128]{1,0:T(8,128)S(1)}, f32[64,128]{1,0:T(8,128)}, u32[]{:S(2)}) copy-start(f32[64,128]{1,0:T(8,128)} %cohesive_ref.1) | copy-start | bytes 98308
  2.2 38.1 %copy-start = (f32[160,1536]{1,0:T(8,128)S(1)}, f32[160,1536]{1,0:T(8,128)}, u32[]{:S(2)}) copy-start(f32[160,1536]{1,0:T(8,128)} %history_ref.1) | copy-start | bytes 2949124
  16.9 14.1 %collective-permute-start = (f32[72,128]{1,0:T(8,128)S(1)}, f32[72,128]{1,0:T(8,128)S(1)}, u32[]{:S(2)}, u32[]{:S(2)}) collective-permute-start(f32[72,128]{1,0:T(8,128)S(1)} %get-tuple-element.15), channel_id=1, source_target_pairs={{0,16},{32,48},{64,80},{96,112},{16,0},{48,32},{80,64},{112,96},{1... | collective-permute-start | bytes 110600 | tf_op jit(solution)/shard_map/ppermute | solution.py:418
  16.9 14.0 %collective-permute-start.1 = (f32[72,128]{1,0:T(8,128)S(1)}, f32[72,128]{1,0:T(8,128)S(1)}, u32[]{:S(2)}, u32[]{:S(2)}) collective-permute-start(f32[72,128]{1,0:T(8,128)S(1)} %get-tuple-element.16), channel_id=1, source_target_pairs={{16,32},{48,64},{80,96},{32,16},{64,48},{96,80},{17,33},{49,65},{8... | collective-permute-start | bytes 110600 | tf_op jit(solution)/shard_map/ppermute | solution.py:418
  17.6 22.8 %all-to-all-start = ((f32[128,1,128]{2,1,0:T(1,128)}), f32[128,1,128]{2,1,0:T(1,128)S(1)}, u32[]{:S(2)}, u32[]{:S(2)}) async-start(f32[128,1,128]{2,1,0:T(1,128)} %shard_map.147.after_ref), calls=%async_computation | async-start | bytes 131072 | tf_op jit(solution)/shard_map/all_to_all | solution.py:466
  31.4 12.3 %collective-permute-start.2 = (f32[72,128]{1,0:T(8,128)S(1)}, f32[72,128]{1,0:T(8,128)S(1)}, u32[]{:S(2)}, u32[]{:S(2)}) collective-permute-start(f32[72,128]{1,0:T(8,128)S(1)} %get-tuple-element.17), channel_id=1, source_target_pairs={{0,1},{2,3},{4,5},{6,7},{8,9},{10,11},{12,13},{14,15},{1,0},{3,2},... | collective-permute-start | bytes 110600 | tf_op jit(solution)/shard_map/ppermute | solution.py:418
  32.5 11.2 %collective-permute-start.3 = (f32[72,128]{1,0:T(8,128)S(1)}, f32[72,128]{1,0:T(8,128)S(1)}, u32[]{:S(2)}, u32[]{:S(2)}) collective-permute-start(f32[72,128]{1,0:T(8,128)S(1)} %get-tuple-element.18), channel_id=1, source_target_pairs={{1,2},{3,4},{5,6},{7,8},{9,10},{11,12},{13,14},{2,1},{4,3},{6,5},{... | collective-permute-start | bytes 110600 | tf_op jit(solution)/shard_map/ppermute | solution.py:418
  46.9 47.2 %all-to-all-start.1 = ((f32[128,1,6272]{2,1,0:T(1,128)}), f32[128,1,6272]{2,1,0:T(1,128)S(1)}, u32[]{:S(2)}, u32[]{:S(2)}) async-start(f32[128,1,6272]{2,1,0:T(1,128)} %get-tuple-element.20), calls=%async_computation.1 | async-start | bytes 6422528 | tf_op jit(solution)/shard_map/all_to_all | solution.py:484

commit v10 on v9

--- a/solution.py
+++ b/solution.py
@@ -82,11 +82,11 @@
 
 
 def newton_kernel(
-    ids_ref, steps_ref, jump_ref, stiffness_hbm, coupling_ref, old_state_hbm, history_hbm, after_ref,
-    state_ref, grid_ref,
+    ids_ref, steps_ref, jump_ref, stiffness_hbm, coupling_ref, old_state_hbm, history_hbm, count_in,
+    state_ref, grid_ref, count_out,
     stiffness_ref, damage_ref, load_ref, diagonal_ref, rounded_ref, sems,
 ):
-    del after_ref
+    del count_in, count_out
     width = 256
     cuts = [slice(t * width, (t + 1) * width) for t in range(stiffness_hbm.shape[1] // width)]
     copies = [
@@ -435,11 +435,11 @@
     steps_row = newton_steps.reshape(1, slots)
 
     mine = call(count_kernel, shape(devices, 1, LANES), [VMEM], VMEM, 2, cost=LONG)(steps_row)
-    state, grid = call(
+    state, grid, mine = call(
         newton_kernel,
-        (shape(slots, cells), shape(FIELDS - INPUT_FIELDS, rows, lanes)),
+        (shape(slots, cells), shape(FIELDS - INPUT_FIELDS, rows, lanes), shape(devices, 1, LANES)),
         [VMEM] * 3 + [HBM, VMEM, HBM, HBM, HBM],
-        (VMEM, VMEM),
+        (VMEM, VMEM, HBM),
         NEWTON_MIB,
         scratch=(
             pltpu.VMEM(stiffness.shape, BF16),
@@ -454,6 +454,7 @@
             transcendentals=2 * MAX_STEPS * slots * cells,
             bytes_accessed=2 * cells * cells + 12 * slots * cells,
         ),
+        aliases={7: 2},
     )(ids_row, steps_row, jump, stiffness, coupling, old_state, old_history, mine)
     fields, near, far = call(
         fields_kernel,

time: 97 us -> 97 us (level)
  no operation moved by 1% of the time
where the time goes in v10:
time: 97 us; the launch traced here: 96.5 us
  waiting for transfers between devices  46.8 us (48%)
  Pallas kernels  24.9 us (26%)
  starting transfers between devices  21.9 us (23%)
  between operations  2.09 us (2%)
    all_to_all x1, waiting for transfers between devices, on_device(): arrived = lax.all_to_all(packed, ROWS_COLS, 0, 0, tiled=True)  40.2 us
    pallas_call x1, Pallas kernels, on_device(): call(newton_kernel, (shape(slots, cells), shape(FIELDS - INPUT_FIELDS, ro...  14.4 us
    all_to_all x1, starting transfers between devices, on_device(): lax.all_to_all(mine, ROWS_COLS, 0, 0, tiled=True).reshape(devices, LANES)  13.3 us
    all_to_all x1, waiting for transfers between devices, on_device(): lax.all_to_all(mine, ROWS_COLS, 0, 0, tiled=True).reshape(devices, LANES)  6.5 us
    all_to_all x1, starting transfers between devices, on_device(): arrived = lax.all_to_all(packed, ROWS_COLS, 0, 0, tiled=True)  6.11 us
    pallas_call x1, Pallas kernels, on_device(): call(pack_kernel, packed_shape, [SMEM, SMEM, VMEM, VMEM, VMEM], VMEM, 12)  3.31 us
    pallas_call x1, Pallas kernels, on_device(): call(macro_kernel, (shape(6, rows, lanes), packed_shape), [SMEM, SMEM] +...  3.18 us
    pallas_call x1, Pallas kernels, on_device(): call(functools.partial(last_kernel, 3.0 * rows * lanes * devices), (shape...  2.45 us
  transfers between devices with their start and end apart: 6, of which 2 were waited for; matrix products, arithmetic and copies ran while one was open for 0% of the time, Pallas kernels for 4%

profile of v10, /device:TPU:0, one launch (start us, length us, event | category | flops | bytes accessed | tf_op | source)
XLA Modules:
  0.0 96.5 jit_solution(3017020481685360668)
XLA Ops:
  0.6 0.7 copy-done.5
  1.3 0.7 shard_map.147.count_in
  2.1 0.1 copy-done.1
  2.2 0.0 copy-start.3
  2.2 0.0 copy-start.4
  2.2 0.0 copy-start
  2.3 14.4 %shard_map.148 = (f32[160,1536]{1,0:T(8,128)S(1)}, f32[9,64,128]{2,1,0:T(8,128)S(1)}, f32[128,1,128]{2,1,0:T(1,128)}) custom-call(s32[1,160]{1,0:T(1,128)S(1)} %bitcast.11, s32[1,160]{1,0:T(1,128)S(1)} %bitcast.9, f32[3,64,128]{2,1,0:T(8,128)S(1)} %copy-done.1, bf16[1536,1536]{1,0:T(8,128)(2,1)} %stiffness_hbm.1, ...), custom_call_target="tpu_custom_call", output_to_operand_aliasing={{2}: (7, {})} | custom-call | flops 6794772480 | bytes 7667712 | tf_op jit(solution)/shard_map/pallas_call | solution.py:438
  16.7 0.2 shard_map.150
  16.9 0.0 collective-permute-start
  16.9 0.7 collective-permute-start.1
  17.6 13.3 %all-to-all-start = ((f32[128,1,128]{2,1,0:T(1,128)}), f32[128,1,128]{2,1,0:T(1,128)S(1)}, u32[]{:S(2)}, u32[]{:S(2)}) async-start(f32[128,1,128]{2,1,0:T(1,128)} %get-tuple-element.14), calls=%async_computation | async-start | bytes 131072 | tf_op jit(solution)/shard_map/all_to_all | solution.py:467
  30.9 0.0 collective-permute-done.row_near_ref
  30.9 0.0 collective-permute-done.1.row_far_ref
  31.0 0.5 shard_map.151
  31.4 1.0 %collective-permute-start.2 = (f32[72,128]{1,0:T(8,128)S(1)}, f32[72,128]{1,0:T(8,128)S(1)}, u32[]{:S(2)}, u32[]{:S(2)}) collective-permute-start(f32[72,128]{1,0:T(8,128)S(1)} %get-tuple-element.19), channel_id=1, source_target_pairs={{0,1},{2,3},{4,5},{6,7},{8,9},{10,11},{12,13},{14,15},{1,0},{3,2},... | collective-permute-start | bytes 110600 | tf_op jit(solution)/shard_map/ppermute | solution.py:418
  32.5 0.7 collective-permute-start.3
  33.1 0.1 pad_add_fusion.place_ref
  33.9 6.5 %all-to-all-done = f32[128,1,128]{2,1,0:T(1,128)S(1)} async-done(((f32[128,1,128]{2,1,0:T(1,128)}), f32[128,1,128]{2,1,0:T(1,128)S(1)}, u32[]{:S(2)}, u32[]{:S(2)}) %all-to-all-start) | async-done | bytes 65568 | tf_op jit(solution)/shard_map/all_to_all | solution.py:467
  40.4 3.3 %shard_map.152.packed_hbm = f32[128,1,6272]{2,1,0:T(1,128)} custom-call(s32[1]{0:T(128)} %bitcast.here_ref, s32[160]{0:T(256)S(1)} %copy-done.6, f32[128,128]{1,0:T(8,128)S(1)} %bitcast.6, f32[160,1536]{1,0:T(8,128)S(1)} %get-tuple-element.21.state_ref, f32[160,1536]{1,0:T(8,128)S(1)} %copy-done), custom_call_target="tpu_custom_call" | custom-call | tf_op jit(solution)/shard_map/pallas_call | solution.py:468
  43.7 3.2 %shard_map.153 = (f32[6,64,128]{2,1,0:T(8,128)S(1)}, f32[128,1,6272]{2,1,0:T(1,128)}) custom-call(s32[4]{0:T(128)S(1)} %pad_add_fusion.place_ref, f32[1]{0:T(128)S(6)} %copy.21.load_ref, f32[18,64,128]{2,1,0:T(8,128)S(1)} %get-tuple-element.16.field_ref, f32[72,128]{1,0:T(8,128)S(1)} %collective-permute-done.row_near_ref, ...), custom_call_target="tpu_custom_call", output_to_operand_aliasing={{1}: (7, {})} | custom-call | flops 200000000 | bytes 2000000 | tf_op jit(solution)/shard_map/pallas_call | solution.py:475
  46.9 6.1 %all-to-all-start.1 = ((f32[128,1,6272]{2,1,0:T(1,128)}), f32[128,1,6272]{2,1,0:T(1,128)S(1)}, u32[]{:S(2)}, u32[]{:S(2)}) async-start(f32[128,1,6272]{2,1,0:T(1,128)} %get-tuple-element.22), calls=%async_computation.1 | async-start | bytes 6422528 | tf_op jit(solution)/shard_map/all_to_all | solution.py:485
  53.6 0.2 shard_map.149.plan_ref
  53.8 40.2 %all-to-all-done.1.arrived_ref = f32[128,1,6272]{2,1,0:T(1,128)S(1)} async-done(((f32[128,1,6272]{2,1,0:T(1,128)}), f32[128,1,6272]{2,1,0:T(1,128)S(1)}, u32[]{:S(2)}, u32[]{:S(2)}) %all-to-all-start.1) | async-done | bytes 3211296 | tf_op jit(solution)/shard_map/all_to_all | solution.py:485
  94.0 2.4 %shard_map.154 = (f32[3,64,128]{2,1,0:T(8,128)}, f32[1]{0:T(128)}, f32[80,1536]{1,0:T(8,128)}, f32[80,1536]{1,0:T(8,128)}) custom-call(s32[8,128]{1,0:T(8,128)S(1)} %shard_map.149.plan_ref, f32[1]{0:T(128)S(6)} %copy.21.load_ref, f32[1]{0:T(128)S(6)} %copy.22.radius_ref, f32[128,1,6272]{2,1,0:T(1,128)S(1)} %all-to-all-done.1.arrived_ref, ...), custom_call_target="tpu_custom_call" | custom-call | tf_op jit(solution)/shard_map/pallas_call | solution.py:487
  (15 shorter events, 0.0 us)
Async XLA Ops:
  0.6 0.7 copy-start.5
  1.3 0.9 copy-start.1
  1.3 0.9 copy-start.6
  1.3 0.9 copy-start.7
  1.3 0.9 copy-start.8
  2.2 14.4 %copy-start.2 = (f32[3,64,128]{2,1,0:T(8,128)S(1)}, f32[3,64,128]{2,1,0:T(8,128)}, u32[]{:S(2)}) copy-start(f32[3,64,128]{2,1,0:T(8,128)} %external_ref.1) | copy-start | bytes 294916
  2.2 14.5 %copy-start.3 = (s32[2,64,128]{2,1,0:T(8,128)S(1)}, s32[2,64,128]{2,1,0:T(8,128)}, u32[]{:S(2)}) copy-start(s32[2,64,128]{2,1,0:T(8,128)} %mask_ref.1) | copy-start | bytes 196612
  2.2 14.4 %copy-start.4 = (f32[64,128]{1,0:T(8,128)S(1)}, f32[64,128]{1,0:T(8,128)}, u32[]{:S(2)}) copy-start(f32[64,128]{1,0:T(8,128)} %cohesive_ref.1) | copy-start | bytes 98308
  2.2 38.1 %copy-start = (f32[160,1536]{1,0:T(8,128)S(1)}, f32[160,1536]{1,0:T(8,128)}, u32[]{:S(2)}) copy-start(f32[160,1536]{1,0:T(8,128)} %history_ref.1) | copy-start | bytes 2949124
  16.9 14.1 %collective-permute-start = (f32[72,128]{1,0:T(8,128)S(1)}, f32[72,128]{1,0:T(8,128)S(1)}, u32[]{:S(2)}, u32[]{:S(2)}) collective-permute-start(f32[72,128]{1,0:T(8,128)S(1)} %get-tuple-element.17), channel_id=1, source_target_pairs={{0,16},{32,48},{64,80},{96,112},{16,0},{48,32},{80,64},{112,96},{1... | collective-permute-start | bytes 110600 | tf_op jit(solution)/shard_map/ppermute | solution.py:418
  16.9 14.0 %collective-permute-start.1 = (f32[72,128]{1,0:T(8,128)S(1)}, f32[72,128]{1,0:T(8,128)S(1)}, u32[]{:S(2)}, u32[]{:S(2)}) collective-permute-start(f32[72,128]{1,0:T(8,128)S(1)} %get-tuple-element.18), channel_id=1, source_target_pairs={{16,32},{48,64},{80,96},{32,16},{64,48},{96,80},{17,33},{49,65},{8... | collective-permute-start | bytes 110600 | tf_op jit(solution)/shard_map/ppermute | solution.py:418
  17.6 22.8 %all-to-all-start = ((f32[128,1,128]{2,1,0:T(1,128)}), f32[128,1,128]{2,1,0:T(1,128)S(1)}, u32[]{:S(2)}, u32[]{:S(2)}) async-start(f32[128,1,128]{2,1,0:T(1,128)} %get-tuple-element.14), calls=%async_computation | async-start | bytes 131072 | tf_op jit(solution)/shard_map/all_to_all | solution.py:467
  31.4 12.3 %collective-permute-start.2 = (f32[72,128]{1,0:T(8,128)S(1)}, f32[72,128]{1,0:T(8,128)S(1)}, u32[]{:S(2)}, u32[]{:S(2)}) collective-permute-start(f32[72,128]{1,0:T(8,128)S(1)} %get-tuple-element.19), channel_id=1, source_target_pairs={{0,1},{2,3},{4,5},{6,7},{8,9},{10,11},{12,13},{14,15},{1,0},{3,2},... | collective-permute-start | bytes 110600 | tf_op jit(solution)/shard_map/ppermute | solution.py:418
  32.5 11.2 %collective-permute-start.3 = (f32[72,128]{1,0:T(8,128)S(1)}, f32[72,128]{1,0:T(8,128)S(1)}, u32[]{:S(2)}, u32[]{:S(2)}) collective-permute-start(f32[72,128]{1,0:T(8,128)S(1)} %get-tuple-element.20), channel_id=1, source_target_pairs={{1,2},{3,4},{5,6},{7,8},{9,10},{11,12},{13,14},{2,1},{4,3},{6,5},{... | collective-permute-start | bytes 110600 | tf_op jit(solution)/shard_map/ppermute | solution.py:418
  46.9 47.2 %all-to-all-start.1 = ((f32[128,1,6272]{2,1,0:T(1,128)}), f32[128,1,6272]{2,1,0:T(1,128)S(1)}, u32[]{:S(2)}, u32[]{:S(2)}) async-start(f32[128,1,6272]{2,1,0:T(1,128)} %get-tuple-element.22), calls=%async_computation.1 | async-start | bytes 6422528 | tf_op jit(solution)/shard_map/all_to_all | solution.py:485
